TPU v7x, 128 devices: a whole 4x4x4 slice. The times are simulated.
128 devices in a mesh: along: 32 (over x, y, core), across: 4 (over z).
Axes of the slice: x: 4, y: 4, z: 4, core: 2. Of those that a mesh axis runs over, the one named last changes fastest.
Arguments:
- fields: float32 [40, 3, 32, 16384], P(None, None, 'across', 'along'), may hold values from -6 to 6
- first_feet: int32 [32, 16384], P('across', 'along'), may hold values from 0 to 524287, as said below
- first_fraction: float32 [40, 32, 16384], P(None, 'across', 'along'), may hold values from 0 to 1
- second_feet: int32 [32, 16384], P('across', 'along'), may hold values from 0 to 524287, as said below
- second_fraction: float32 [40, 32, 16384], P(None, 'across', 'along'), may hold values from 0 to 1
- lateral_mix: float32 [32, 16384], P('across', 'along'), may hold values from 0.02 to 0.2
- vertical_mix: float32 [2, 39, 32, 16384], P(None, None, 'across', 'along'), may hold values from 0.05 to 5
- bottom_drag: float32 [32, 16384], P('across', 'along'), may hold values from 0.05 to 2
- surface_stress: float32 [2, 32, 16384], P(None, 'across', 'along'), may hold values from -3 to 3
Outputs:
- advanced: float32 [40, 3, 32, 16384], P(None, None, 'across', 'along')
Inputs may be any that keep to these rules, and one draw needn't show every extreme that they name: `first_feet`: A cell in the block of 8 x 512 cells with along block index a has its foot point (row p // 16384, column p % 16384) in a block whose along index lies from w to w + 3, w = max(a - 3, 0), at any cross block index. At most 288 cells of one block have foot points in one block, and some pair of blocks reaches 288. `second_feet`: as for first_feet.
All inputs are finite; a program needn't handle non-finite values.
Results may differ from a plain program's by a relative error of at most 0.00002.
Values sent between devices are 32-bit elements; how exact they have to be, the bound alone decides.
No kernel may reach another device: no remote copies, remote signals or barrier semaphores. Data moves between devices by JAX's collectives and lax.ppermute only.
A program may use at most 64 MiB of HBM per device.

v0:
```python
import jax
import jax.numpy as jnp
from jax import lax
from jax.sharding import PartitionSpec as P


def shifted(block, axis, distance):
    devices = range(lax.axis_size(axis))
    route = [(i - distance, i) for i in devices if i - distance in devices]
    return lax.ppermute(block, axis, route)


def padded_2(value, sides, width):
    edges = {}
    for axis, dim in sides:
        count, length = (lax.axis_size(axis), value.shape[dim])
        up = [(i, (i + 1) % count) for i in range(count - 1)]
        last = lax.slice_in_dim(value, length - width, length, axis=dim)
        first = lax.slice_in_dim(value, 0, width, axis=dim)
        edges[dim] = (
            lax.ppermute(last, axis, up),
            lax.ppermute(first, axis, [(b, a) for a, b in up]),
        )
    done = []
    for _, dim in sides:
        low, high = edges[dim]
        around = [(width, width) if d in done else (0, 0) for d in range(value.ndim)]
        value = jnp.concatenate([jnp.pad(low, around), value, jnp.pad(high, around)], axis=dim)
        done.append(dim)
    return value


def interpolate(columns, fraction):
    upper = jnp.concatenate([columns[1:], columns[-1:]], axis=0)
    weight = fraction[:, None]
    return (1.0 - weight) * columns + weight * upper


def neighbour_sum(padded):
    total = padded[:, :, :-2, 1:-1] + padded[:, :, 2:, 1:-1]
    return total + padded[:, :, 1:-1, :-2] + padded[:, :, 1:-1, 2:]


def solve_columns(forcing, vertical_mix, bottom_drag, surface_stress):
    layers = forcing.shape[0]
    coupling = jnp.stack([vertical_mix[0], vertical_mix[0], vertical_mix[1]], axis=1)
    nothing = jnp.zeros_like(coupling[:1])
    below = jnp.concatenate([nothing, coupling], axis=0)
    above = jnp.concatenate([coupling, nothing], axis=0)
    friction = jnp.stack([bottom_drag, bottom_drag, jnp.zeros_like(bottom_drag)], axis=0)
    diagonal = (1.0 + below + above).at[0].add(friction)
    source = forcing.at[layers - 1, 0:2].add(surface_stress)
    factor = above[0] / diagonal[0]
    partial_value = source[0] / diagonal[0]
    factors = [factor]
    partials = [partial_value]
    for level_index in range(1, layers):
        denominator = diagonal[level_index] - below[level_index] * factor
        factor = above[level_index] / denominator
        partial_value = (source[level_index] + below[level_index] * partial_value) / denominator
        factors.append(factor)
        partials.append(partial_value)
    solution = partials[layers - 1]
    results = [solution]
    for level_index in range(layers - 2, -1, -1):
        solution = partials[level_index] + factors[level_index] * solution
        results.append(solution)
    return jnp.stack(results[::-1], axis=0)


def owners(feet, cross_dev, along_dev, along_total):
    flat_feet = feet.reshape(-1)
    global_row = flat_feet // along_total
    global_column = flat_feet % along_total
    local_cell = global_row % cross_dev * along_dev + global_column % along_dev
    return (global_column // along_dev, global_row // cross_dev, local_cell)


def slot_position(partner):
    order = jnp.argsort(partner, stable=True)
    sorted_partner = partner[order]
    first = jnp.searchsorted(sorted_partner, sorted_partner, side="left")
    ranked = jnp.arange(partner.shape[0], dtype=jnp.int32) - first
    return jnp.zeros_like(partner).at[order].set(ranked)


def window_request_move(message, steps):
    return shifted(message, "along", steps)


def window_column_move(message, steps):
    return shifted(message, "along", steps)


def fetch(table, feet, cross_dev, along_dev):
    along_count = lax.axis_size("along")
    across_count = lax.axis_size("across")
    reach = along_count // 8
    capacity = 9 * cross_dev * along_dev // (8 * across_count * reach)
    width = table.shape[1]
    owner_along, owner_across, local_cell = owners(
        feet, cross_dev, along_dev, along_dev * along_count
    )
    partner = owner_along * across_count + owner_across
    position = slot_position(partner)
    here = lax.axis_index("along")
    start = jnp.maximum(here - (reach - 1), 0)
    target = (owner_across * reach + owner_along - start) * capacity + position
    requests = jnp.zeros((across_count * reach * capacity,), jnp.int32).at[target].set(local_cell)
    requests = requests.reshape(across_count, reach, capacity)
    arrived = lax.all_to_all(requests, "across", split_axis=0, concat_axis=0, tiled=True)
    incoming = []
    for distance in range(1 - reach, reach):
        slot = jnp.clip(here + distance - start, 0, reach - 1)
        block = lax.dynamic_index_in_dim(arrived, slot, axis=1, keepdims=False)
        if distance == 0:
            incoming.append(block)
        else:
            incoming.append(window_request_move(block, distance))
    wanted = jnp.stack(incoming, axis=1)
    span = 2 * reach - 1
    picked = jnp.take(table, wanted.reshape(-1), axis=0).reshape(
        across_count, span, capacity, width
    )
    outgoing = []
    for index in range(span):
        distance = index - (reach - 1)
        if distance == 0:
            outgoing.append(picked[:, index])
        else:
            outgoing.append(window_column_move(picked[:, index], -distance))
    answered = jnp.stack(outgoing, axis=1)
    selector = start + jnp.arange(reach, dtype=jnp.int32) - here + reach - 1
    ordered = jnp.take(answered, selector, axis=1)
    returned = lax.all_to_all(ordered, "across", split_axis=0, concat_axis=0, tiled=True)
    return jnp.take(returned.reshape(-1, width), target, axis=0)


def body(
    fields,
    first_feet,
    first_fraction,
    second_feet,
    second_fraction,
    lateral_mix,
    vertical_mix,
    bottom_drag,
    surface_stress,
):
    layers, components, cross_dev, along_dev = fields.shape
    row_count = layers * components
    width = (row_count + 127) // 128 * 128

    def advect(current, feet, fraction):
        table = current.reshape(row_count, cross_dev * along_dev).T
        table = jnp.pad(table, ((0, 0), (0, width - row_count)))
        gathered = fetch(table, feet, cross_dev, along_dev)[:, :row_count].T
        return interpolate(gathered.reshape(layers, components, cross_dev, along_dev), fraction)

    middle = advect(fields, first_feet, first_fraction)
    moved = advect(middle, second_feet, second_fraction)
    padded = padded_2(moved, (("across", 2), ("along", 3)), 1)
    beside_all = neighbour_sum(padded)
    row_total = cross_dev * lax.axis_size("across")
    column_total = along_dev * lax.axis_size("along")
    row_index = lax.axis_index("across") * cross_dev + jnp.arange(cross_dev, dtype=jnp.int32)
    column_index = lax.axis_index("along") * along_dev + jnp.arange(along_dev, dtype=jnp.int32)
    row_present = (row_index > 0).astype(jnp.float32) + (row_index < row_total - 1).astype(
        jnp.float32
    )
    column_present = (column_index > 0).astype(jnp.float32) + (
        column_index < column_total - 1
    ).astype(jnp.float32)
    present = row_present[:, None] + column_present[None, :]
    mixed = moved + lateral_mix * (beside_all - present * moved)
    return solve_columns(mixed, vertical_mix, bottom_drag, surface_stress)


def solution(mesh):
    in_specs = (
        P(None, None, "across", "along"),
        P("across", "along"),
        P(None, "across", "along"),
        P("across", "along"),
        P(None, "across", "along"),
        P("across", "along"),
        P(None, None, "across", "along"),
        P("across", "along"),
        P(None, "across", "along"),
    )
    out_specs = P(None, None, "across", "along")
    return jax.shard_map(body, mesh=mesh, in_specs=in_specs, out_specs=out_specs, check_vma=False)
```

profile of v0, /device:TPU:61, one launch (start us, length us, event | category | flops | bytes accessed | tf_op | source)
XLA Modules:
  0.0 1147.2 jit_solution(587793504798495941)
XLA Ops:
  6.6 23.0 %gather_fusion.2 = s32[4096]{0:T(1024)S(1)} fusion(s32[4096]{0:T(1024)S(1)} %get-tuple-element.368, s32[4096]{0:T(1024)S(1)} %get-tuple-element.369), kind=kCustom, calls=%fused_computation.8 | custom fusion | bytes 49152 | tf_op jit(solution)/shard_map/gather | solution.py:81
  29.6 300.6 %while.41 = (s32[]{:T(128)}, u32[4096]{0:T(1024)S(1)}, u32[4096]{0:T(1024)S(1)}, s32[4096]{0:T(1024)S(1)}, s32[]{:T(128)}, /*index=5*/s32[]{:T(128)}, s32[]{}) while((s32[]{:T(128)}, u32[4096]{0:T(1024)S(1)}, u32[4096]{0:T(1024)S(1)}, s32[4096]{0:T(1024)S(1)}, s32[]{:T(128)}, /*index=5*/s32[]{:T(128)}, s32[]{}) %tuple.206), condition=%wide.region_2.3_spmd.clone, body=%wide.region_1.2_spmd.clone.sunk | while | flops 77828 | bytes 270437 | solution.py:82
  29.6 23.0 %gather_fusion = s32[4096]{0:T(1024)S(1)} fusion(s32[4096]{0:T(1024)S(1)} %get-tuple-element.469, u32[4096]{0:T(1024)S(1)} %broadcast_clamp_fusion.8), kind=kCustom, calls=%fused_computation.clone.clone.1 | custom fusion | bytes 49152 | tf_op jit(solution)/shard_map/jit(searchsorted)/jit(_searchsorted_scan_impl)/vmap(jit(_searchsorted_scan_impl))/while/body/eval_jaxpr/gather | solution.py:82
  52.8 23.0 %gather_fusion = s32[4096]{0:T(1024)S(1)} fusion(s32[4096]{0:T(1024)S(1)} %get-tuple-element.469, u32[4096]{0:T(1024)S(1)} %broadcast_clamp_fusion.8), kind=kCustom, calls=%fused_computation.clone.clone.1 | custom fusion | bytes 49152 | tf_op jit(solution)/shard_map/jit(searchsorted)/jit(_searchsorted_scan_impl)/vmap(jit(_searchsorted_scan_impl))/while/body/eval_jaxpr/gather | solution.py:82
  75.9 23.0 %gather_fusion = s32[4096]{0:T(1024)S(1)} fusion(s32[4096]{0:T(1024)S(1)} %get-tuple-element.469, u32[4096]{0:T(1024)S(1)} %broadcast_clamp_fusion.8), kind=kCustom, calls=%fused_computation.clone.clone.1 | custom fusion | bytes 49152 | tf_op jit(solution)/shard_map/jit(searchsorted)/jit(_searchsorted_scan_impl)/vmap(jit(_searchsorted_scan_impl))/while/body/eval_jaxpr/gather | solution.py:82
  99.0 23.0 %gather_fusion = s32[4096]{0:T(1024)S(1)} fusion(s32[4096]{0:T(1024)S(1)} %get-tuple-element.469, u32[4096]{0:T(1024)S(1)} %broadcast_clamp_fusion.8), kind=kCustom, calls=%fused_computation.clone.clone.1 | custom fusion | bytes 49152 | tf_op jit(solution)/shard_map/jit(searchsorted)/jit(_searchsorted_scan_impl)/vmap(jit(_searchsorted_scan_impl))/while/body/eval_jaxpr/gather | solution.py:82
  122.2 23.0 %gather_fusion = s32[4096]{0:T(1024)S(1)} fusion(s32[4096]{0:T(1024)S(1)} %get-tuple-element.469, u32[4096]{0:T(1024)S(1)} %broadcast_clamp_fusion.8), kind=kCustom, calls=%fused_computation.clone.clone.1 | custom fusion | bytes 49152 | tf_op jit(solution)/shard_map/jit(searchsorted)/jit(_searchsorted_scan_impl)/vmap(jit(_searchsorted_scan_impl))/while/body/eval_jaxpr/gather | solution.py:82
  145.3 23.0 %gather_fusion = s32[4096]{0:T(1024)S(1)} fusion(s32[4096]{0:T(1024)S(1)} %get-tuple-element.469, u32[4096]{0:T(1024)S(1)} %broadcast_clamp_fusion.8), kind=kCustom, calls=%fused_computation.clone.clone.1 | custom fusion | bytes 49152 | tf_op jit(solution)/shard_map/jit(searchsorted)/jit(_searchsorted_scan_impl)/vmap(jit(_searchsorted_scan_impl))/while/body/eval_jaxpr/gather | solution.py:82
  168.4 23.0 %gather_fusion = s32[4096]{0:T(1024)S(1)} fusion(s32[4096]{0:T(1024)S(1)} %get-tuple-element.469, u32[4096]{0:T(1024)S(1)} %broadcast_clamp_fusion.8), kind=kCustom, calls=%fused_computation.clone.clone.1 | custom fusion | bytes 49152 | tf_op jit(solution)/shard_map/jit(searchsorted)/jit(_searchsorted_scan_impl)/vmap(jit(_searchsorted_scan_impl))/while/body/eval_jaxpr/gather | solution.py:82
  191.5 23.0 %gather_fusion = s32[4096]{0:T(1024)S(1)} fusion(s32[4096]{0:T(1024)S(1)} %get-tuple-element.469, u32[4096]{0:T(1024)S(1)} %broadcast_clamp_fusion.8), kind=kCustom, calls=%fused_computation.clone.clone.1 | custom fusion | bytes 49152 | tf_op jit(solution)/shard_map/jit(searchsorted)/jit(_searchsorted_scan_impl)/vmap(jit(_searchsorted_scan_impl))/while/body/eval_jaxpr/gather | solution.py:82
  214.7 23.0 %gather_fusion = s32[4096]{0:T(1024)S(1)} fusion(s32[4096]{0:T(1024)S(1)} %get-tuple-element.469, u32[4096]{0:T(1024)S(1)} %broadcast_clamp_fusion.8), kind=kCustom, calls=%fused_computation.clone.clone.1 | custom fusion | bytes 49152 | tf_op jit(solution)/shard_map/jit(searchsorted)/jit(_searchsorted_scan_impl)/vmap(jit(_searchsorted_scan_impl))/while/body/eval_jaxpr/gather | solution.py:82
  237.8 23.0 %gather_fusion = s32[4096]{0:T(1024)S(1)} fusion(s32[4096]{0:T(1024)S(1)} %get-tuple-element.469, u32[4096]{0:T(1024)S(1)} %broadcast_clamp_fusion.8), kind=kCustom, calls=%fused_computation.clone.clone.1 | custom fusion | bytes 49152 | tf_op jit(solution)/shard_map/jit(searchsorted)/jit(_searchsorted_scan_impl)/vmap(jit(_searchsorted_scan_impl))/while/body/eval_jaxpr/gather | solution.py:82
  260.9 23.0 %gather_fusion = s32[4096]{0:T(1024)S(1)} fusion(s32[4096]{0:T(1024)S(1)} %get-tuple-element.469, u32[4096]{0:T(1024)S(1)} %broadcast_clamp_fusion.8), kind=kCustom, calls=%fused_computation.clone.clone.1 | custom fusion | bytes 49152 | tf_op jit(solution)/shard_map/jit(searchsorted)/jit(_searchsorted_scan_impl)/vmap(jit(_searchsorted_scan_impl))/while/body/eval_jaxpr/gather | solution.py:82
  284.0 23.0 %gather_fusion = s32[4096]{0:T(1024)S(1)} fusion(s32[4096]{0:T(1024)S(1)} %get-tuple-element.469, u32[4096]{0:T(1024)S(1)} %broadcast_clamp_fusion.8), kind=kCustom, calls=%fused_computation.clone.clone.1 | custom fusion | bytes 49152 | tf_op jit(solution)/shard_map/jit(searchsorted)/jit(_searchsorted_scan_impl)/vmap(jit(_searchsorted_scan_impl))/while/body/eval_jaxpr/gather | solution.py:82
  307.2 23.0 %gather_fusion = s32[4096]{0:T(1024)S(1)} fusion(s32[4096]{0:T(1024)S(1)} %get-tuple-element.469, u32[4096]{0:T(1024)S(1)} %broadcast_clamp_fusion.8), kind=kCustom, calls=%fused_computation.clone.clone.1 | custom fusion | bytes 49152 | tf_op jit(solution)/shard_map/jit(searchsorted)/jit(_searchsorted_scan_impl)/vmap(jit(_searchsorted_scan_impl))/while/body/eval_jaxpr/gather | solution.py:82
  330.3 15.5 %scatter_custom_fusion = s32[4096]{0:T(1024)S(1)} fusion(s32[4096]{0:T(1024)S(1)} %get-tuple-element.370, s32[4096]{0:T(1024)S(1)} %convert_subtract_fusion.1, s32[]{:T(128)} %constant.302.clone.1), kind=kCustom, calls=%fused_computation.402 | custom fusion | bytes 16388 | tf_op jit(solution)/shard_map/scatter | solution.py:84
  345.9 15.5 %scatter_custom_fusion.1 = s32[4608]{0:T(1024)S(1)} fusion(s32[4096]{0:T(1024)S(1)} %get-tuple-element.326, s32[4096]{0:T(1024)S(1)} %get-tuple-element.367, s32[]{:T(128)} %constant.302.clone.1), kind=kCustom, calls=%fused_computation.393 | custom fusion | bytes 18436 | tf_op jit(solution)/shard_map/scatter | solution.py:109
  372.8 23.0 %gather_fusion.3 = s32[4096]{0:T(1024)S(1)} fusion(s32[4096]{0:T(1024)S(1)} %get-tuple-element.364, s32[4096]{0:T(1024)S(1)} %get-tuple-element.365), kind=kCustom, calls=%fused_computation.9 | custom fusion | bytes 49152 | tf_op jit(solution)/shard_map/gather | solution.py:81
  395.9 300.6 %while.42 = (s32[]{:T(128)}, u32[4096]{0:T(1024)S(1)}, u32[4096]{0:T(1024)S(1)}, s32[4096]{0:T(1024)S(1)}, s32[]{:T(128)}, /*index=5*/s32[]{:T(128)}, s32[]{}) while((s32[]{:T(128)}, u32[4096]{0:T(1024)S(1)}, u32[4096]{0:T(1024)S(1)}, s32[4096]{0:T(1024)S(1)}, s32[]{:T(128)}, /*index=5*/s32[]{:T(128)}, s32[]{}) %tuple.203), condition=%wide.region_7.11_spmd.clone, body=%wide.region_6.10_spmd.clone.sunk | while | flops 77828 | bytes 270437 | solution.py:82
  395.9 23.0 %gather_fusion.1 = s32[4096]{0:T(1024)S(1)} fusion(s32[4096]{0:T(1024)S(1)} %get-tuple-element.448, u32[4096]{0:T(1024)S(1)} %broadcast_clamp_fusion.9), kind=kCustom, calls=%fused_computation.4.clone.clone.1 | custom fusion | bytes 49152 | tf_op jit(solution)/shard_map/jit(searchsorted)/jit(_searchsorted_scan_impl)/vmap(jit(_searchsorted_scan_impl))/while/body/eval_jaxpr/gather | solution.py:82
  419.0 23.0 %gather_fusion.1 = s32[4096]{0:T(1024)S(1)} fusion(s32[4096]{0:T(1024)S(1)} %get-tuple-element.448, u32[4096]{0:T(1024)S(1)} %broadcast_clamp_fusion.9), kind=kCustom, calls=%fused_computation.4.clone.clone.1 | custom fusion | bytes 49152 | tf_op jit(solution)/shard_map/jit(searchsorted)/jit(_searchsorted_scan_impl)/vmap(jit(_searchsorted_scan_impl))/while/body/eval_jaxpr/gather | solution.py:82
  442.1 23.0 %gather_fusion.1 = s32[4096]{0:T(1024)S(1)} fusion(s32[4096]{0:T(1024)S(1)} %get-tuple-element.448, u32[4096]{0:T(1024)S(1)} %broadcast_clamp_fusion.9), kind=kCustom, calls=%fused_computation.4.clone.clone.1 | custom fusion | bytes 49152 | tf_op jit(solution)/shard_map/jit(searchsorted)/jit(_searchsorted_scan_impl)/vmap(jit(_searchsorted_scan_impl))/while/body/eval_jaxpr/gather | solution.py:82
  465.3 23.0 %gather_fusion.1 = s32[4096]{0:T(1024)S(1)} fusion(s32[4096]{0:T(1024)S(1)} %get-tuple-element.448, u32[4096]{0:T(1024)S(1)} %broadcast_clamp_fusion.9), kind=kCustom, calls=%fused_computation.4.clone.clone.1 | custom fusion | bytes 49152 | tf_op jit(solution)/shard_map/jit(searchsorted)/jit(_searchsorted_scan_impl)/vmap(jit(_searchsorted_scan_impl))/while/body/eval_jaxpr/gather | solution.py:82
  488.4 23.0 %gather_fusion.1 = s32[4096]{0:T(1024)S(1)} fusion(s32[4096]{0:T(1024)S(1)} %get-tuple-element.448, u32[4096]{0:T(1024)S(1)} %broadcast_clamp_fusion.9), kind=kCustom, calls=%fused_computation.4.clone.clone.1 | custom fusion | bytes 49152 | tf_op jit(solution)/shard_map/jit(searchsorted)/jit(_searchsorted_scan_impl)/vmap(jit(_searchsorted_scan_impl))/while/body/eval_jaxpr/gather | solution.py:82
  511.5 23.0 %gather_fusion.1 = s32[4096]{0:T(1024)S(1)} fusion(s32[4096]{0:T(1024)S(1)} %get-tuple-element.448, u32[4096]{0:T(1024)S(1)} %broadcast_clamp_fusion.9), kind=kCustom, calls=%fused_computation.4.clone.clone.1 | custom fusion | bytes 49152 | tf_op jit(solution)/shard_map/jit(searchsorted)/jit(_searchsorted_scan_impl)/vmap(jit(_searchsorted_scan_impl))/while/body/eval_jaxpr/gather | solution.py:82
  534.7 23.0 %gather_fusion.1 = s32[4096]{0:T(1024)S(1)} fusion(s32[4096]{0:T(1024)S(1)} %get-tuple-element.448, u32[4096]{0:T(1024)S(1)} %broadcast_clamp_fusion.9), kind=kCustom, calls=%fused_computation.4.clone.clone.1 | custom fusion | bytes 49152 | tf_op jit(solution)/shard_map/jit(searchsorted)/jit(_searchsorted_scan_impl)/vmap(jit(_searchsorted_scan_impl))/while/body/eval_jaxpr/gather | solution.py:82
  557.8 23.0 %gather_fusion.1 = s32[4096]{0:T(1024)S(1)} fusion(s32[4096]{0:T(1024)S(1)} %get-tuple-element.448, u32[4096]{0:T(1024)S(1)} %broadcast_clamp_fusion.9), kind=kCustom, calls=%fused_computation.4.clone.clone.1 | custom fusion | bytes 49152 | tf_op jit(solution)/shard_map/jit(searchsorted)/jit(_searchsorted_scan_impl)/vmap(jit(_searchsorted_scan_impl))/while/body/eval_jaxpr/gather | solution.py:82
  580.9 23.0 %gather_fusion.1 = s32[4096]{0:T(1024)S(1)} fusion(s32[4096]{0:T(1024)S(1)} %get-tuple-element.448, u32[4096]{0:T(1024)S(1)} %broadcast_clamp_fusion.9), kind=kCustom, calls=%fused_computation.4.clone.clone.1 | custom fusion | bytes 49152 | tf_op jit(solution)/shard_map/jit(searchsorted)/jit(_searchsorted_scan_impl)/vmap(jit(_searchsorted_scan_impl))/while/body/eval_jaxpr/gather | solution.py:82
  604.0 23.0 %gather_fusion.1 = s32[4096]{0:T(1024)S(1)} fusion(s32[4096]{0:T(1024)S(1)} %get-tuple-element.448, u32[4096]{0:T(1024)S(1)} %broadcast_clamp_fusion.9), kind=kCustom, calls=%fused_computation.4.clone.clone.1 | custom fusion | bytes 49152 | tf_op jit(solution)/shard_map/jit(searchsorted)/jit(_searchsorted_scan_impl)/vmap(jit(_searchsorted_scan_impl))/while/body/eval_jaxpr/gather | solution.py:82
  627.2 23.0 %gather_fusion.1 = s32[4096]{0:T(1024)S(1)} fusion(s32[4096]{0:T(1024)S(1)} %get-tuple-element.448, u32[4096]{0:T(1024)S(1)} %broadcast_clamp_fusion.9), kind=kCustom, calls=%fused_computation.4.clone.clone.1 | custom fusion | bytes 49152 | tf_op jit(solution)/shard_map/jit(searchsorted)/jit(_searchsorted_scan_impl)/vmap(jit(_searchsorted_scan_impl))/while/body/eval_jaxpr/gather | solution.py:82
  650.3 23.0 %gather_fusion.1 = s32[4096]{0:T(1024)S(1)} fusion(s32[4096]{0:T(1024)S(1)} %get-tuple-element.448, u32[4096]{0:T(1024)S(1)} %broadcast_clamp_fusion.9), kind=kCustom, calls=%fused_computation.4.clone.clone.1 | custom fusion | bytes 49152 | tf_op jit(solution)/shard_map/jit(searchsorted)/jit(_searchsorted_scan_impl)/vmap(jit(_searchsorted_scan_impl))/while/body/eval_jaxpr/gather | solution.py:82
  673.4 23.0 %gather_fusion.1 = s32[4096]{0:T(1024)S(1)} fusion(s32[4096]{0:T(1024)S(1)} %get-tuple-element.448, u32[4096]{0:T(1024)S(1)} %broadcast_clamp_fusion.9), kind=kCustom, calls=%fused_computation.4.clone.clone.1 | custom fusion | bytes 49152 | tf_op jit(solution)/shard_map/jit(searchsorted)/jit(_searchsorted_scan_impl)/vmap(jit(_searchsorted_scan_impl))/while/body/eval_jaxpr/gather | solution.py:82
  696.5 15.5 %scatter_custom_fusion.2 = s32[4096]{0:T(1024)S(1)} fusion(s32[4096]{0:T(1024)S(1)} %get-tuple-element.366, s32[4096]{0:T(1024)S(1)} %convert_subtract_fusion, s32[]{:T(128)} %constant.302.clone.1), kind=kCustom, calls=%fused_computation.400 | custom fusion | bytes 16388 | tf_op jit(solution)/shard_map/scatter | solution.py:84
  712.1 15.5 %scatter_custom_fusion.3 = s32[4608]{0:T(1024)S(1)} fusion(s32[4096]{0:T(1024)S(1)} %get-tuple-element.324, s32[4096]{0:T(1024)S(1)} %get-tuple-element.363, s32[]{:T(128)} %constant.302.clone.1), kind=kCustom, calls=%fused_computation.391 | custom fusion | bytes 18436 | tf_op jit(solution)/shard_map/scatter | solution.py:109
  781.1 15.7 %gather_fusion.4 = f32[8064,128]{1,0:T(8,128)} fusion(f32[4096,128]{1,0:T(8,128)S(1)} %pad.22, s32[8192]{0:T(1024)S(1)} %get-tuple-element.372), kind=kCustom, calls=%fused_computation.1.clone | custom fusion | bytes 8289792 | tf_op jit(solution)/shard_map/jit(_take)/gather | solution.py:122
  812.5 12.8 %collective-permute-done.6 = f32[4,288,128]{2,1,0:T(8,128)S(1)} collective-permute-done((f32[4,288,128]{2,1,0:T(8,128)S(1)}, f32[4,288,128]{2,1,0:T(8,128)S(1)}, u32[]{:S(2)}, u32[]{:S(2)}) %collective-permute-start.6) | collective-permute-done | bytes 589856 | tf_op jit(solution)/shard_map/ppermute | solution.py:10
  826.2 8.0 collective-permute-done.7
  848.7 19.0 %collective-permute-done.9 = f32[4,288,128]{2,1,0:T(8,128)S(1)} collective-permute-done((f32[4,288,128]{2,1,0:T(8,128)S(1)}, f32[4,288,128]{2,1,0:T(8,128)S(1)}, u32[]{:S(2)}, u32[]{:S(2)}) %collective-permute-start.9) | collective-permute-done | bytes 589856 | tf_op jit(solution)/shard_map/ppermute | solution.py:10
  885.7 12.5 %all-to-all-done.1 = f32[4,4,288,128]{3,2,1,0:T(8,128)S(1)} async-done(((f32[4,4,288,128]{3,2,1,0:T(8,128)}), f32[4,4,288,128]{3,2,1,0:T(8,128)S(1)}, u32[]{:S(2)}, u32[]{:S(2)}) %all-to-all-start.1) | async-done | bytes 2359328 | tf_op jit(solution)/shard_map/all_to_all | solution.py:135
  898.2 14.1 %gather_fusion.6 = f32[4096,128]{1,0:T(8,128)} fusion(f32[4608,128]{1,0:T(8,128)S(1)} %bitcast.183, s32[4096]{0:T(1024)S(1)} %broadcast_clamp_fusion.3), kind=kCustom, calls=%fused_computation.3.clone | custom fusion | bytes 4210688 | tf_op jit(solution)/shard_map/jit(_take)/gather | solution.py:136
  924.4 15.7 %gather_fusion.7 = f32[8064,128]{1,0:T(8,128)} fusion(f32[4096,128]{1,0:T(8,128)S(1)} %pad.23.clone, s32[8192]{0:T(1024)S(1)} %get-tuple-element.371), kind=kCustom, calls=%fused_computation.5.clone | custom fusion | bytes 8289792 | tf_op jit(solution)/shard_map/jit(_take)/gather | solution.py:122
  946.4 21.4 %collective-permute-start.18 = (f32[4,288,128]{2,1,0:T(8,128)S(1)}, f32[4,288,128]{2,1,0:T(8,128)S(1)}, u32[]{:S(2)}, u32[]{:S(2)}) collective-permute-start(f32[4,288,128]{2,1,0:T(8,128)S(1)} %get-tuple-element.335), channel_id=1, source_target_pairs={{0,12},{4,16},{8,20},{12,24},{16,28},{20,32},{24,36},{28,40},{32,4... | collective-permute-start | bytes 1769480 | tf_op jit(solution)/shard_map/ppermute | solution.py:10
  969.8 6.5 collective-permute-start.20
  982.2 13.1 %collective-permute-done.19 = f32[4,288,128]{2,1,0:T(8,128)S(1)} collective-permute-done((f32[4,288,128]{2,1,0:T(8,128)S(1)}, f32[4,288,128]{2,1,0:T(8,128)S(1)}, u32[]{:S(2)}, u32[]{:S(2)}) %collective-permute-start.19) | collective-permute-done | bytes 589856 | tf_op jit(solution)/shard_map/ppermute | solution.py:10
  1009.2 19.2 %collective-permute-done.21 = f32[4,288,128]{2,1,0:T(8,128)S(1)} collective-permute-done((f32[4,288,128]{2,1,0:T(8,128)S(1)}, f32[4,288,128]{2,1,0:T(8,128)S(1)}, u32[]{:S(2)}, u32[]{:S(2)}) %collective-permute-start.21) | collective-permute-done | bytes 589856 | tf_op jit(solution)/shard_map/ppermute | solution.py:10
  1048.2 11.1 all-to-all-done.3
  1059.4 14.1 %gather_fusion.9 = f32[4096,128]{1,0:T(8,128)} fusion(f32[4608,128]{1,0:T(8,128)S(1)} %bitcast.182, s32[4096]{0:T(1024)S(1)} %broadcast_clamp_fusion.2), kind=kCustom, calls=%fused_computation.7.clone | custom fusion | bytes 4210688 | tf_op jit(solution)/shard_map/jit(_take)/gather | solution.py:136
  1100.8 26.6 %collective-permute-start.26 = (f32[40,3,8,1]{3,2,1,0:T(8,128)S(1)}, f32[40,3,8,1]{3,2,1,0:T(8,128)S(1)}, u32[]{:S(2)}, u32[]{:S(2)}) collective-permute-start(f32[40,3,8,1]{3,2,1,0:T(8,128)S(1)} %get-tuple-element.343), channel_id=1, source_target_pairs={{0,4},{4,8},{8,12},{12,16},{16,20},{20,24},{24,28},{28,32},{32,36}... | collective-permute-start | bytes 11528 | tf_op jit(solution)/shard_map/ppermute | solution.py:21
  (352 shorter events, 226.9 us)
Async XLA Ops:
  29.6 337.4 %copy-start.12 = (s32[8,512]{1,0:T(8,128)S(1)}, s32[8,512]{1,0:T(8,128)}, u32[]{:S(2)}) copy-start(s32[8,512]{1,0:T(8,128)} %param.26) | copy-start | bytes 49156
  362.1 366.3 %all-to-all-start = ((s32[4,4,288]{2,1,0:T(4,128)}), s32[4,4,288]{2,1,0:T(4,128)S(1)}, u32[]{:S(2)}, u32[]{:S(2)}) async-start(s32[4,4,288]{2,1,0:T(4,128)} %reshape.195), calls=%async_computation | async-start | bytes 49152 | tf_op jit(solution)/shard_map/all_to_all | solution.py:111
  728.4 31.1 %all-to-all-start.2 = ((s32[4,4,288]{2,1,0:T(4,128)}), s32[4,4,288]{2,1,0:T(4,128)S(1)}, u32[]{:S(2)}, u32[]{:S(2)}) async-start(s32[4,4,288]{2,1,0:T(4,128)} %reshape.200), calls=%async_computation.2 | async-start | bytes 49152 | tf_op jit(solution)/shard_map/all_to_all | solution.py:111
  732.7 23.9 %collective-permute-start = (s32[4,288]{1,0:T(4,128)S(1)}, s32[4,288]{1,0:T(4,128)S(1)}, u32[]{:S(2)}, u32[]{:S(2)}) collective-permute-start(s32[4,288]{1,0:T(4,128)S(1)} %bitcast.226), channel_id=1, source_target_pairs={{12,0},{16,4},{20,8},{24,12},{28,16},{32,20},{36,24},{40,28},{44,3... | collective-permute-start | bytes 13832 | tf_op jit(solution)/shard_map/ppermute | solution.py:10
  743.5 16.1 %collective-permute-start.1 = (s32[4,288]{1,0:T(4,128)S(1)}, s32[4,288]{1,0:T(4,128)S(1)}, u32[]{:S(2)}, u32[]{:S(2)}) collective-permute-start(s32[4,288]{1,0:T(4,128)S(1)} %bitcast.225), channel_id=1, source_target_pairs={{8,0},{12,4},{16,8},{20,12},{24,16},{28,20},{32,24},{36,28},{40,32... | collective-permute-start | bytes 13832 | tf_op jit(solution)/shard_map/ppermute | solution.py:10
  745.6 16.7 %collective-permute-start.2 = (s32[4,288]{1,0:T(4,128)S(1)}, s32[4,288]{1,0:T(4,128)S(1)}, u32[]{:S(2)}, u32[]{:S(2)}) collective-permute-start(s32[4,288]{1,0:T(4,128)S(1)} %bitcast.224), channel_id=1, source_target_pairs={{4,0},{8,4},{12,8},{16,12},{20,16},{24,20},{28,24},{32,28},{36,32}... | collective-permute-start | bytes 13832 | tf_op jit(solution)/shard_map/ppermute | solution.py:10
  747.8 16.6 %collective-permute-start.3 = (s32[4,288]{1,0:T(4,128)S(1)}, s32[4,288]{1,0:T(4,128)S(1)}, u32[]{:S(2)}, u32[]{:S(2)}) collective-permute-start(s32[4,288]{1,0:T(4,128)S(1)} %bitcast.222), channel_id=1, source_target_pairs={{0,4},{4,8},{8,12},{12,16},{16,20},{20,24},{24,28},{28,32},{32,36}... | collective-permute-start | bytes 13832 | tf_op jit(solution)/shard_map/ppermute | solution.py:10
  753.3 13.5 %collective-permute-start.4 = (s32[4,288]{1,0:T(4,128)S(1)}, s32[4,288]{1,0:T(4,128)S(1)}, u32[]{:S(2)}, u32[]{:S(2)}) collective-permute-start(s32[4,288]{1,0:T(4,128)S(1)} %bitcast.221), channel_id=1, source_target_pairs={{0,8},{4,12},{8,16},{12,20},{16,24},{20,28},{24,32},{28,36},{32,40... | collective-permute-start | bytes 13832 | tf_op jit(solution)/shard_map/ppermute | solution.py:10
  756.6 15.9 %collective-permute-start.5 = (s32[4,288]{1,0:T(4,128)S(1)}, s32[4,288]{1,0:T(4,128)S(1)}, u32[]{:S(2)}, u32[]{:S(2)}) collective-permute-start(s32[4,288]{1,0:T(4,128)S(1)} %bitcast.220), channel_id=1, source_target_pairs={{0,12},{4,16},{8,20},{12,24},{16,28},{20,32},{24,36},{28,40},{32,4... | collective-permute-start | bytes 13832 | tf_op jit(solution)/shard_map/ppermute | solution.py:10
  759.7 15.9 %collective-permute-start.12 = (s32[4,288]{1,0:T(4,128)S(1)}, s32[4,288]{1,0:T(4,128)S(1)}, u32[]{:S(2)}, u32[]{:S(2)}) collective-permute-start(s32[4,288]{1,0:T(4,128)S(1)} %bitcast.223), channel_id=1, source_target_pairs={{12,0},{16,4},{20,8},{24,12},{28,16},{32,20},{36,24},{40,28},{44,3... | collective-permute-start | bytes 13832 | tf_op jit(solution)/shard_map/ppermute | solution.py:10
  762.3 16.2 %collective-permute-start.13 = (s32[4,288]{1,0:T(4,128)S(1)}, s32[4,288]{1,0:T(4,128)S(1)}, u32[]{:S(2)}, u32[]{:S(2)}) collective-permute-start(s32[4,288]{1,0:T(4,128)S(1)} %bitcast.219), channel_id=1, source_target_pairs={{8,0},{12,4},{16,8},{20,12},{24,16},{28,20},{32,24},{36,28},{40,32... | collective-permute-start | bytes 13832 | tf_op jit(solution)/shard_map/ppermute | solution.py:10
  764.4 14.2 %collective-permute-start.14 = (s32[4,288]{1,0:T(4,128)S(1)}, s32[4,288]{1,0:T(4,128)S(1)}, u32[]{:S(2)}, u32[]{:S(2)}) collective-permute-start(s32[4,288]{1,0:T(4,128)S(1)} %bitcast.218), channel_id=1, source_target_pairs={{4,0},{8,4},{12,8},{16,12},{20,16},{24,20},{28,24},{32,28},{36,32}... | collective-permute-start | bytes 13832 | tf_op jit(solution)/shard_map/ppermute | solution.py:10
  766.8 11.8 %collective-permute-start.15 = (s32[4,288]{1,0:T(4,128)S(1)}, s32[4,288]{1,0:T(4,128)S(1)}, u32[]{:S(2)}, u32[]{:S(2)}) collective-permute-start(s32[4,288]{1,0:T(4,128)S(1)} %bitcast.217), channel_id=1, source_target_pairs={{0,4},{4,8},{8,12},{12,16},{16,20},{20,24},{24,28},{28,32},{32,36}... | collective-permute-start | bytes 13832 | tf_op jit(solution)/shard_map/ppermute | solution.py:10
  772.5 6.1 collective-permute-start.16
  775.6 5.2 collective-permute-start.17
  803.1 22.2 %collective-permute-start.6 = (f32[4,288,128]{2,1,0:T(8,128)S(1)}, f32[4,288,128]{2,1,0:T(8,128)S(1)}, u32[]{:S(2)}, u32[]{:S(2)}) collective-permute-start(f32[4,288,128]{2,1,0:T(8,128)S(1)} %get-tuple-element.342), channel_id=1, source_target_pairs={{0,12},{4,16},{8,20},{12,24},{16,28},{20,32},{24,36},{28,40},{32,4... | collective-permute-start | bytes 1769480 | tf_op jit(solution)/shard_map/ppermute | solution.py:10
  808.1 26.1 %collective-permute-start.7 = (f32[4,288,128]{2,1,0:T(8,128)S(1)}, f32[4,288,128]{2,1,0:T(8,128)S(1)}, u32[]{:S(2)}, u32[]{:S(2)}) collective-permute-start(f32[4,288,128]{2,1,0:T(8,128)S(1)} %get-tuple-element.341), channel_id=1, source_target_pairs={{0,8},{4,12},{8,16},{12,20},{16,24},{20,28},{24,32},{28,36},{32,40... | collective-permute-start | bytes 1769480 | tf_op jit(solution)/shard_map/ppermute | solution.py:10
  810.1 30.8 %collective-permute-start.8 = (f32[4,288,128]{2,1,0:T(8,128)S(1)}, f32[4,288,128]{2,1,0:T(8,128)S(1)}, u32[]{:S(2)}, u32[]{:S(2)}) collective-permute-start(f32[4,288,128]{2,1,0:T(8,128)S(1)} %get-tuple-element.340), channel_id=1, source_target_pairs={{0,4},{4,8},{8,12},{12,16},{16,20},{20,24},{24,28},{28,32},{32,36}... | collective-permute-start | bytes 1769480 | tf_op jit(solution)/shard_map/ppermute | solution.py:10
  842.7 24.9 %collective-permute-start.9 = (f32[4,288,128]{2,1,0:T(8,128)S(1)}, f32[4,288,128]{2,1,0:T(8,128)S(1)}, u32[]{:S(2)}, u32[]{:S(2)}) collective-permute-start(f32[4,288,128]{2,1,0:T(8,128)S(1)} %get-tuple-element.338), channel_id=1, source_target_pairs={{4,0},{8,4},{12,8},{16,12},{20,16},{24,20},{28,24},{32,28},{36,32}... | collective-permute-start | bytes 1769480 | tf_op jit(solution)/shard_map/ppermute | solution.py:10
  844.6 26.7 %collective-permute-start.10 = (f32[4,288,128]{2,1,0:T(8,128)S(1)}, f32[4,288,128]{2,1,0:T(8,128)S(1)}, u32[]{:S(2)}, u32[]{:S(2)}) collective-permute-start(f32[4,288,128]{2,1,0:T(8,128)S(1)} %get-tuple-element.337), channel_id=1, source_target_pairs={{8,0},{12,4},{16,8},{20,12},{24,16},{28,20},{32,24},{36,28},{40,32... | collective-permute-start | bytes 1769480 | tf_op jit(solution)/shard_map/ppermute | solution.py:10
  846.6 25.7 %collective-permute-start.11 = (f32[4,288,128]{2,1,0:T(8,128)S(1)}, f32[4,288,128]{2,1,0:T(8,128)S(1)}, u32[]{:S(2)}, u32[]{:S(2)}) collective-permute-start(f32[4,288,128]{2,1,0:T(8,128)S(1)} %get-tuple-element.336), channel_id=1, source_target_pairs={{12,0},{16,4},{20,8},{24,12},{28,16},{32,20},{36,24},{40,28},{44,3... | collective-permute-start | bytes 1769480 | tf_op jit(solution)/shard_map/ppermute | solution.py:10
  878.0 4.6 copy-start.7
  878.0 20.2 %all-to-all-start.1 = ((f32[4,4,288,128]{3,2,1,0:T(8,128)}), f32[4,4,288,128]{3,2,1,0:T(8,128)S(1)}, u32[]{:S(2)}, u32[]{:S(2)}) async-start(f32[4,4,288,128]{3,2,1,0:T(8,128)} %copy.102), calls=%async_computation.1 | async-start | bytes 4718592 | tf_op jit(solution)/shard_map/all_to_all | solution.py:135
  916.5 1.5 copy-start.5
  946.4 34.9 %collective-permute-start.18 = (f32[4,288,128]{2,1,0:T(8,128)S(1)}, f32[4,288,128]{2,1,0:T(8,128)S(1)}, u32[]{:S(2)}, u32[]{:S(2)}) collective-permute-start(f32[4,288,128]{2,1,0:T(8,128)S(1)} %get-tuple-element.335), channel_id=1, source_target_pairs={{0,12},{4,16},{8,20},{12,24},{16,28},{20,32},{24,36},{28,40},{32,4... | collective-permute-start | bytes 1769480 | tf_op jit(solution)/shard_map/ppermute | solution.py:10
  967.9 27.4 %collective-permute-start.19 = (f32[4,288,128]{2,1,0:T(8,128)S(1)}, f32[4,288,128]{2,1,0:T(8,128)S(1)}, u32[]{:S(2)}, u32[]{:S(2)}) collective-permute-start(f32[4,288,128]{2,1,0:T(8,128)S(1)} %get-tuple-element.334), channel_id=1, source_target_pairs={{0,8},{4,12},{8,16},{12,20},{16,24},{20,28},{24,32},{28,36},{32,40... | collective-permute-start | bytes 1769480 | tf_op jit(solution)/shard_map/ppermute | solution.py:10
  969.8 31.8 %collective-permute-start.20 = (f32[4,288,128]{2,1,0:T(8,128)S(1)}, f32[4,288,128]{2,1,0:T(8,128)S(1)}, u32[]{:S(2)}, u32[]{:S(2)}) collective-permute-start(f32[4,288,128]{2,1,0:T(8,128)S(1)} %get-tuple-element.333), channel_id=1, source_target_pairs={{0,4},{4,8},{8,12},{12,16},{16,20},{20,24},{24,28},{28,32},{32,36}... | collective-permute-start | bytes 1769480 | tf_op jit(solution)/shard_map/ppermute | solution.py:10
  1003.4 25.0 %collective-permute-start.21 = (f32[4,288,128]{2,1,0:T(8,128)S(1)}, f32[4,288,128]{2,1,0:T(8,128)S(1)}, u32[]{:S(2)}, u32[]{:S(2)}) collective-permute-start(f32[4,288,128]{2,1,0:T(8,128)S(1)} %get-tuple-element.331), channel_id=1, source_target_pairs={{4,0},{8,4},{12,8},{16,12},{20,16},{24,20},{28,24},{32,28},{36,32}... | collective-permute-start | bytes 1769480 | tf_op jit(solution)/shard_map/ppermute | solution.py:10
  1005.4 26.8 %collective-permute-start.22 = (f32[4,288,128]{2,1,0:T(8,128)S(1)}, f32[4,288,128]{2,1,0:T(8,128)S(1)}, u32[]{:S(2)}, u32[]{:S(2)}) collective-permute-start(f32[4,288,128]{2,1,0:T(8,128)S(1)} %get-tuple-element.330), channel_id=1, source_target_pairs={{8,0},{12,4},{16,8},{20,12},{24,16},{28,20},{32,24},{36,28},{40,32... | collective-permute-start | bytes 1769480 | tf_op jit(solution)/shard_map/ppermute | solution.py:10
  1007.3 25.8 %collective-permute-start.23 = (f32[4,288,128]{2,1,0:T(8,128)S(1)}, f32[4,288,128]{2,1,0:T(8,128)S(1)}, u32[]{:S(2)}, u32[]{:S(2)}) collective-permute-start(f32[4,288,128]{2,1,0:T(8,128)S(1)} %get-tuple-element.329), channel_id=1, source_target_pairs={{12,0},{16,4},{20,8},{24,12},{28,16},{32,20},{36,24},{40,28},{44,3... | collective-permute-start | bytes 1769480 | tf_op jit(solution)/shard_map/ppermute | solution.py:10
  1038.7 20.7 %all-to-all-start.3 = ((f32[4,4,288,128]{3,2,1,0:T(8,128)}), f32[4,4,288,128]{3,2,1,0:T(8,128)S(1)}, u32[]{:S(2)}, u32[]{:S(2)}) async-start(f32[4,4,288,128]{3,2,1,0:T(8,128)} %copy.111), calls=%async_computation.3 | async-start | bytes 4718592 | tf_op jit(solution)/shard_map/all_to_all | solution.py:135
  1045.4 1.3 copy-start
  1045.4 0.7 copy-start.9
  1045.4 1.9 copy-start.8
  1045.7 1.6 copy-start.2
  1086.3 2.2 copy-start.6
  1088.5 2.8 copy-start.4
  1095.0 44.7 %copy-start.11 = (f32[8,512]{1,0:T(8,128)S(1)}, f32[8,512]{1,0:T(8,128)}, u32[]{:S(2)}) copy-start(f32[8,512]{1,0:T(8,128)} %param.28) | copy-start | bytes 49156
  1095.3 44.4 %collective-permute-start.24 = (f32[40,3,1,512]{3,2,1,0:T(1,128)S(1)}, f32[40,3,1,512]{3,2,1,0:T(1,128)S(1)}, u32[]{:S(2)}, u32[]{:S(2)}) collective-permute-start(f32[40,3,1,512]{3,2,1,0:T(1,128)S(1)} %get-tuple-element.345), channel_id=1, source_target_pairs={{0,1},{1,2},{2,3},{4,5},{5,6},{6,7},{8,9},{9,10},{10,11},{12,13},{... | collective-permute-start | bytes 737288 | tf_op jit(solution)/shard_map/ppermute | solution.py:21
  1097.3 42.5 %collective-permute-start.25 = (f32[40,3,1,512]{3,2,1,0:T(1,128)S(1)}, f32[40,3,1,512]{3,2,1,0:T(1,128)S(1)}, u32[]{:S(2)}, u32[]{:S(2)}) collective-permute-start(f32[40,3,1,512]{3,2,1,0:T(1,128)S(1)} %get-tuple-element.346), channel_id=1, source_target_pairs={{1,0},{2,1},{3,2},{5,4},{6,5},{7,6},{9,8},{10,9},{11,10},{13,12},{... | collective-permute-start | bytes 737288 | tf_op jit(solution)/shard_map/ppermute | solution.py:22
  1100.8 32.4 %collective-permute-start.26 = (f32[40,3,8,1]{3,2,1,0:T(8,128)S(1)}, f32[40,3,8,1]{3,2,1,0:T(8,128)S(1)}, u32[]{:S(2)}, u32[]{:S(2)}) collective-permute-start(f32[40,3,8,1]{3,2,1,0:T(8,128)S(1)} %get-tuple-element.343), channel_id=1, source_target_pairs={{0,4},{4,8},{8,12},{12,16},{16,20},{20,24},{24,28},{28,32},{32,36}... | collective-permute-start | bytes 11528 | tf_op jit(solution)/shard_map/ppermute | solution.py:21
  1127.5 12.3 %collective-permute-start.27 = (f32[40,3,8,1]{3,2,1,0:T(8,128)S(1)}, f32[40,3,8,1]{3,2,1,0:T(8,128)S(1)}, u32[]{:S(2)}, u32[]{:S(2)}) collective-permute-start(f32[40,3,8,1]{3,2,1,0:T(8,128)S(1)} %get-tuple-element.344), channel_id=1, source_target_pairs={{4,0},{8,4},{12,8},{16,12},{20,16},{24,20},{28,24},{32,28},{36,32}... | collective-permute-start | bytes 11528 | tf_op jit(solution)/shard_map/ppermute | solution.py:22
  1129.5 13.3 %copy-start.10 = (f32[2,8,512]{2,1,0:T(8,128)S(1)}, f32[2,8,512]{2,1,0:T(8,128)}, u32[]{:S(2)}) copy-start(f32[2,8,512]{2,1,0:T(8,128)} %param.31) | copy-start | bytes 98308
  1129.5 13.4 %copy-start.1 = (f32[39,3,8,512]{3,2,1,0:T(8,128)S(1)}, f32[39,3,8,512]{3,2,1,0:T(8,128)}, u32[]{:S(2)}) copy-start(f32[39,3,8,512]{3,2,1,0:T(8,128)} %copy-done) | copy-start | bytes 5750788
  1129.5 13.4 %copy-start.3 = (f32[40,3,8,512]{3,2,1,0:T(8,128)S(1)}, f32[40,3,8,512]{3,2,1,0:T(8,128)}, u32[]{:S(2)}) copy-start(f32[40,3,8,512]{3,2,1,0:T(8,128)} %copy-done.2) | copy-start | bytes 5898244
  1144.8 1.3 copy-start.13
where the time goes:
time: 1160 us; the launch traced here: 1150 us
  local copies, waits for them, and re-layouts  831 us (72%)
  starting transfers between devices  142 us (12%)
  waiting for transfers between devices  130 us (11%)
  other arithmetic  40.8 us (4%)
    gather x26, local copies, waits for them, and re-layouts, slot_position(): first = jnp.searchsorted(sorted_partner, sorted_partner, side='left')  599 us
    ppermute x24, waiting for transfers between devices, shifted(): return lax.ppermute(block, axis, route)  96.2 us
    ppermute x24, starting transfers between devices, shifted(): return lax.ppermute(block, axis, route)  89.6 us
    gather x2, local copies, waits for them, and re-layouts, slot_position(): sorted_partner = partner[order]  46 us
    unnamed x82, local copies, waits for them, and re-layouts  32.8 us
    gather x2, local copies, waits for them, and re-layouts, fetch(): jnp.take(table, wanted.reshape(-1), axis=0)  31.5 us
    scatter x2, local copies, waits for them, and re-layouts, fetch(): jnp.zeros((across_count * reach * capacity,), jnp.int32).at[target]  31.1 us
    scatter x2, local copies, waits for them, and re-layouts, slot_position(): return jnp.zeros_like(partner).at[order].set(ranked)  31.1 us
  transfers between devices with their start and end apart: 32, of which 16 were waited for; matrix products, arithmetic and copies ran while one was open for 33% of the time, Pallas kernels for 0%

commit v1 on v0

v1 whole, which is shorter than its diff:
```python
import functools

import jax
import jax.numpy as jnp
from jax import lax
from jax.experimental import pallas as pl
from jax.experimental.pallas import tpu as pltpu
from jax.sharding import PartitionSpec as P

LAYERS = 40
ROWS = 8
COLS = 512
CELLS = ROWS * COLS
SLOTS = 288
SPAN = 4
WIDE = 128
CHUNKS = COLS // WIDE
LEVELS = 3 * LAYERS
F32 = jnp.float32
I32 = jnp.int32
VMEM = pl.BlockSpec(memory_space=pltpu.VMEM)
SMEM = pl.BlockSpec(memory_space=pltpu.SMEM)


def iota(shape, dim):
    return lax.broadcasted_iota(I32, shape, dim)


def kernel_call(body, out_shapes, in_specs, out_specs, operands, flops=1 << 20, grid=None, scratch=(), name=None):
    extra = {} if grid is None else {"grid": grid}
    return pl.pallas_call(
        body,
        out_shape=out_shapes,
        in_specs=in_specs,
        out_specs=out_specs,
        scratch_shapes=list(scratch),
        cost_estimate=pl.CostEstimate(flops=flops, bytes_accessed=1 << 21, transcendentals=0),
        name=name,
        **extra,
    )(*operands)


def slots_body(along_ref, first_ref, second_ref, wanted_ref, own_ref):
    along = along_ref[0]
    before = (iota((COLS, COLS), 0) < iota((COLS, COLS), 1)).astype(jnp.bfloat16)
    partner_rows = iota((16, COLS), 0)
    slot_rows = iota((128, COLS), 0)
    lane_rows = iota((WIDE, COLS), 0)
    lane = iota((1, COLS), 1)
    total = jnp.zeros((512, WIDE), F32)
    for which, feet_ref in enumerate((first_ref, second_ref)):
        carry = jnp.zeros((16, 1), F32)
        for row in range(ROWS):
            feet = feet_ref[row : row + 1, :]
            global_row = feet >> 14
            column = feet & 16383
            across = global_row >> 3
            owner = column >> 9
            local = (global_row & 7) * COLS + (column & 511)
            kind = jnp.where(owner <= along, along - owner, owner)
            partner = across * SPAN + kind
            mask = partner_rows == partner
            ones = mask.astype(F32)
            prefix = jnp.dot(ones.astype(jnp.bfloat16), before, preferred_element_type=F32)
            rank = jnp.sum(jnp.where(mask, prefix + carry, 0.0), axis=0, keepdims=True).astype(I32)
            carry = carry + jnp.sum(ones, axis=1, keepdims=True)
            slot_row = partner * 8 + which * 3 + (rank >> 7)
            hit = slot_rows == slot_row
            place = (lane_rows == (rank & 127)).astype(F32).astype(jnp.bfloat16)
            own = CELLS - (row * COLS + lane)
            values = []
            for value in (local & 63, local >> 6, own & 63, own >> 6):
                values.append(jnp.where(hit, value.astype(F32), 0.0).astype(jnp.bfloat16))
            total = total + lax.dot_general(
                jnp.concatenate(values, axis=0),
                place,
                (((1,), (1,)), ((), ())),
                preferred_element_type=F32,
            )
    whole = total.astype(I32)
    wanted_ref[...] = whole[0:128] + whole[128:256] * 64
    own_ref[...] = CELLS - (whole[256:384] + whole[384:512] * 64)


def table_body(copies, x_ref, o_ref):
    for row in range(ROWS):
        if copies == 1:
            parts = [x_ref[pl.ds(m * 8 + row, LAYERS, stride=24), :] for m in range(3)]
        else:
            part = x_ref[pl.ds(row, LAYERS, stride=8), :]
            parts = [part, part, part]
        parts.append(jnp.zeros((WIDE - LEVELS, WIDE), F32))
        o_ref[row] = jnp.concatenate(parts, axis=0).T


def cells_first(x, copies):
    rows = x.shape[0]
    return kernel_call(
        functools.partial(table_body, copies),
        jax.ShapeDtypeStruct((ROWS, COLS, WIDE), F32),
        [pl.BlockSpec((rows, WIDE), lambda j: (0, j))],
        pl.BlockSpec((ROWS, WIDE, WIDE), lambda j: (0, j, 0)),
        (x,),
        grid=(CHUNKS,),
        name="cells_first",
    )


def pick_rows(which, wanted_ref, table_ref, out_ref):
    def per_across(z, _):
        def some(i, _):
            for u in range(32):
                s = i * 32 + u
                out_ref[pl.ds(z * SLOTS + s, 1), :] = table_ref[pl.ds(wanted_ref[z * 1024 + which * 384 + s], 1), :]
            return 0

        return lax.fori_loop(0, SLOTS // 32, some, 0)

    lax.fori_loop(0, 4, per_across, 0)


def pick_body(which, wanted_ref, table_ref, out_ref):
    pick_rows(which, wanted_ref, table_ref, out_ref)


def pick_back_body(which, along_ref, w1, w2, w3, table_ref, o1, o2, o3):
    @pl.when(along_ref[0] < SPAN)
    def _():
        for w, o in ((w1, o1), (w2, o2), (w3, o3)):
            pick_rows(which, w, table_ref, o)


MESSAGE = jax.ShapeDtypeStruct((4 * SLOTS, WIDE), F32)


def pick(which, wanted, table):
    return kernel_call(
        functools.partial(pick_body, which), MESSAGE, [SMEM, VMEM], VMEM, (wanted, table), flops=1 << 24, name="pick"
    )


def pick_back(which, along, wanted, table):
    return kernel_call(
        functools.partial(pick_back_body, which),
        (MESSAGE,) * 3,
        [SMEM] * 4 + [VMEM],
        (VMEM,) * 3,
        (along, *wanted, table),
        name="pick_back",
    )


def place_body(which, own_ref, x0, x1, x2, x3, weight_ref, out_ref, cells):
    for kind, x in enumerate((x0, x1, x2, x3)):
        def per_across(z, _, kind=kind, x=x):
            def some(i, _):
                for u in range(32):
                    s = i * 32 + u
                    cell = own_ref[(z * SPAN + kind) * 1024 + which * 384 + s]
                    cells[pl.ds(cell, 1), :] = x[pl.ds(z * SLOTS + s, 1), :]
                return 0

            return lax.fori_loop(0, SLOTS // 32, some, 0)

        lax.fori_loop(0, 4, per_across, 0)
    lane = iota((64, WIDE), 1)
    top = (lane == LAYERS - 1) | (lane == 2 * LAYERS - 1) | (lane == 3 * LAYERS - 1)

    def mix(i, _):
        rows = pl.ds(pl.multiple_of(i * 64, 64), 64)
        here = cells[rows, :]
        upper = jnp.where(top, here, pltpu.roll(here, WIDE - 1, 1))
        weight = weight_ref[rows, :]
        out_ref[rows, :] = (1.0 - weight) * here + weight * upper
        return 0

    lax.fori_loop(0, CELLS // 64, mix, 0)


def place(which, own, xs, weight):
    return kernel_call(
        functools.partial(place_body, which),
        jax.ShapeDtypeStruct((CELLS, WIDE), F32),
        [SMEM] + [VMEM] * 5,
        VMEM,
        (own, *xs, weight),
        scratch=[pltpu.VMEM((CELLS + 8, WIDE), F32)],
        name="place",
    )


def pivots_body(mix_ref, drag_ref, out_ref):
    for which in range(2):
        factor = None
        for k in range(LAYERS):
            below = None if k == 0 else mix_ref[(which * 39 + k - 1) * 8 : (which * 39 + k) * 8, :]
            above = None if k == LAYERS - 1 else mix_ref[(which * 39 + k) * 8 : (which * 39 + k + 1) * 8, :]
            diagonal = 1.0
            for term in (below, above):
                if term is not None:
                    diagonal = diagonal + term
            if k == 0 and which == 0:
                diagonal = diagonal + drag_ref[...]
            if k > 0:
                diagonal = diagonal - below * factor
            inverse = 1.0 / diagonal
            out_ref[(which * LAYERS + k) * 8 : (which * LAYERS + k + 1) * 8, :] = inverse
            if above is not None:
                factor = above * inverse


def pivots(mix, drag):
    return kernel_call(
        pivots_body,
        jax.ShapeDtypeStruct((2 * LAYERS * 8, COLS), F32),
        [pl.BlockSpec((2 * 39 * 8, WIDE), lambda j: (0, j)), pl.BlockSpec((8, WIDE), lambda j: (0, j))],
        pl.BlockSpec((2 * LAYERS * 8, WIDE), lambda j: (0, j)),
        (mix, drag),
        grid=(CHUNKS,),
        name="pivots",
    )


def layers_body(x_ref, o_ref):
    for row in range(ROWS):
        o_ref[pl.ds(row, LEVELS, stride=8), :] = x_ref[row].T[0:LEVELS, :]


def layers_first(x):
    return kernel_call(
        layers_body,
        jax.ShapeDtypeStruct((CHUNKS * LEVELS * 8, WIDE), F32),
        [pl.BlockSpec((ROWS, WIDE, WIDE), lambda j: (0, j, 0))],
        pl.BlockSpec((LEVELS * 8, WIDE), lambda j: (j, 0)),
        (x,),
        grid=(CHUNKS,),
        name="layers_first",
    )


def solve_body(
    place_ref, moved_ref, up_ref, down_ref, left_ref, right_ref, lateral_ref, mix_ref, inverse_ref, stress_ref, out_ref, edge
):
    j = pl.program_id(0)
    sub, lane = iota((8, WIDE), 0), iota((8, WIDE), 1)
    size = LEVELS * 8

    def spread(source_ref):
        source = source_ref[...]
        for level in range(LEVELS):
            edge[level * 8 : level * 8 + 8, :] = jnp.broadcast_to(source[:, level : level + 1], (8, WIDE))

    @pl.when(j == 0)
    def _():
        spread(left_ref)

    @pl.when(j == CHUNKS - 1)
    def _():
        spread(right_ref)

    start = pl.multiple_of(j * size, size)
    before = pl.multiple_of(jnp.maximum(j - 1, 0) * size, size)
    after = pl.multiple_of(jnp.minimum(j + 1, CHUNKS - 1) * size, size)
    up, down = up_ref[...].T, down_ref[...].T
    lateral = lateral_ref[...]
    count = 4.0 - (
        ((place_ref[0] == 0) & (j == 0) & (lane == 0)).astype(F32)
        + ((place_ref[0] == 31) & (j == CHUNKS - 1) & (lane == WIDE - 1)).astype(F32)
        + ((place_ref[1] == 0) & (sub == 0)).astype(F32)
        + ((place_ref[1] == 3) & (sub == 7)).astype(F32)
    )
    first_chunk, last_chunk = j == 0, j == CHUNKS - 1
    for m in range(3):
        which = 0 if m < 2 else 1
        value = None
        for k in range(LAYERS):
            level = m * LAYERS + k
            at = level * 8
            here = moved_ref[pl.ds(start + at, 8), :]
            halo = edge[at : at + 8, :]
            lower = jnp.where(first_chunk, halo, moved_ref[pl.ds(before + at, 8), :])
            upper = jnp.where(last_chunk, halo, moved_ref[pl.ds(after + at, 8), :])
            west = jnp.where(lane == 0, pltpu.roll(lower, 1, 1), pltpu.roll(here, 1, 1))
            east = jnp.where(lane == WIDE - 1, pltpu.roll(upper, WIDE - 1, 1), pltpu.roll(here, WIDE - 1, 1))
            north = jnp.where(sub == 0, up[level : level + 1, :], pltpu.roll(here, 1, 0))
            south = jnp.where(sub == 7, down[level : level + 1, :], pltpu.roll(here, 7, 0))
            source = here + lateral * (((north + south) + west) + east - count * here)
            if k == LAYERS - 1 and m < 2:
                source = source + stress_ref[m * 8 : m * 8 + 8, :]
            if k > 0:
                source = source + mix_ref[(which * 39 + k - 1) * 8 : (which * 39 + k) * 8, :] * value
            value = source * inverse_ref[(which * LAYERS + k) * 8 : (which * LAYERS + k + 1) * 8, :]
            out_ref[(k * 3 + m) * 8 : (k * 3 + m + 1) * 8, :] = value
        for k in range(LAYERS - 2, -1, -1):
            rows = slice((k * 3 + m) * 8, (k * 3 + m + 1) * 8)
            factor = (
                mix_ref[(which * 39 + k) * 8 : (which * 39 + k + 1) * 8, :]
                * inverse_ref[(which * LAYERS + k) * 8 : (which * LAYERS + k + 1) * 8, :]
            )
            value = out_ref[rows, :] + factor * value
            out_ref[rows, :] = value


def solve(where, moved, up, down, left, right, lateral, mix, inverse, stress):
    def chunk(rows):
        return pl.BlockSpec((rows, WIDE), lambda j: (0, j))

    def cells(rows):
        return pl.BlockSpec((rows, WIDE), lambda j: (j, 0))

    def fixed(rows):
        return pl.BlockSpec((rows, WIDE), lambda j: (0, 0))

    return kernel_call(
        solve_body,
        jax.ShapeDtypeStruct((LEVELS * 8, COLS), F32),
        [
            SMEM,
            fixed(CHUNKS * LEVELS * 8),
            cells(WIDE),
            cells(WIDE),
            fixed(8),
            fixed(8),
            chunk(8),
            chunk(2 * 39 * 8),
            chunk(2 * LAYERS * 8),
            chunk(16),
        ],
        chunk(LEVELS * 8),
        (where, moved, up, down, left, right, lateral, mix, inverse, stress),
        grid=(CHUNKS,),
        scratch=[pltpu.VMEM((LEVELS * 8, WIDE), F32)],
        name="solve",
    )


def move(x, axis, distance, low=0, high=None):
    count = lax.axis_size(axis)
    high = count if high is None else high
    pairs = [(i, i + distance) for i in range(low, high) if 0 <= i + distance < count]
    return lax.ppermute(x, axis, pairs)


def body(fields, first_feet, first_fraction, second_feet, second_fraction, lateral_mix, vertical_mix, bottom_drag, surface_stress):
    along = lax.axis_index("along")
    across = lax.axis_index("across")
    where = jnp.stack([along, across]).astype(I32)

    wanted, own = kernel_call(
        slots_body,
        (jax.ShapeDtypeStruct((128, WIDE), I32),) * 2,
        [SMEM, VMEM, VMEM],
        (VMEM, VMEM),
        (where, first_feet, second_feet),
        name="slots",
    )
    own = own.reshape(-1)
    wanted = lax.all_to_all(wanted.reshape(4, SPAN, 8, WIDE), "across", split_axis=0, concat_axis=0, tiled=True)
    ahead = [wanted[:, 0]] + [move(wanted[:, t], "along", -t) for t in range(1, SPAN)]
    back = []
    for u in range(1, SPAN):
        payload = lax.dynamic_index_in_dim(wanted, jnp.minimum(along + u, SPAN - 1), axis=1, keepdims=False)
        pairs = [(i, i + u) for i in range(SPAN - u)]
        back.append(lax.ppermute(payload, "along", pairs))
    ahead = [x.reshape(-1) for x in ahead]
    back = [x.reshape(-1) for x in back]

    def fetch(which, table):
        sent = {}
        for t in (3, 2, 1):
            sent[t] = move(pick(which, ahead[t], table), "along", t)
        behind = [
            lax.ppermute(x, "along", [(i, i - u) for i in range(u, SPAN)])
            for u, x in zip((1, 2, 3), pick_back(which, where, back, table))
        ]
        parts = [pick(which, ahead[0], table)]
        for t in range(1, SPAN):
            part = sent[t]
            for a in range(t):
                part = jnp.where(along == a, behind[t - a - 1], part)
            parts.append(part)
        return [
            lax.all_to_all(x.reshape(4, SLOTS, WIDE), "across", split_axis=0, concat_axis=0, tiled=True).reshape(-1, WIDE)
            for x in parts
        ]

    table = cells_first(fields.reshape(LEVELS * 8, COLS), 1).reshape(CELLS, WIDE)
    first_weight = cells_first(first_fraction.reshape(LAYERS * 8, COLS), 3).reshape(CELLS, WIDE)
    second_weight = cells_first(second_fraction.reshape(LAYERS * 8, COLS), 3).reshape(CELLS, WIDE)
    mix = vertical_mix.reshape(2 * 39 * 8, COLS)
    inverse = pivots(mix, bottom_drag)

    middle = place(0, own, fetch(0, table), first_weight)
    moved = place(1, own, fetch(1, middle), second_weight).reshape(ROWS, COLS, WIDE)
    up = move(moved[ROWS - 1], "across", 1)
    down = move(moved[0], "across", -1)
    left = move(moved[:, COLS - 1], "along", 1)
    right = move(moved[:, 0], "along", -1)
    result = solve(
        where, layers_first(moved), up, down, left, right, lateral_mix, mix, inverse, surface_stress.reshape(16, COLS)
    )
    return result.reshape(LAYERS, 3, ROWS, COLS)


def solution(mesh):
    in_specs = (
        P(None, None, "across", "along"),
        P("across", "along"),
        P(None, "across", "along"),
        P("across", "along"),
        P(None, "across", "along"),
        P("across", "along"),
        P(None, None, "across", "along"),
        P("across", "along"),
        P(None, "across", "along"),
    )
    out_specs = P(None, None, "across", "along")
    return jax.shard_map(body, mesh=mesh, in_specs=in_specs, out_specs=out_specs, check_vma=False)
```

time: 1160 us -> 287 us (0.25)
  the two profiles are of different devices: /device:TPU:61 before, /device:TPU:1 now
where the time goes in v1:
time: 287 us; the launch traced here: 285 us
  Pallas kernels  108 us (38%)
  starting transfers between devices  69.9 us (24%)
  blocking collectives  48.7 us (17%)
  waiting for transfers between devices  45.1 us (16%)
  local copies, waits for them, and re-layouts  7.18 us (3%)
  other arithmetic  5.48 us (2%)
    pallas_call x19, Pallas kernels, kernel_call(): pl.pallas_call(body, out_shape=out_shapes, in_specs=in_specs, out_specs=o...  108 us
    all_to_all x4, blocking collectives, fetch(): lax.all_to_all(x.reshape(4, SLOTS, WIDE), 'across', split_axis=0, concat_...  48.7 us
    ppermute x13, starting transfers between devices, move(): return lax.ppermute(x, axis, pairs)  32.7 us
    ppermute x13, waiting for transfers between devices, move(): return lax.ppermute(x, axis, pairs)  27.7 us
    all_to_all x4, starting transfers between devices, fetch(): lax.all_to_all(x.reshape(4, SLOTS, WIDE), 'across', split_axis=0, concat_...  13.9 us
    all_to_all x4, waiting for transfers between devices, fetch(): lax.all_to_all(x.reshape(4, SLOTS, WIDE), 'across', split_axis=0, concat_...  12.9 us
    ppermute x6, starting transfers between devices, fetch(): lax.ppermute(x, 'along', [(i, i - u) for i in range(u, SPAN)])  10.4 us
    ppermute x3, starting transfers between devices, body(): back.append(lax.ppermute(payload, 'along', pairs))  7.14 us
  transfers between devices with their start and end apart: 27, of which 8 were waited for; matrix products, arithmetic and copies ran while one was open for 2% of the time, Pallas kernels for 18%

profile of v1, /device:TPU:1, one launch (start us, length us, event | category | flops | bytes accessed | tf_op | source)
XLA Modules:
  0.0 285.0 jit_solution(8973853797196578865)
XLA Ops:
  0.6 7.0 %slots.1 = (s32[128,128]{1,0:T(8,128)}, s32[128,128]{1,0:T(8,128)}) custom-call(s32[2]{0:T(128)} %pad_add_fusion.along_ref.place_ref, s32[8,512]{1,0:T(8,128)} %first_ref.1, s32[8,512]{1,0:T(8,128)} %second_ref.1), custom_call_target="tpu_custom_call" | custom-call | flops 1048576 | bytes 2097152 | tf_op jit(solution)/shard_map/slots/pallas_call | solution.py:31
  7.6 5.8 %all-to-all-start = ((s32[4,4,8,128]{3,2,1,0:T(8,128)}), s32[4,4,8,128]{3,2,1,0:T(8,128)S(1)}, u32[]{:S(2)}, u32[]{:S(2)}) async-start(s32[4,4,8,128]{3,2,1,0:T(8,128)} %bitcast.98), calls=%async_computation | async-start | bytes 131072 | tf_op jit(solution)/shard_map/all_to_all | solution.py:358
  13.4 4.5 %all-to-all-done = s32[4,4,8,128]{3,2,1,0:T(8,128)S(1)} async-done(((s32[4,4,8,128]{3,2,1,0:T(8,128)}), s32[4,4,8,128]{3,2,1,0:T(8,128)S(1)}, u32[]{:S(2)}, u32[]{:S(2)}) %all-to-all-start) | async-done | bytes 65568 | tf_op jit(solution)/shard_map/all_to_all | solution.py:358
  18.5 5.2 %collective-permute-start = (s32[4,8,128]{2,1,0:T(8,128)S(1)}, s32[4,8,128]{2,1,0:T(8,128)S(1)}, u32[]{:S(2)}, u32[]{:S(2)}) collective-permute-start(s32[4,8,128]{2,1,0:T(8,128)S(1)} %get-tuple-element.36), channel_id=1, source_target_pairs={{0,4},{4,8},{8,12},{1,5},{5,9},{9,13},{2,6},{6,10},{10,14},{3,7},{... | collective-permute-start | bytes 49160 | tf_op jit(solution)/shard_map/ppermute | solution.py:364
  25.7 4.2 %cells_first.3 = f32[8,512,128]{2,1,0:T(8,128)} custom-call(f32[960,512]{1,0:T(8,128)} %bitcast.81), custom_call_target="tpu_custom_call" | custom-call | flops 1048576 | bytes 2097152 | tf_op jit(solution)/shard_map/cells_first/pallas_call | solution.py:31
  30.5 7.1 %pick_back.2 = (f32[1152,128]{1,0:T(8,128)}, f32[1152,128]{1,0:T(8,128)}, f32[1152,128]{1,0:T(8,128)}) custom-call(s32[2]{0:T(128)} %pad_add_fusion.along_ref.place_ref, s32[4096]{0:T(1024)} %bitcast.86, s32[4096]{0:T(1024)} %bitcast.88, s32[4096]{0:T(1024)} %bitcast.90, f32[4096,128]{1,0:T(8,128)} %bitcast.56), custom_call_target="tpu_custom_call" | custom-call | flops 1048576 | bytes 2097152 | tf_op jit(solution)/shard_map/pick_back/pallas_call | solution.py:31
  37.5 3.5 %collective-permute-start.3 = (f32[1152,128]{1,0:T(8,128)}, f32[1152,128]{1,0:T(8,128)S(1)}, u32[]{:S(2)}, u32[]{:S(2)}) collective-permute-start(f32[1152,128]{1,0:T(8,128)} %get-tuple-element.15), channel_id=1, source_target_pairs={{4,0},{8,4},{12,8},{5,1},{9,5},{13,9},{6,2},{10,6},{14,10},{7,3},{... | collective-permute-start | bytes 1769480 | tf_op jit(solution)/shard_map/ppermute | solution.py:373
  43.7 1.9 collective-permute-start.4
  48.4 3.8 %pick.11 = f32[1152,128]{1,0:T(8,128)} custom-call(s32[4096]{0:T(1024)} %bitcast.92, f32[4096,128]{1,0:T(8,128)} %bitcast.57), custom_call_target="tpu_custom_call" | custom-call | flops 16777216 | bytes 2097152 | tf_op jit(solution)/shard_map/pick/pallas_call | solution.py:31
  52.2 5.1 %collective-permute-start.11 = (f32[1152,128]{1,0:T(8,128)}, f32[1152,128]{1,0:T(8,128)S(1)}, u32[]{:S(2)}, u32[]{:S(2)}) collective-permute-start(f32[1152,128]{1,0:T(8,128)} %pick.11), channel_id=1, source_target_pairs={{0,12},{4,16},{8,20},{12,24},{16,28},{20,32},{24,36},{28,40},{32,4... | collective-permute-start | bytes 1769480 | tf_op jit(solution)/shard_map/ppermute | solution.py:341
  57.3 3.9 %pick.10 = f32[1152,128]{1,0:T(8,128)} custom-call(s32[4096]{0:T(1024)} %bitcast.94, f32[4096,128]{1,0:T(8,128)} %bitcast.58), custom_call_target="tpu_custom_call" | custom-call | flops 16777216 | bytes 2097152 | tf_op jit(solution)/shard_map/pick/pallas_call | solution.py:31
  61.2 3.0 %collective-permute-start.8 = (f32[1152,128]{1,0:T(8,128)}, f32[1152,128]{1,0:T(8,128)S(1)}, u32[]{:S(2)}, u32[]{:S(2)}) collective-permute-start(f32[1152,128]{1,0:T(8,128)} %pick.10), channel_id=1, source_target_pairs={{0,8},{4,12},{8,16},{12,20},{16,24},{20,28},{24,32},{28,36},{32,40... | collective-permute-start | bytes 1769480 | tf_op jit(solution)/shard_map/ppermute | solution.py:341
  64.3 3.9 %pick.9 = f32[1152,128]{1,0:T(8,128)} custom-call(s32[4096]{0:T(1024)} %bitcast.96, f32[4096,128]{1,0:T(8,128)} %bitcast.59), custom_call_target="tpu_custom_call" | custom-call | flops 16777216 | bytes 2097152 | tf_op jit(solution)/shard_map/pick/pallas_call | solution.py:31
  68.1 2.8 collective-permute-start.5
  71.0 3.8 %pick.8 = f32[1152,128]{1,0:T(8,128)} custom-call(s32[4096]{0:T(1024)} %get-tuple-element.37.wanted_ref, f32[4096,128]{1,0:T(8,128)} %bitcast.60), custom_call_target="tpu_custom_call" | custom-call | flops 16777216 | bytes 2097152 | tf_op jit(solution)/shard_map/pick/pallas_call | solution.py:31
  74.8 3.5 %all-to-all-start.1 = ((f32[4,288,128]{2,1,0:T(8,128)}), f32[4,288,128]{2,1,0:T(8,128)S(1)}, u32[]{:S(2)}, u32[]{:S(2)}) async-start(f32[4,288,128]{2,1,0:T(8,128)} %bitcast.80), calls=%async_computation.1 | async-start | bytes 1179648 | tf_op jit(solution)/shard_map/all_to_all | solution.py:383
  78.3 4.5 %collective-permute-done.8 = f32[1152,128]{1,0:T(8,128)S(1)} collective-permute-done((f32[1152,128]{1,0:T(8,128)}, f32[1152,128]{1,0:T(8,128)S(1)}, u32[]{:S(2)}, u32[]{:S(2)}) %collective-permute-start.8) | collective-permute-done | bytes 589856 | tf_op jit(solution)/shard_map/ppermute | solution.py:341
  83.7 5.5 %collective-permute-done.5 = f32[1152,128]{1,0:T(8,128)} collective-permute-done((f32[1152,128]{1,0:T(8,128)}, f32[1152,128]{1,0:T(8,128)}, u32[]{:S(2)}, u32[]{:S(2)}) %collective-permute-start.5) | collective-permute-done | bytes 589856 | tf_op jit(solution)/shard_map/ppermute | solution.py:341
  89.1 2.4 select_select_fusion.2
  91.6 11.8 %all_to_all.45 = f32[4,288,128]{2,1,0:T(8,128)} all-to-all(f32[4,288,128]{2,1,0:T(8,128)S(1)} %bitcast.76), channel_id=1, replica_groups=mesh['along'=32,'across'=4] {'across'}, dimensions={0} | all-to-all | bytes 1179648 | tf_op jit(solution)/shard_map/all_to_all | solution.py:383
  103.4 13.0 %all_to_all.46 = f32[4,288,128]{2,1,0:T(8,128)} all-to-all(f32[4,288,128]{2,1,0:T(8,128)S(1)} %bitcast.75), channel_id=1, replica_groups=mesh['along'=32,'across'=4] {'across'}, dimensions={0} | all-to-all | bytes 1179648 | tf_op jit(solution)/shard_map/all_to_all | solution.py:383
  116.3 3.5 %all-to-all-start.4 = ((f32[4,288,128]{2,1,0:T(8,128)}), f32[4,288,128]{2,1,0:T(8,128)S(1)}, u32[]{:S(2)}, u32[]{:S(2)}) async-start(f32[4,288,128]{2,1,0:T(8,128)} %bitcast.25), calls=%async_computation.4 | async-start | bytes 1179648 | tf_op jit(solution)/shard_map/all_to_all | solution.py:383
  119.8 3.9 %cells_first.4 = f32[8,512,128]{2,1,0:T(8,128)} custom-call(f32[320,512]{1,0:T(8,128)} %bitcast.82), custom_call_target="tpu_custom_call" | custom-call | flops 1048576 | bytes 2097152 | tf_op jit(solution)/shard_map/cells_first/pallas_call | solution.py:31
  123.7 6.3 %all-to-all-done.4 = f32[4,288,128]{2,1,0:T(8,128)S(1)} async-done(((f32[4,288,128]{2,1,0:T(8,128)}), f32[4,288,128]{2,1,0:T(8,128)S(1)}, u32[]{:S(2)}, u32[]{:S(2)}) %all-to-all-start.4) | async-done | bytes 589856 | tf_op jit(solution)/shard_map/all_to_all | solution.py:383
  130.8 14.4 %place.2.table_ref = f32[4096,128]{1,0:T(8,128)} custom-call(s32[16384]{0:T(1024)} %bitcast.84, f32[1152,128]{1,0:T(8,128)} %bitcast.68, f32[1152,128]{1,0:T(8,128)} %bitcast.70, f32[1152,128]{1,0:T(8,128)} %bitcast.73, f32[1152,128]{1,0:T(8,128)} %bitcast.77, f32[4096,128]{1,0:T(8,128)} %bitcast.63), custom_call_target="tpu_custom_call" | custom-call | flops 1048576 | bytes 2097152 | tf_op jit(solution)/shard_map/place/pallas_call | solution.py:31
  145.2 7.2 %pick_back.3 = (f32[1152,128]{1,0:T(8,128)}, f32[1152,128]{1,0:T(8,128)}, f32[1152,128]{1,0:T(8,128)}) custom-call(s32[2]{0:T(128)} %pad_add_fusion.along_ref.place_ref, s32[4096]{0:T(1024)} %bitcast.87, s32[4096]{0:T(1024)} %bitcast.89, s32[4096]{0:T(1024)} %bitcast.91, f32[4096,128]{1,0:T(8,128)} %place.2.table_ref), custom_call_target="tpu_custom_call" | custom-call | flops 1048576 | bytes 2097152 | tf_op jit(solution)/shard_map/pick_back/pallas_call | solution.py:31
  152.3 2.9 %collective-permute-start.12 = (f32[1152,128]{1,0:T(8,128)}, f32[1152,128]{1,0:T(8,128)S(1)}, u32[]{:S(2)}, u32[]{:S(2)}) collective-permute-start(f32[1152,128]{1,0:T(8,128)} %get-tuple-element.18), channel_id=1, source_target_pairs={{4,0},{8,4},{12,8},{5,1},{9,5},{13,9},{6,2},{10,6},{14,10},{7,3},{... | collective-permute-start | bytes 1769480 | tf_op jit(solution)/shard_map/ppermute | solution.py:373
  156.5 3.9 %pick.15 = f32[1152,128]{1,0:T(8,128)} custom-call(s32[4096]{0:T(1024)} %bitcast.93, f32[4096,128]{1,0:T(8,128)} %place.2.table_ref), custom_call_target="tpu_custom_call" | custom-call | flops 16777216 | bytes 2097152 | tf_op jit(solution)/shard_map/pick/pallas_call | solution.py:31
  160.4 3.9 %pick.14 = f32[1152,128]{1,0:T(8,128)} custom-call(s32[4096]{0:T(1024)} %bitcast.95, f32[4096,128]{1,0:T(8,128)} %place.2.table_ref), custom_call_target="tpu_custom_call" | custom-call | flops 16777216 | bytes 2097152 | tf_op jit(solution)/shard_map/pick/pallas_call | solution.py:31
  164.3 3.9 %pick.13 = f32[1152,128]{1,0:T(8,128)} custom-call(s32[4096]{0:T(1024)} %bitcast.97, f32[4096,128]{1,0:T(8,128)} %place.2.table_ref), custom_call_target="tpu_custom_call" | custom-call | flops 16777216 | bytes 2097152 | tf_op jit(solution)/shard_map/pick/pallas_call | solution.py:31
  170.2 5.3 %collective-permute-start.15 = (f32[1152,128]{1,0:T(8,128)}, f32[1152,128]{1,0:T(8,128)S(1)}, u32[]{:S(2)}, u32[]{:S(2)}) collective-permute-start(f32[1152,128]{1,0:T(8,128)} %pick.14), channel_id=1, source_target_pairs={{0,8},{4,12},{8,16},{12,20},{16,24},{20,28},{24,32},{28,36},{32,40... | collective-permute-start | bytes 1769480 | tf_op jit(solution)/shard_map/ppermute | solution.py:341
  175.5 1.9 collective-permute-start.13
  177.4 3.9 %pick.12 = f32[1152,128]{1,0:T(8,128)} custom-call(s32[4096]{0:T(1024)} %get-tuple-element.37.wanted_ref, f32[4096,128]{1,0:T(8,128)} %place.2.table_ref), custom_call_target="tpu_custom_call" | custom-call | flops 16777216 | bytes 2097152 | tf_op jit(solution)/shard_map/pick/pallas_call | solution.py:31
  181.3 3.5 %all-to-all-start.5 = ((f32[4,288,128]{2,1,0:T(8,128)}), f32[4,288,128]{2,1,0:T(8,128)S(1)}, u32[]{:S(2)}, u32[]{:S(2)}) async-start(f32[4,288,128]{2,1,0:T(8,128)} %bitcast.79), calls=%async_computation.5 | async-start | bytes 1179648 | tf_op jit(solution)/shard_map/all_to_all | solution.py:383
  184.8 7.6 %collective-permute-done.15 = f32[1152,128]{1,0:T(8,128)S(1)} collective-permute-done((f32[1152,128]{1,0:T(8,128)}, f32[1152,128]{1,0:T(8,128)S(1)}, u32[]{:S(2)}, u32[]{:S(2)}) %collective-permute-start.15) | collective-permute-done | bytes 589856 | tf_op jit(solution)/shard_map/ppermute | solution.py:341
  193.2 9.4 %collective-permute-done.13 = f32[1152,128]{1,0:T(8,128)} collective-permute-done((f32[1152,128]{1,0:T(8,128)}, f32[1152,128]{1,0:T(8,128)}, u32[]{:S(2)}, u32[]{:S(2)}) %collective-permute-start.13) | collective-permute-done | bytes 589856 | tf_op jit(solution)/shard_map/ppermute | solution.py:341
  202.6 2.4 select_select_fusion
  205.1 11.4 %all_to_all.47 = f32[4,288,128]{2,1,0:T(8,128)} all-to-all(f32[4,288,128]{2,1,0:T(8,128)S(1)} %bitcast.71), channel_id=1, replica_groups=mesh['along'=32,'across'=4] {'across'}, dimensions={0} | all-to-all | bytes 1179648 | tf_op jit(solution)/shard_map/all_to_all | solution.py:383
  216.4 12.5 %all_to_all.48 = f32[4,288,128]{2,1,0:T(8,128)} all-to-all(f32[4,288,128]{2,1,0:T(8,128)S(1)} %bitcast.69), channel_id=1, replica_groups=mesh['along'=32,'across'=4] {'across'}, dimensions={0} | all-to-all | bytes 1179648 | tf_op jit(solution)/shard_map/all_to_all | solution.py:383
  229.0 3.5 %all-to-all-start.8 = ((f32[4,288,128]{2,1,0:T(8,128)}), f32[4,288,128]{2,1,0:T(8,128)S(1)}, u32[]{:S(2)}, u32[]{:S(2)}) async-start(f32[4,288,128]{2,1,0:T(8,128)} %bitcast.35), calls=%async_computation.8 | async-start | bytes 1179648 | tf_op jit(solution)/shard_map/all_to_all | solution.py:383
  232.4 3.9 %cells_first.5 = f32[8,512,128]{2,1,0:T(8,128)} custom-call(f32[320,512]{1,0:T(8,128)} %bitcast.83), custom_call_target="tpu_custom_call" | custom-call | flops 1048576 | bytes 2097152 | tf_op jit(solution)/shard_map/cells_first/pallas_call | solution.py:31
  236.3 6.7 %all-to-all-done.8 = f32[4,288,128]{2,1,0:T(8,128)S(1)} async-done(((f32[4,288,128]{2,1,0:T(8,128)}), f32[4,288,128]{2,1,0:T(8,128)S(1)}, u32[]{:S(2)}, u32[]{:S(2)}) %all-to-all-start.8) | async-done | bytes 589856 | tf_op jit(solution)/shard_map/all_to_all | solution.py:383
  243.8 14.4 %place.3 = f32[4096,128]{1,0:T(8,128)} custom-call(s32[16384]{0:T(1024)} %bitcast.85, f32[1152,128]{1,0:T(8,128)} %bitcast.67, f32[1152,128]{1,0:T(8,128)} %bitcast.72, f32[1152,128]{1,0:T(8,128)} %bitcast.74, f32[1152,128]{1,0:T(8,128)} %bitcast.78, f32[4096,128]{1,0:T(8,128)} %bitcast.64), custom_call_target="tpu_custom_call" | custom-call | flops 1048576 | bytes 2097152 | tf_op jit(solution)/shard_map/place/pallas_call | solution.py:31
  259.3 2.2 collective-permute-start.18
  263.6 3.3 %collective-permute-start.20 = (f32[8,128]{1,0:T(8,128)S(1)}, f32[8,128]{1,0:T(8,128)S(1)}, u32[]{:S(2)}, u32[]{:S(2)}) collective-permute-start(f32[8,128]{1,0:T(8,128)S(1)} %bitcast.101), channel_id=1, source_target_pairs={{0,4},{4,8},{8,12},{12,16},{16,20},{20,24},{24,28},{28,32},{32,36}... | collective-permute-start | bytes 12296 | tf_op jit(solution)/shard_map/ppermute | solution.py:341
  268.9 4.2 %pivots.1.inverse_ref = f32[640,512]{1,0:T(8,128)} custom-call(f32[624,512]{1,0:T(8,128)} %bitcast.65, f32[8,512]{1,0:T(8,128)} %drag_ref.1), custom_call_target="tpu_custom_call" | custom-call | flops 1048576 | bytes 2097152 | tf_op jit(solution)/shard_map/pivots/pallas_call | solution.py:31
  273.0 4.1 %layers_first.1.moved_ref = f32[3840,128]{1,0:T(8,128)} custom-call(f32[8,512,128]{2,1,0:T(8,128)} %bitcast.62), custom_call_target="tpu_custom_call" | custom-call | flops 1048576 | bytes 2097152 | tf_op jit(solution)/shard_map/layers_first/pallas_call | solution.py:31
  278.0 7.0 %solve.1 = f32[960,512]{1,0:T(8,128)} custom-call(s32[2]{0:T(128)} %pad_add_fusion.along_ref.place_ref, f32[3840,128]{1,0:T(8,128)} %layers_first.1.moved_ref, f32[512,128]{1,0:T(8,128)} %copy-done.8, f32[512,128]{1,0:T(8,128)} %copy-done.9, f32[8,128]{1,0:T(8,128)} %copy-done.16, f32[8,128]{1,0:T(8,128)} %copy-done.17, f32[8,512]{1,0:T(8,128)} %lateral_ref.1, ...), custom_call_target="tpu_custom_call" | custom-call | flops 1048576 | bytes 2097152 | tf_op jit(solution)/shard_map/solve/pallas_call | solution.py:31
  (71 shorter events, 21.6 us)
Async XLA Ops:
  7.6 10.3 %all-to-all-start = ((s32[4,4,8,128]{3,2,1,0:T(8,128)}), s32[4,4,8,128]{3,2,1,0:T(8,128)S(1)}, u32[]{:S(2)}, u32[]{:S(2)}) async-start(s32[4,4,8,128]{3,2,1,0:T(8,128)} %bitcast.98), calls=%async_computation | async-start | bytes 131072 | tf_op jit(solution)/shard_map/all_to_all | solution.py:358
  18.5 11.3 %collective-permute-start = (s32[4,8,128]{2,1,0:T(8,128)S(1)}, s32[4,8,128]{2,1,0:T(8,128)S(1)}, u32[]{:S(2)}, u32[]{:S(2)}) collective-permute-start(s32[4,8,128]{2,1,0:T(8,128)S(1)} %get-tuple-element.36), channel_id=1, source_target_pairs={{0,4},{4,8},{8,12},{1,5},{5,9},{9,13},{2,6},{6,10},{10,14},{3,7},{... | collective-permute-start | bytes 49160 | tf_op jit(solution)/shard_map/ppermute | solution.py:364
  23.7 6.1 %collective-permute-start.1 = (s32[4,8,128]{2,1,0:T(8,128)S(1)}, s32[4,8,128]{2,1,0:T(8,128)S(1)}, u32[]{:S(2)}, u32[]{:S(2)}) collective-permute-start(s32[4,8,128]{2,1,0:T(8,128)S(1)} %get-tuple-element.35), channel_id=1, source_target_pairs={{0,8},{4,12},{1,9},{5,13},{2,10},{6,14},{3,11},{7,15}} | collective-permute-start | bytes 49160 | tf_op jit(solution)/shard_map/ppermute | solution.py:364
  25.0 4.8 %collective-permute-start.2 = (s32[4,8,128]{2,1,0:T(8,128)S(1)}, s32[4,8,128]{2,1,0:T(8,128)S(1)}, u32[]{:S(2)}, u32[]{:S(2)}) collective-permute-start(s32[4,8,128]{2,1,0:T(8,128)S(1)} %get-tuple-element.34), channel_id=1, source_target_pairs={{0,12},{1,13},{2,14},{3,15}} | collective-permute-start | bytes 49160 | tf_op jit(solution)/shard_map/ppermute | solution.py:364
  29.8 0.6 copy-start.10
  29.8 0.6 copy-start.11
  29.9 0.6 copy-start.12
  37.5 30.6 %collective-permute-start.3 = (f32[1152,128]{1,0:T(8,128)}, f32[1152,128]{1,0:T(8,128)S(1)}, u32[]{:S(2)}, u32[]{:S(2)}) collective-permute-start(f32[1152,128]{1,0:T(8,128)} %get-tuple-element.15), channel_id=1, source_target_pairs={{4,0},{8,4},{12,8},{5,1},{9,5},{13,9},{6,2},{10,6},{14,10},{7,3},{... | collective-permute-start | bytes 1769480 | tf_op jit(solution)/shard_map/ppermute | solution.py:373
  41.1 6.6 %collective-permute-start.10 = (s32[4,8,128]{2,1,0:T(8,128)S(1)}, s32[4,8,128]{2,1,0:T(8,128)S(1)}, u32[]{:S(2)}, u32[]{:S(2)}) collective-permute-start(s32[4,8,128]{2,1,0:T(8,128)S(1)} %get-tuple-element.31), channel_id=1, source_target_pairs={{12,0},{16,4},{20,8},{24,12},{28,16},{32,20},{36,24},{40,28},{44,3... | collective-permute-start | bytes 49160 | tf_op jit(solution)/shard_map/ppermute | solution.py:341
  42.4 9.8 %collective-permute-start.7 = (s32[4,8,128]{2,1,0:T(8,128)S(1)}, s32[4,8,128]{2,1,0:T(8,128)S(1)}, u32[]{:S(2)}, u32[]{:S(2)}) collective-permute-start(s32[4,8,128]{2,1,0:T(8,128)S(1)} %get-tuple-element.32), channel_id=1, source_target_pairs={{8,0},{12,4},{16,8},{20,12},{24,16},{28,20},{32,24},{36,28},{40,32... | collective-permute-start | bytes 49160 | tf_op jit(solution)/shard_map/ppermute | solution.py:341
  43.7 17.5 %collective-permute-start.4 = (s32[4,8,128]{2,1,0:T(8,128)S(1)}, s32[4,8,128]{2,1,0:T(8,128)S(1)}, u32[]{:S(2)}, u32[]{:S(2)}) collective-permute-start(s32[4,8,128]{2,1,0:T(8,128)S(1)} %get-tuple-element.33), channel_id=1, source_target_pairs={{4,0},{8,4},{12,8},{16,12},{20,16},{24,20},{28,24},{32,28},{36,32}... | collective-permute-start | bytes 49160 | tf_op jit(solution)/shard_map/ppermute | solution.py:341
  45.6 32.7 %collective-permute-start.6 = (f32[1152,128]{1,0:T(8,128)}, f32[1152,128]{1,0:T(8,128)S(1)}, u32[]{:S(2)}, u32[]{:S(2)}) collective-permute-start(f32[1152,128]{1,0:T(8,128)} %get-tuple-element.16), channel_id=1, source_target_pairs={{8,0},{12,4},{9,1},{13,5},{10,2},{14,6},{11,3},{15,7}} | collective-permute-start | bytes 1769480 | tf_op jit(solution)/shard_map/ppermute | solution.py:373
  47.6 0.7 copy-start.13
  47.6 30.6 %collective-permute-start.9 = (f32[1152,128]{1,0:T(8,128)}, f32[1152,128]{1,0:T(8,128)S(1)}, u32[]{:S(2)}, u32[]{:S(2)}) collective-permute-start(f32[1152,128]{1,0:T(8,128)} %get-tuple-element.17), channel_id=1, source_target_pairs={{12,0},{13,1},{14,2},{15,3}} | collective-permute-start | bytes 1769480 | tf_op jit(solution)/shard_map/ppermute | solution.py:373
  52.2 5.1 %copy-start.14 = (s32[4,8,128]{2,1,0:T(8,128)}, s32[4,8,128]{2,1,0:T(8,128)S(1)}, u32[]{:S(2)}) copy-start(s32[4,8,128]{2,1,0:T(8,128)S(1)} %collective-permute-done.7) | copy-start | bytes 49156
  52.2 26.1 %collective-permute-start.11 = (f32[1152,128]{1,0:T(8,128)}, f32[1152,128]{1,0:T(8,128)S(1)}, u32[]{:S(2)}, u32[]{:S(2)}) collective-permute-start(f32[1152,128]{1,0:T(8,128)} %pick.11), channel_id=1, source_target_pairs={{0,12},{4,16},{8,20},{12,24},{16,28},{20,32},{24,36},{28,40},{32,4... | collective-permute-start | bytes 1769480 | tf_op jit(solution)/shard_map/ppermute | solution.py:341
  61.2 3.0 %copy-start.15 = (s32[4,8,128]{2,1,0:T(8,128)}, s32[4,8,128]{2,1,0:T(8,128)S(1)}, u32[]{:S(2)}) copy-start(s32[4,8,128]{2,1,0:T(8,128)S(1)} %collective-permute-done.4) | copy-start | bytes 49156
  61.2 21.6 %collective-permute-start.8 = (f32[1152,128]{1,0:T(8,128)}, f32[1152,128]{1,0:T(8,128)S(1)}, u32[]{:S(2)}, u32[]{:S(2)}) collective-permute-start(f32[1152,128]{1,0:T(8,128)} %pick.10), channel_id=1, source_target_pairs={{0,8},{4,12},{8,16},{12,20},{16,24},{20,28},{24,32},{28,36},{32,40... | collective-permute-start | bytes 1769480 | tf_op jit(solution)/shard_map/ppermute | solution.py:341
  68.1 21.0 %collective-permute-start.5 = (f32[1152,128]{1,0:T(8,128)}, f32[1152,128]{1,0:T(8,128)}, u32[]{:S(2)}, u32[]{:S(2)}) collective-permute-start(f32[1152,128]{1,0:T(8,128)} %pick.9), channel_id=1, source_target_pairs={{0,4},{4,8},{8,12},{12,16},{16,20},{20,24},{24,28},{28,32},{32,36}... | collective-permute-start | bytes 1769480 | tf_op jit(solution)/shard_map/ppermute | solution.py:341
  74.8 16.8 %all-to-all-start.1 = ((f32[4,288,128]{2,1,0:T(8,128)}), f32[4,288,128]{2,1,0:T(8,128)S(1)}, u32[]{:S(2)}, u32[]{:S(2)}) async-start(f32[4,288,128]{2,1,0:T(8,128)} %bitcast.80), calls=%async_computation.1 | async-start | bytes 1179648 | tf_op jit(solution)/shard_map/all_to_all | solution.py:383
  78.3 4.5 %copy-start.4 = (f32[1152,128]{1,0:T(8,128)}, f32[1152,128]{1,0:T(8,128)S(1)}, u32[]{:S(2)}) copy-start(f32[1152,128]{1,0:T(8,128)S(1)} %collective-permute-done.11) | copy-start | bytes 1769476
  82.8 0.9 copy-start.5
  91.6 32.1 %copy-start.1 = (f32[4,288,128]{2,1,0:T(8,128)}, f32[4,288,128]{2,1,0:T(8,128)S(1)}, u32[]{:S(2)}) copy-start(f32[4,288,128]{2,1,0:T(8,128)S(1)} %all-to-all-done.1) | copy-start | bytes 1769476
  116.3 13.6 %all-to-all-start.4 = ((f32[4,288,128]{2,1,0:T(8,128)}), f32[4,288,128]{2,1,0:T(8,128)S(1)}, u32[]{:S(2)}, u32[]{:S(2)}) async-start(f32[4,288,128]{2,1,0:T(8,128)} %bitcast.25), calls=%async_computation.4 | async-start | bytes 1179648 | tf_op jit(solution)/shard_map/all_to_all | solution.py:383
  129.9 0.8 copy-start.2
  152.3 23.2 %collective-permute-start.12 = (f32[1152,128]{1,0:T(8,128)}, f32[1152,128]{1,0:T(8,128)S(1)}, u32[]{:S(2)}, u32[]{:S(2)}) collective-permute-start(f32[1152,128]{1,0:T(8,128)} %get-tuple-element.18), channel_id=1, source_target_pairs={{4,0},{8,4},{12,8},{5,1},{9,5},{13,9},{6,2},{10,6},{14,10},{7,3},{... | collective-permute-start | bytes 1769480 | tf_op jit(solution)/shard_map/ppermute | solution.py:373
  155.2 29.6 %collective-permute-start.14 = (f32[1152,128]{1,0:T(8,128)}, f32[1152,128]{1,0:T(8,128)S(1)}, u32[]{:S(2)}, u32[]{:S(2)}) collective-permute-start(f32[1152,128]{1,0:T(8,128)} %get-tuple-element.19), channel_id=1, source_target_pairs={{8,0},{12,4},{9,1},{13,5},{10,2},{14,6},{11,3},{15,7}} | collective-permute-start | bytes 1769480 | tf_op jit(solution)/shard_map/ppermute | solution.py:373
  168.2 16.6 %collective-permute-start.16 = (f32[1152,128]{1,0:T(8,128)}, f32[1152,128]{1,0:T(8,128)S(1)}, u32[]{:S(2)}, u32[]{:S(2)}) collective-permute-start(f32[1152,128]{1,0:T(8,128)} %get-tuple-element.20), channel_id=1, source_target_pairs={{12,0},{13,1},{14,2},{15,3}} | collective-permute-start | bytes 1769480 | tf_op jit(solution)/shard_map/ppermute | solution.py:373
  168.9 15.9 %collective-permute-start.17 = (f32[1152,128]{1,0:T(8,128)}, f32[1152,128]{1,0:T(8,128)S(1)}, u32[]{:S(2)}, u32[]{:S(2)}) collective-permute-start(f32[1152,128]{1,0:T(8,128)} %pick.15), channel_id=1, source_target_pairs={{0,12},{4,16},{8,20},{12,24},{16,28},{20,32},{24,36},{28,40},{32,4... | collective-permute-start | bytes 1769480 | tf_op jit(solution)/shard_map/ppermute | solution.py:341
  170.2 22.2 %collective-permute-start.15 = (f32[1152,128]{1,0:T(8,128)}, f32[1152,128]{1,0:T(8,128)S(1)}, u32[]{:S(2)}, u32[]{:S(2)}) collective-permute-start(f32[1152,128]{1,0:T(8,128)} %pick.14), channel_id=1, source_target_pairs={{0,8},{4,12},{8,16},{12,20},{16,24},{20,28},{24,32},{28,36},{32,40... | collective-permute-start | bytes 1769480 | tf_op jit(solution)/shard_map/ppermute | solution.py:341
  175.5 27.1 %collective-permute-start.13 = (f32[1152,128]{1,0:T(8,128)}, f32[1152,128]{1,0:T(8,128)}, u32[]{:S(2)}, u32[]{:S(2)}) collective-permute-start(f32[1152,128]{1,0:T(8,128)} %pick.13), channel_id=1, source_target_pairs={{0,4},{4,8},{8,12},{12,16},{16,20},{20,24},{24,28},{28,32},{32,36}... | collective-permute-start | bytes 1769480 | tf_op jit(solution)/shard_map/ppermute | solution.py:341
  181.3 23.7 %all-to-all-start.5 = ((f32[4,288,128]{2,1,0:T(8,128)}), f32[4,288,128]{2,1,0:T(8,128)S(1)}, u32[]{:S(2)}, u32[]{:S(2)}) async-start(f32[4,288,128]{2,1,0:T(8,128)} %bitcast.79), calls=%async_computation.5 | async-start | bytes 1179648 | tf_op jit(solution)/shard_map/all_to_all | solution.py:383
  184.8 7.6 %copy-start.6 = (f32[1152,128]{1,0:T(8,128)}, f32[1152,128]{1,0:T(8,128)S(1)}, u32[]{:S(2)}) copy-start(f32[1152,128]{1,0:T(8,128)S(1)} %collective-permute-done.17) | copy-start | bytes 1769476
  192.4 0.8 copy-start.7
  205.1 31.3 %copy-start = (f32[4,288,128]{2,1,0:T(8,128)}, f32[4,288,128]{2,1,0:T(8,128)S(1)}, u32[]{:S(2)}) copy-start(f32[4,288,128]{2,1,0:T(8,128)S(1)} %all-to-all-done.5) | copy-start | bytes 1769476
  229.0 14.0 %all-to-all-start.8 = ((f32[4,288,128]{2,1,0:T(8,128)}), f32[4,288,128]{2,1,0:T(8,128)S(1)}, u32[]{:S(2)}, u32[]{:S(2)}) async-start(f32[4,288,128]{2,1,0:T(8,128)} %bitcast.35), calls=%async_computation.8 | async-start | bytes 1179648 | tf_op jit(solution)/shard_map/all_to_all | solution.py:383
  243.0 0.8 copy-start.3
  259.3 17.8 %collective-permute-start.18 = (f32[512,128]{1,0:T(8,128)S(1)}, f32[512,128]{1,0:T(8,128)S(1)}, u32[]{:S(2)}, u32[]{:S(2)}) collective-permute-start(f32[512,128]{1,0:T(8,128)S(1)} %get-tuple-element.24), channel_id=1, source_target_pairs={{0,1},{1,2},{2,3},{4,5},{5,6},{6,7},{8,9},{9,10},{10,11},{12,13},{... | collective-permute-start | bytes 786440 | tf_op jit(solution)/shard_map/ppermute | solution.py:341
  261.5 15.6 %collective-permute-start.19 = (f32[512,128]{1,0:T(8,128)S(1)}, f32[512,128]{1,0:T(8,128)S(1)}, u32[]{:S(2)}, u32[]{:S(2)}) collective-permute-start(f32[512,128]{1,0:T(8,128)S(1)} %get-tuple-element.23), channel_id=1, source_target_pairs={{1,0},{2,1},{3,2},{5,4},{6,5},{7,6},{9,8},{10,9},{11,10},{13,12},{... | collective-permute-start | bytes 786440 | tf_op jit(solution)/shard_map/ppermute | solution.py:341
  263.6 13.5 %collective-permute-start.20 = (f32[8,128]{1,0:T(8,128)S(1)}, f32[8,128]{1,0:T(8,128)S(1)}, u32[]{:S(2)}, u32[]{:S(2)}) collective-permute-start(f32[8,128]{1,0:T(8,128)S(1)} %bitcast.101), channel_id=1, source_target_pairs={{0,4},{4,8},{8,12},{12,16},{16,20},{20,24},{24,28},{28,32},{32,36}... | collective-permute-start | bytes 12296 | tf_op jit(solution)/shard_map/ppermute | solution.py:341
  266.9 10.2 %collective-permute-start.21 = (f32[8,128]{1,0:T(8,128)S(1)}, f32[8,128]{1,0:T(8,128)S(1)}, u32[]{:S(2)}, u32[]{:S(2)}) collective-permute-start(f32[8,128]{1,0:T(8,128)S(1)} %bitcast.100), channel_id=1, source_target_pairs={{4,0},{8,4},{12,8},{16,12},{20,16},{24,20},{28,24},{32,28},{36,32}... | collective-permute-start | bytes 12296 | tf_op jit(solution)/shard_map/ppermute | solution.py:341
  277.1 0.6 copy-start.16
  277.1 0.6 copy-start.17
  277.2 0.7 copy-start.8
  277.2 0.8 copy-start.9

commit v2 on v1

--- a/solution.py
+++ b/solution.py
@@ -7,12 +7,14 @@
 from jax.experimental.pallas import tpu as pltpu
 from jax.sharding import PartitionSpec as P
 
+
 LAYERS = 40
 ROWS = 8
 COLS = 512
 CELLS = ROWS * COLS
 SLOTS = 288
 SPAN = 4
+ORDER = (1, 2, 3)
 WIDE = 128
 CHUNKS = COLS // WIDE
 LEVELS = 3 * LAYERS
@@ -20,13 +22,14 @@
 I32 = jnp.int32
 VMEM = pl.BlockSpec(memory_space=pltpu.VMEM)
 SMEM = pl.BlockSpec(memory_space=pltpu.SMEM)
+ANY = pl.BlockSpec(memory_space=pl.ANY)
 
 
 def iota(shape, dim):
     return lax.broadcasted_iota(I32, shape, dim)
 
 
-def kernel_call(body, out_shapes, in_specs, out_specs, operands, flops=1 << 20, grid=None, scratch=(), name=None):
+def kernel_call(body, out_shapes, in_specs, out_specs, operands, flops=1 << 20, grid=None, scratch=(), limit=6):
     extra = {} if grid is None else {"grid": grid}
     return pl.pallas_call(
         body,
@@ -35,21 +38,22 @@
         out_specs=out_specs,
         scratch_shapes=list(scratch),
         cost_estimate=pl.CostEstimate(flops=flops, bytes_accessed=1 << 21, transcendentals=0),
-        name=name,
+        compiler_params=pltpu.CompilerParams(vmem_limit_bytes=limit << 20),
         **extra,
     )(*operands)
 
 
 def slots_body(along_ref, first_ref, second_ref, wanted_ref, own_ref):
     along = along_ref[0]
-    before = (iota((COLS, COLS), 0) < iota((COLS, COLS), 1)).astype(jnp.bfloat16)
+    before = (iota((COLS, COLS), 0) < iota((COLS, COLS), 1)).astype(F32).astype(jnp.bfloat16)
     partner_rows = iota((16, COLS), 0)
-    slot_rows = iota((128, COLS), 0)
+    slot_rows = iota((48, COLS), 0)
     lane_rows = iota((WIDE, COLS), 0)
     lane = iota((1, COLS), 1)
-    total = jnp.zeros((512, WIDE), F32)
+    wanted_ref[...] = jnp.zeros((128, WIDE), I32)
     for which, feet_ref in enumerate((first_ref, second_ref)):
         carry = jnp.zeros((16, 1), F32)
+        total = jnp.zeros((192, WIDE), F32)
         for row in range(ROWS):
             feet = feet_ref[row : row + 1, :]
             global_row = feet >> 14
@@ -64,132 +68,254 @@
             prefix = jnp.dot(ones.astype(jnp.bfloat16), before, preferred_element_type=F32)
             rank = jnp.sum(jnp.where(mask, prefix + carry, 0.0), axis=0, keepdims=True).astype(I32)
             carry = carry + jnp.sum(ones, axis=1, keepdims=True)
-            slot_row = partner * 8 + which * 3 + (rank >> 7)
-            hit = slot_rows == slot_row
-            place = (lane_rows == (rank & 127)).astype(F32).astype(jnp.bfloat16)
+            hit = slot_rows == partner * 3 + (rank >> 7)
+            spot = (lane_rows == (rank & 127)).astype(F32).astype(jnp.bfloat16)
             own = CELLS - (row * COLS + lane)
             values = []
             for value in (local & 63, local >> 6, own & 63, own >> 6):
                 values.append(jnp.where(hit, value.astype(F32), 0.0).astype(jnp.bfloat16))
             total = total + lax.dot_general(
                 jnp.concatenate(values, axis=0),
-                place,
+                spot,
                 (((1,), (1,)), ((), ())),
                 preferred_element_type=F32,
             )
-    whole = total.astype(I32)
-    wanted_ref[...] = whole[0:128] + whole[128:256] * 64
-    own_ref[...] = CELLS - (whole[256:384] + whole[384:512] * 64)
-
-
-def table_body(copies, x_ref, o_ref):
+        whole = total.astype(I32)
+        wanted = whole[0:48] + whole[48:96] * 64
+        own = CELLS - (whole[96:144] + whole[144:192] * 64)
+        for z in range(4):
+            for kind in range(SPAN):
+                partner = z * SPAN + kind
+                wanted_ref[partner * 8 + which * 3 : partner * 8 + which * 3 + 3, :] = wanted[partner * 3 : partner * 3 + 3]
+                place = (which * SPAN + kind) * 16 + z * 4
+                own_ref[place : place + 3, :] = own[partner * 3 : partner * 3 + 3]
+
+
+def table_body(copies, x_ref, *refs):
+    o_ref = refs[-1]
     for row in range(ROWS):
         if copies == 1:
             parts = [x_ref[pl.ds(m * 8 + row, LAYERS, stride=24), :] for m in range(3)]
         else:
             part = x_ref[pl.ds(row, LAYERS, stride=8), :]
+            part = jnp.where(iota((LAYERS, WIDE), 0) == LAYERS - 1, 0.0, part)
             parts = [part, part, part]
         parts.append(jnp.zeros((WIDE - LEVELS, WIDE), F32))
         o_ref[row] = jnp.concatenate(parts, axis=0).T
 
 
-def cells_first(x, copies):
+def cells_first(x, copies, *after):
     rows = x.shape[0]
     return kernel_call(
         functools.partial(table_body, copies),
         jax.ShapeDtypeStruct((ROWS, COLS, WIDE), F32),
-        [pl.BlockSpec((rows, WIDE), lambda j: (0, j))],
+        [pl.BlockSpec((rows, WIDE), lambda j: (0, j))] + [ANY] * len(after),
         pl.BlockSpec((ROWS, WIDE, WIDE), lambda j: (0, j, 0)),
-        (x,),
+        (x, *after),
         grid=(CHUNKS,),
-        name="cells_first",
-    )
-
-
-def pick_rows(which, wanted_ref, table_ref, out_ref):
+    )
+
+
+def copy_rows(source, target, from_row, to_row, index_of):
+    def some(i, _):
+        for u in range(32):
+            s = i * 32 + u
+            index = index_of(s)
+            target[pl.ds(to_row(s, index), 1), :] = source[pl.ds(from_row(s, index), 1), :]
+        return 0
+
+    lax.fori_loop(0, SLOTS // 32, some, 0)
+
+
+def pick_rows(which, wanted_ref, table_ref, out_ref, pitch=SLOTS):
     def per_across(z, _):
-        def some(i, _):
-            for u in range(32):
-                s = i * 32 + u
-                out_ref[pl.ds(z * SLOTS + s, 1), :] = table_ref[pl.ds(wanted_ref[z * 1024 + which * 384 + s], 1), :]
-            return 0
-
-        return lax.fori_loop(0, SLOTS // 32, some, 0)
+        copy_rows(
+            table_ref,
+            out_ref,
+            lambda s, index: index,
+            lambda s, index: z * pitch + s,
+            lambda s: wanted_ref[z * 1024 + which * 384 + s],
+        )
+        return 0
 
     lax.fori_loop(0, 4, per_across, 0)
 
 
-def pick_body(which, wanted_ref, table_ref, out_ref):
-    pick_rows(which, wanted_ref, table_ref, out_ref)
-
-
-def pick_back_body(which, along_ref, w1, w2, w3, table_ref, o1, o2, o3):
-    @pl.when(along_ref[0] < SPAN)
-    def _():
-        for w, o in ((w1, o1), (w2, o2), (w3, o3)):
-            pick_rows(which, w, table_ref, o)
+def pick_body(which, wanted_ref, table_ref, *refs):
+    pick_rows(which, wanted_ref, table_ref, refs[-1])
 
 
 MESSAGE = jax.ShapeDtypeStruct((4 * SLOTS, WIDE), F32)
 
 
-def pick(which, wanted, table):
-    return kernel_call(
-        functools.partial(pick_body, which), MESSAGE, [SMEM, VMEM], VMEM, (wanted, table), flops=1 << 24, name="pick"
-    )
-
-
-def pick_back(which, along, wanted, table):
+def pick(which, wanted, table, *after):
+    return kernel_call(
+        functools.partial(pick_body, which),
+        MESSAGE,
+        [SMEM, VMEM] + [ANY] * len(after),
+        VMEM,
+        (wanted, table, *after),
+        flops=1 << 28,
+    )
+
+
+def pick_back_body(which, along_ref, w1, w2, w3, table, after, o1, o2, o3, wanted, sem):
+    for u, w, o in ((1, w1, o1), (2, w2, o2), (3, w3, o3)):
+
+        @pl.when((along_ref[0] < SPAN) & (along_ref[0] >= u))
+        def _(w=w, o=o):
+            load = pltpu.make_async_copy(w, wanted, sem)
+            load.start()
+            load.wait()
+            pick_rows(which, wanted, table, o)
+
+
+def pick_back(which, along, wanted, table, after):
     return kernel_call(
         functools.partial(pick_back_body, which),
         (MESSAGE,) * 3,
-        [SMEM] * 4 + [VMEM],
+        [SMEM] + [ANY] * 3 + [VMEM, ANY],
         (VMEM,) * 3,
-        (along, *wanted, table),
-        name="pick_back",
-    )
-
-
-def place_body(which, own_ref, x0, x1, x2, x3, weight_ref, out_ref, cells):
-    for kind, x in enumerate((x0, x1, x2, x3)):
-        def per_across(z, _, kind=kind, x=x):
-            def some(i, _):
-                for u in range(32):
-                    s = i * 32 + u
-                    cell = own_ref[(z * SPAN + kind) * 1024 + which * 384 + s]
-                    cells[pl.ds(cell, 1), :] = x[pl.ds(z * SLOTS + s, 1), :]
-                return 0
-
-            return lax.fori_loop(0, SLOTS // 32, some, 0)
-
-        lax.fori_loop(0, 4, per_across, 0)
-    lane = iota((64, WIDE), 1)
-    top = (lane == LAYERS - 1) | (lane == 2 * LAYERS - 1) | (lane == 3 * LAYERS - 1)
+        (along, *wanted, table, after),
+        scratch=[pltpu.SMEM((4096,), I32), pltpu.SemaphoreType.DMA],
+    )
+
+
+def put_class(along_ref, kind, spot, x_ref, backs, out_ref, buffer, sem):
+    def put(source):
+        for z in range(4):
+            start = (2 * z + spot) * SLOTS
+            out_ref[start : start + SLOTS, :] = source[z * SLOTS : (z + 1) * SLOTS, :]
+
+    put(x_ref)
+    for a in range(kind):
+
+        @pl.when(along_ref[0] == a)
+        def _(a=a):
+            load = pltpu.make_async_copy(backs[kind - a - 1], buffer, sem)
+            load.start()
+            load.wait()
+            put(buffer)
+
+
+PAIR = jax.ShapeDtypeStruct((8 * SLOTS, WIDE), F32)
+
+
+def pick_join_body(which, kind, along_ref, wanted_ref, table_ref, x_ref, *refs):
+    out_ref, buffer, sem = refs[-3:]
+    pick_rows(which, wanted_ref, table_ref, out_ref, 2 * SLOTS)
+    put_class(along_ref, kind, 1, x_ref, refs[:kind], out_ref, buffer, sem)
+
+
+def pick_join(which, kind, along, wanted, table, x, backs, *after):
+    return kernel_call(
+        functools.partial(pick_join_body, which, kind),
+        PAIR,
+        [SMEM, SMEM, VMEM, VMEM] + [ANY] * (kind + len(after)),
+        VMEM,
+        (along, wanted, table, x, *backs[:kind], *after),
+        scratch=[pltpu.VMEM((4 * SLOTS, WIDE), F32), pltpu.SemaphoreType.DMA],
+        flops=1 << 28,
+        limit=8,
+    )
+
+
+def join_body(kinds, along_ref, x_ref, y_ref, b1, b2, b3, *refs):
+    out_ref, buffer, sem = refs[-3:]
+    for spot, (kind, ref) in enumerate(zip(kinds, (x_ref, y_ref))):
+        put_class(along_ref, kind, spot, ref, (b1, b2, b3), out_ref, buffer, sem)
+
+
+def join(kinds, along, x, y, backs, *after):
+    return kernel_call(
+        functools.partial(join_body, kinds),
+        PAIR,
+        [SMEM, VMEM, VMEM] + [ANY] * (3 + len(after)),
+        VMEM,
+        (along, x, y, *backs, *after),
+        scratch=[pltpu.VMEM((4 * SLOTS, WIDE), F32), pltpu.SemaphoreType.DMA],
+        flops=1 << 27,
+        limit=8,
+    )
+
+
+def put_rows(own_ref, x, cells, pitch=SLOTS, start=0):
+    def per_across(z, _):
+        copy_rows(
+            x,
+            cells,
+            lambda s, index: z * pitch + start + s,
+            lambda s, index: index,
+            lambda s: own_ref[z * 512 + s],
+        )
+        return 0
+
+    lax.fori_loop(0, 4, per_across, 0)
+
+
+def load_own(which, kinds, own_any, own, sems):
+    loads = [
+        pltpu.make_async_copy(own_any.at[pl.ds((which * SPAN + kind) * 2048, 2048)], own[i], sems.at[i])
+        for i, kind in enumerate(kinds)
+    ]
+    for load in loads:
+        load.start()
+    return loads
+
+
+def place_early_body(which, kinds, own_any, x, after, cells, own0, own1, sems):
+    for i, load in enumerate(load_own(which, kinds, own_any, (own0, own1), sems)):
+        load.wait()
+        put_rows((own0, own1)[i], x, cells, 2 * SLOTS, i * SLOTS)
+
+
+def place_early(which, kinds, own, x, after):
+    return kernel_call(
+        functools.partial(place_early_body, which, kinds),
+        jax.ShapeDtypeStruct((CELLS + 8, WIDE), F32),
+        [ANY, VMEM, ANY],
+        VMEM,
+        (own, x, after),
+        scratch=[*([pltpu.SMEM((2048,), I32)] * 2), pltpu.SemaphoreType.DMA((2,))],
+        flops=1 << 28,
+    )
+
+
+def place_body(which, kinds, own_any, cells_ref, x, weight_ref, out_ref, cells, own0, own1, sems):
+    loads = load_own(which, kinds, own_any, (own0, own1), sems)
+    cells[...] = cells_ref[...]
+    for i, load in enumerate(loads):
+        load.wait()
+        put_rows((own0, own1)[i], x, cells, 2 * SLOTS, i * SLOTS)
 
     def mix(i, _):
-        rows = pl.ds(pl.multiple_of(i * 64, 64), 64)
+        rows = pl.ds(pl.multiple_of(i * 128, 128), 128)
         here = cells[rows, :]
-        upper = jnp.where(top, here, pltpu.roll(here, WIDE - 1, 1))
-        weight = weight_ref[rows, :]
-        out_ref[rows, :] = (1.0 - weight) * here + weight * upper
+        upper = pltpu.roll(here, WIDE - 1, 1)
+        out_ref[rows, :] = here + weight_ref[rows, :] * (upper - here)
         return 0
 
-    lax.fori_loop(0, CELLS // 64, mix, 0)
-
-
-def place(which, own, xs, weight):
-    return kernel_call(
-        functools.partial(place_body, which),
+    lax.fori_loop(0, CELLS // 128, mix, 0)
+
+
+def place(which, kinds, own, cells, x, weight):
+    return kernel_call(
+        functools.partial(place_body, which, kinds),
         jax.ShapeDtypeStruct((CELLS, WIDE), F32),
-        [SMEM] + [VMEM] * 5,
+        [ANY] + [VMEM] * 3,
         VMEM,
-        (own, *xs, weight),
-        scratch=[pltpu.VMEM((CELLS + 8, WIDE), F32)],
-        name="place",
-    )
-
-
-def pivots_body(mix_ref, drag_ref, out_ref):
+        (own, cells, x, weight),
+        scratch=[
+            pltpu.VMEM((CELLS + 8, WIDE), F32),
+            *([pltpu.SMEM((2048,), I32)] * 2),
+            pltpu.SemaphoreType.DMA((2,)),
+        ],
+        flops=1 << 28,
+        limit=12,
+    )
+
+
+def pivots_body(mix_ref, drag_ref, after_ref, out_ref):
     for which in range(2):
         factor = None
         for k in range(LAYERS):
@@ -209,15 +335,14 @@
                 factor = above * inverse
 
 
-def pivots(mix, drag):
+def pivots(mix, drag, after):
     return kernel_call(
         pivots_body,
         jax.ShapeDtypeStruct((2 * LAYERS * 8, COLS), F32),
-        [pl.BlockSpec((2 * 39 * 8, WIDE), lambda j: (0, j)), pl.BlockSpec((8, WIDE), lambda j: (0, j))],
+        [pl.BlockSpec((2 * 39 * 8, WIDE), lambda j: (0, j)), pl.BlockSpec((8, WIDE), lambda j: (0, j)), ANY],
         pl.BlockSpec((2 * LAYERS * 8, WIDE), lambda j: (0, j)),
-        (mix, drag),
+        (mix, drag, after),
         grid=(CHUNKS,),
-        name="pivots",
     )
 
 
@@ -234,7 +359,6 @@
         pl.BlockSpec((LEVELS * 8, WIDE), lambda j: (j, 0)),
         (x,),
         grid=(CHUNKS,),
-        name="layers_first",
     )
 
 
@@ -330,7 +454,7 @@
         (where, moved, up, down, left, right, lateral, mix, inverse, stress),
         grid=(CHUNKS,),
         scratch=[pltpu.VMEM((LEVELS * 8, WIDE), F32)],
-        name="solve",
+        limit=14,
     )
 
 
@@ -350,11 +474,9 @@
         slots_body,
         (jax.ShapeDtypeStruct((128, WIDE), I32),) * 2,
         [SMEM, VMEM, VMEM],
-        (VMEM, VMEM),
+        (VMEM,) * 2,
         (where, first_feet, second_feet),
-        name="slots",
-    )
-    own = own.reshape(-1)
+    )
     wanted = lax.all_to_all(wanted.reshape(4, SPAN, 8, WIDE), "across", split_axis=0, concat_axis=0, tiled=True)
     ahead = [wanted[:, 0]] + [move(wanted[:, t], "along", -t) for t in range(1, SPAN)]
     back = []
@@ -362,42 +484,52 @@
         payload = lax.dynamic_index_in_dim(wanted, jnp.minimum(along + u, SPAN - 1), axis=1, keepdims=False)
         pairs = [(i, i + u) for i in range(SPAN - u)]
         back.append(lax.ppermute(payload, "along", pairs))
+    own = own.reshape(-1)
     ahead = [x.reshape(-1) for x in ahead]
     back = [x.reshape(-1) for x in back]
 
-    def fetch(which, table):
-        sent = {}
-        for t in (3, 2, 1):
-            sent[t] = move(pick(which, ahead[t], table), "along", t)
+    def turn(x):
+        x = x.reshape(4, 2 * SLOTS, WIDE)
+        return lax.all_to_all(x, "across", split_axis=0, concat_axis=0, tiled=True).reshape(-1, WIDE)
+
+    def fetch(which, table, weigh):
+        i, j, k = ORDER
+        pi = pick(which, ahead[i], table, *ahead[1:], *back)
+        pj = pick(which, ahead[j], table, pi)
+        pk = pick(which, ahead[k], table, pj)
+        xi, xj, xk = [move(p, "along", t) for t, p in ((i, pi), (j, pj), (k, pk))]
         behind = [
-            lax.ppermute(x, "along", [(i, i - u) for i in range(u, SPAN)])
-            for u, x in zip((1, 2, 3), pick_back(which, where, back, table))
+            lax.ppermute(x, "along", [(b, b - u) for b in range(u, SPAN)])
+            for u, x in zip((1, 2, 3), pick_back(which, where, back, table, pk))
         ]
-        parts = [pick(which, ahead[0], table)]
-        for t in range(1, SPAN):
-            part = sent[t]
-            for a in range(t):
-                part = jnp.where(along == a, behind[t - a - 1], part)
-            parts.append(part)
-        return [
-            lax.all_to_all(x.reshape(4, SLOTS, WIDE), "across", split_axis=0, concat_axis=0, tiled=True).reshape(-1, WIDE)
-            for x in parts
-        ]
+        weight, done = weigh(pk)
+        joined = pick_join(which, i, where, ahead[0], table, xi, behind, pk, *done)
+        early = turn(joined)
+        cells = place_early(which, (0, i), own, early, joined)
+        late = turn(join((j, k), where, xj, xk, behind, cells))
+        return place(which, (j, k), own, cells, late, weight)
+
+    mix = vertical_mix.reshape(2 * 39 * 8, COLS)
+    inverse = []
+
+    def first_weight(after):
+        inverse.append(pivots(mix, bottom_drag, after))
+        weight = cells_first(first_fraction.reshape(LAYERS * 8, COLS), 3, after)
+        return weight.reshape(CELLS, WIDE), (weight, inverse[0])
+
+    def second_weight(after):
+        weight = cells_first(second_fraction.reshape(LAYERS * 8, COLS), 3, after)
+        return weight.reshape(CELLS, WIDE), (weight,)
 
     table = cells_first(fields.reshape(LEVELS * 8, COLS), 1).reshape(CELLS, WIDE)
-    first_weight = cells_first(first_fraction.reshape(LAYERS * 8, COLS), 3).reshape(CELLS, WIDE)
-    second_weight = cells_first(second_fraction.reshape(LAYERS * 8, COLS), 3).reshape(CELLS, WIDE)
-    mix = vertical_mix.reshape(2 * 39 * 8, COLS)
-    inverse = pivots(mix, bottom_drag)
-
-    middle = place(0, own, fetch(0, table), first_weight)
-    moved = place(1, own, fetch(1, middle), second_weight).reshape(ROWS, COLS, WIDE)
+    middle = fetch(0, table, first_weight)
+    moved = fetch(1, middle, second_weight).reshape(ROWS, COLS, WIDE)
     up = move(moved[ROWS - 1], "across", 1)
     down = move(moved[0], "across", -1)
     left = move(moved[:, COLS - 1], "along", 1)
     right = move(moved[:, 0], "along", -1)
     result = solve(
-        where, layers_first(moved), up, down, left, right, lateral_mix, mix, inverse, surface_stress.reshape(16, COLS)
+        where, layers_first(moved), up, down, left, right, lateral_mix, mix, inverse[0], surface_stress.reshape(16, COLS)
     )
     return result.reshape(LAYERS, 3, ROWS, COLS)
 

time: 287 us -> 230 us (0.80)
  Pallas kernels: 108 us -> 67.3 us
  blocking collectives: 48.7 us -> 31.8 us
  other arithmetic: 5.48 us -> 0.07 us
    pallas_call x19 -> x23, Pallas kernels: 108 us -> 67.3 us  [kernel_call(): pl.pallas_call(body, out_shape=out_shapes, in_specs=in_specs, out_specs=o...]
    all_to_all x4 -> x2, blocking collectives: 48.7 us -> 31.8 us  [turn(): lax.all_to_all(x, 'across', split_axis=0, concat_axis=0, tiled=True)]
    ppermute x6, waiting for transfers between devices: 0.02 us -> 16.4 us  [fetch(): lax.ppermute(x, 'along', [(b, b - u) for b in range(u, SPAN)])]
    ppermute x13, waiting for transfers between devices: 27.7 us -> 19.6 us  [move(): return lax.ppermute(x, axis, pairs)]
    ppermute x13, starting transfers between devices: 32.7 us -> 40.5 us  [move(): return lax.ppermute(x, axis, pairs)]
    all_to_all x4 -> x2, waiting for transfers between devices: 12.9 us -> 6.98 us  [turn(): lax.all_to_all(x, 'across', split_axis=0, concat_axis=0, tiled=True)]
    all_to_all x4 -> x2, starting transfers between devices: 13.9 us -> 8.54 us  [turn(): lax.all_to_all(x, 'across', split_axis=0, concat_axis=0, tiled=True)]
    select_n x2 -> x0, other arithmetic: 4.86 us -> none  [fetch(): part = jnp.where(along == a, behind[t - a - 1], part)]
  transfers between devices with their start and end apart: 27 -> 25, of which waited for: 8 -> 9; matrix products, arithmetic and copies ran while one was open for 2% -> 0% of each run, Pallas kernels for 18% -> 11%
where the time goes in v2:
time: 230 us; the launch traced here: 228 us
  starting transfers between devices  71.5 us (31%)
  Pallas kernels  67.3 us (29%)
  waiting for transfers between devices  47.5 us (21%)
  blocking collectives  31.8 us (14%)
  local copies, waits for them, and re-layouts  9.48 us (4%)
    pallas_call x23, Pallas kernels, kernel_call(): pl.pallas_call(body, out_shape=out_shapes, in_specs=in_specs, out_specs=o...  67.3 us
    ppermute x13, starting transfers between devices, move(): return lax.ppermute(x, axis, pairs)  40.5 us
    all_to_all x2, blocking collectives, turn(): lax.all_to_all(x, 'across', split_axis=0, concat_axis=0, tiled=True)  31.8 us
    ppermute x13, waiting for transfers between devices, move(): return lax.ppermute(x, axis, pairs)  19.6 us
    ppermute x6, waiting for transfers between devices, fetch(): lax.ppermute(x, 'along', [(b, b - u) for b in range(u, SPAN)])  16.4 us
    ppermute x6, starting transfers between devices, fetch(): lax.ppermute(x, 'along', [(b, b - u) for b in range(u, SPAN)])  9.51 us
    unnamed x42, local copies, waits for them, and re-layouts  9.42 us
    all_to_all x2, starting transfers between devices, turn(): lax.all_to_all(x, 'across', split_axis=0, concat_axis=0, tiled=True)  8.54 us
  transfers between devices with their start and end apart: 25, of which 9 were waited for; matrix products, arithmetic and copies ran while one was open for 0% of the time, Pallas kernels for 11%

profile of v2, /device:TPU:1, one launch (start us, length us, event | category | flops | bytes accessed | tf_op | source)
XLA Modules:
  0.0 228.3 jit_solution(14365021270255763413)
XLA Ops:
  1.5 3.5 %shard_map.91 = (s32[128,128]{1,0:T(8,128)}, s32[128,128]{1,0:T(8,128)S(1)}) custom-call(s32[2]{0:T(128)S(1)} %pad_add_fusion.along_ref.place_ref, s32[8,512]{1,0:T(8,128)S(1)} %copy-done.15, s32[8,512]{1,0:T(8,128)S(1)} %copy-done.16), custom_call_target="tpu_custom_call" | custom-call | flops 1048576 | bytes 2097152 | tf_op jit(solution)/shard_map/pallas_call | solution.py:34
  5.0 5.8 %all-to-all-start = ((s32[4,4,8,128]{3,2,1,0:T(8,128)}), s32[4,4,8,128]{3,2,1,0:T(8,128)S(1)}, u32[]{:S(2)}, u32[]{:S(2)}) async-start(s32[4,4,8,128]{3,2,1,0:T(8,128)} %bitcast.3), calls=%async_computation | async-start | bytes 131072 | tf_op jit(solution)/shard_map/all_to_all | solution.py:480
  10.8 4.5 %all-to-all-done = s32[4,4,8,128]{3,2,1,0:T(8,128)S(1)} async-done(((s32[4,4,8,128]{3,2,1,0:T(8,128)}), s32[4,4,8,128]{3,2,1,0:T(8,128)S(1)}, u32[]{:S(2)}, u32[]{:S(2)}) %all-to-all-start) | async-done | bytes 65568 | tf_op jit(solution)/shard_map/all_to_all | solution.py:480
  16.0 3.8 %collective-permute-start.4 = (s32[4,8,128]{2,1,0:T(8,128)S(1)}, s32[4,8,128]{2,1,0:T(8,128)S(1)}, u32[]{:S(2)}, u32[]{:S(2)}) collective-permute-start(s32[4,8,128]{2,1,0:T(8,128)S(1)} %get-tuple-element.26), channel_id=1, source_target_pairs={{0,8},{4,12},{1,9},{5,13},{2,10},{6,14},{3,11},{7,15}} | collective-permute-start | bytes 49160 | tf_op jit(solution)/shard_map/ppermute | solution.py:486
  19.8 2.7 %collective-permute-start.3 = (s32[4,8,128]{2,1,0:T(8,128)S(1)}, s32[4,8,128]{2,1,0:T(8,128)S(1)}, u32[]{:S(2)}, u32[]{:S(2)}) collective-permute-start(s32[4,8,128]{2,1,0:T(8,128)S(1)} %get-tuple-element.27), channel_id=1, source_target_pairs={{0,4},{4,8},{8,12},{1,5},{5,9},{9,13},{2,6},{6,10},{10,14},{3,7},{... | collective-permute-start | bytes 49160 | tf_op jit(solution)/shard_map/ppermute | solution.py:486
  25.1 2.3 %collective-permute-start = (s32[4,8,128]{2,1,0:T(8,128)S(1)}, s32[4,8,128]{2,1,0:T(8,128)S(1)}, u32[]{:S(2)}, u32[]{:S(2)}) collective-permute-start(s32[4,8,128]{2,1,0:T(8,128)S(1)} %get-tuple-element.30), channel_id=1, source_target_pairs={{4,0},{8,4},{12,8},{16,12},{20,16},{24,20},{28,24},{32,28},{36,32}... | collective-permute-start | bytes 49160 | tf_op jit(solution)/shard_map/ppermute | solution.py:465
  27.4 1.5 copy-done.9
  31.1 2.2 shard_map.93.refs_0_
  33.3 2.2 shard_map.94.refs_0_
  35.5 3.4 %collective-permute-start.6 = (f32[1152,128]{1,0:T(8,128)S(1)}, f32[1152,128]{1,0:T(8,128)S(1)}, u32[]{:S(2)}, u32[]{:S(2)}) collective-permute-start(f32[1152,128]{1,0:T(8,128)S(1)} %shard_map.93.refs_0_), channel_id=1, source_target_pairs={{0,4},{4,8},{8,12},{12,16},{16,20},{20,24},{24,28},{28,32},{32,36}... | collective-permute-start | bytes 1769480 | tf_op jit(solution)/shard_map/ppermute | solution.py:465
  39.0 2.2 shard_map.95.after.refs_0_.after_ref.refs_1_
  41.2 2.8 %shard_map.96 = (f32[1152,128]{1,0:T(8,128)S(1)}, f32[1152,128]{1,0:T(8,128)S(1)}, f32[1152,128]{1,0:T(8,128)S(1)}) custom-call(s32[2]{0:T(128)S(1)} %pad_add_fusion.along_ref.place_ref, s32[4096]{0:T(1024)S(1)} %bitcast.80, s32[4096]{0:T(1024)S(1)} %bitcast.76, s32[4096]{0:T(1024)S(1)} %bitcast.72, f32[4096,128]{1,0:T(8,128)S(1)} %bitcast.51, ...), custom_call_target="tpu_custom_call" | custom-call | flops 1048576 | bytes 2097152 | tf_op jit(solution)/shard_map/pallas_call | solution.py:34
  45.7 2.0 collective-permute-start.7
  48.9 1.7 shard_map.98.refs_3_.inverse_ref
  50.6 7.8 %collective-permute-done.7.refs_0_.b1 = f32[1152,128]{1,0:T(8,128)S(1)} collective-permute-done((f32[1152,128]{1,0:T(8,128)S(1)}, f32[1152,128]{1,0:T(8,128)S(1)}, u32[]{:S(2)}, u32[]{:S(2)}) %collective-permute-start.7) | collective-permute-done | bytes 589856 | tf_op jit(solution)/shard_map/ppermute | solution.py:502
  58.4 2.3 shard_map.99.after
  61.8 4.3 %all-to-all-start.1 = ((f32[4,576,128]{2,1,0:T(8,128)}), f32[4,576,128]{2,1,0:T(8,128)}, u32[]{:S(2)}, u32[]{:S(2)}) async-start(f32[4,576,128]{2,1,0:T(8,128)} %bitcast.57), calls=%async_computation.1 | async-start | bytes 2359296 | tf_op jit(solution)/shard_map/all_to_all | solution.py:493
  66.0 2.1 collective-permute-start.9
  68.2 2.1 collective-permute-start.8
  71.5 1.5 collective-permute-start.11
  73.0 3.5 %all-to-all-done.1 = f32[4,576,128]{2,1,0:T(8,128)} async-done(((f32[4,576,128]{2,1,0:T(8,128)}), f32[4,576,128]{2,1,0:T(8,128)}, u32[]{:S(2)}, u32[]{:S(2)}) %all-to-all-start.1) | async-done | bytes 1179680 | tf_op jit(solution)/shard_map/all_to_all | solution.py:493
  77.8 4.9 %shard_map.100.refs_0_.cells_ref = f32[4104,128]{1,0:T(8,128)S(1)} custom-call(s32[16384]{0:T(1024)S(1)} %bitcast.65, f32[2304,128]{1,0:T(8,128)} %bitcast.22.x, f32[2304,128]{1,0:T(8,128)S(1)} %copy-done.3), custom_call_target="tpu_custom_call" | custom-call | flops 268435456 | bytes 2097152 | tf_op jit(solution)/shard_map/pallas_call | solution.py:34
  82.7 9.8 %collective-permute-done.8.x_ref = f32[1152,128]{1,0:T(8,128)} collective-permute-done((f32[1152,128]{1,0:T(8,128)S(1)}, f32[1152,128]{1,0:T(8,128)}, u32[]{:S(2)}, u32[]{:S(2)}) %collective-permute-start.8) | collective-permute-done | bytes 589856 | tf_op jit(solution)/shard_map/ppermute | solution.py:465
  92.5 2.6 %shard_map.101 = f32[2304,128]{1,0:T(8,128)S(1)} custom-call(s32[2]{0:T(128)S(1)} %pad_add_fusion.along_ref.place_ref, f32[1152,128]{1,0:T(8,128)} %collective-permute-done.8.x_ref, f32[1152,128]{1,0:T(8,128)} %collective-permute-done.9.y_ref, f32[1152,128]{1,0:T(8,128)S(1)} %copy-done.8, f32[1152,128]{1,0:T(8,128)} %collective-permute-done.10.b2, ...), custom_call_target="tpu_custom_call" | custom-call | flops 134217728 | bytes 2097152 | tf_op jit(solution)/shard_map/pallas_call | solution.py:34
  95.1 17.4 %all_to_all.25 = f32[4,576,128]{2,1,0:T(8,128)S(1)} all-to-all(f32[4,576,128]{2,1,0:T(8,128)S(1)} %bitcast.62), channel_id=1, replica_groups=mesh['along'=32,'across'=4] {'across'}, dimensions={0} | all-to-all | bytes 2359296 | tf_op jit(solution)/shard_map/all_to_all | solution.py:493
  112.5 6.3 %shard_map.102.table_ref.table = f32[4096,128]{1,0:T(8,128)S(1)} custom-call(s32[16384]{0:T(1024)S(1)} %bitcast.66, f32[4104,128]{1,0:T(8,128)S(1)} %shard_map.100.refs_0_.cells_ref, f32[2304,128]{1,0:T(8,128)S(1)} %bitcast.61, f32[4096,128]{1,0:T(8,128)S(1)} %bitcast.54), custom_call_target="tpu_custom_call" | custom-call | flops 268435456 | bytes 2097152 | tf_op jit(solution)/shard_map/pallas_call | solution.py:34
  118.8 2.3 shard_map.103.refs_0_
  121.0 2.3 shard_map.104.refs_0_
  123.3 6.6 %collective-permute-start.12 = (f32[1152,128]{1,0:T(8,128)S(1)}, f32[1152,128]{1,0:T(8,128)S(1)}, u32[]{:S(2)}, u32[]{:S(2)}) collective-permute-start(f32[1152,128]{1,0:T(8,128)S(1)} %shard_map.103.refs_0_), channel_id=1, source_target_pairs={{0,4},{4,8},{8,12},{12,16},{16,20},{20,24},{24,28},{28,32},{32,36}... | collective-permute-start | bytes 1769480 | tf_op jit(solution)/shard_map/ppermute | solution.py:465
  129.9 2.3 shard_map.105.after.refs_0_.refs_1_
  133.0 2.8 %shard_map.106 = (f32[1152,128]{1,0:T(8,128)S(1)}, f32[1152,128]{1,0:T(8,128)S(1)}, f32[1152,128]{1,0:T(8,128)S(1)}) custom-call(s32[2]{0:T(128)S(1)} %pad_add_fusion.along_ref.place_ref, s32[4096]{0:T(1024)S(1)} %bitcast.82, s32[4096]{0:T(1024)S(1)} %bitcast.78, s32[4096]{0:T(1024)S(1)} %bitcast.74, f32[4096,128]{1,0:T(8,128)S(1)} %shard_map.102.table_ref.table, ...), custom_call_target="tpu_custom_call" | custom-call | flops 1048576 | bytes 2097152 | tf_op jit(solution)/shard_map/pallas_call | solution.py:34
  137.5 1.9 collective-permute-start.13
  140.6 8.6 %collective-permute-done.13.refs_0_.b1 = f32[1152,128]{1,0:T(8,128)S(1)} collective-permute-done((f32[1152,128]{1,0:T(8,128)S(1)}, f32[1152,128]{1,0:T(8,128)S(1)}, u32[]{:S(2)}, u32[]{:S(2)}) %collective-permute-start.13) | collective-permute-done | bytes 589856 | tf_op jit(solution)/shard_map/ppermute | solution.py:502
  149.2 3.3 %shard_map.108.after = f32[2304,128]{1,0:T(8,128)} custom-call(s32[2]{0:T(128)S(1)} %pad_add_fusion.along_ref.place_ref, s32[4096]{0:T(1024)S(1)} %get-tuple-element.31.wanted_ref, f32[4096,128]{1,0:T(8,128)S(1)} %shard_map.102.table_ref.table, f32[1152,128]{1,0:T(8,128)S(1)} %collective-permute-done.12.x_ref, ...), custom_call_target="tpu_custom_call" | custom-call | flops 268435456 | bytes 2097152 | tf_op jit(solution)/shard_map/pallas_call | solution.py:34
  152.6 4.3 %all-to-all-start.3 = ((f32[4,576,128]{2,1,0:T(8,128)}), f32[4,576,128]{2,1,0:T(8,128)}, u32[]{:S(2)}, u32[]{:S(2)}) async-start(f32[4,576,128]{2,1,0:T(8,128)} %bitcast.27), calls=%async_computation.3 | async-start | bytes 2359296 | tf_op jit(solution)/shard_map/all_to_all | solution.py:493
  156.8 2.1 collective-permute-start.15
  159.0 2.1 collective-permute-start.14
  163.9 3.5 %all-to-all-done.3 = f32[4,576,128]{2,1,0:T(8,128)} async-done(((f32[4,576,128]{2,1,0:T(8,128)}), f32[4,576,128]{2,1,0:T(8,128)}, u32[]{:S(2)}, u32[]{:S(2)}) %all-to-all-start.3) | async-done | bytes 1179680 | tf_op jit(solution)/shard_map/all_to_all | solution.py:493
  167.3 4.8 %shard_map.109.refs_0_.cells_ref = f32[4104,128]{1,0:T(8,128)S(1)} custom-call(s32[16384]{0:T(1024)S(1)} %bitcast.67, f32[2304,128]{1,0:T(8,128)} %bitcast.28.x, f32[2304,128]{1,0:T(8,128)} %shard_map.108.after), custom_call_target="tpu_custom_call" | custom-call | flops 268435456 | bytes 2097152 | tf_op jit(solution)/shard_map/pallas_call | solution.py:34
  172.2 7.5 %collective-permute-done.14.x_ref = f32[1152,128]{1,0:T(8,128)} collective-permute-done((f32[1152,128]{1,0:T(8,128)}, f32[1152,128]{1,0:T(8,128)}, u32[]{:S(2)}, u32[]{:S(2)}) %collective-permute-start.14) | collective-permute-done | bytes 589856 | tf_op jit(solution)/shard_map/ppermute | solution.py:465
  179.7 2.6 %shard_map.110 = f32[2304,128]{1,0:T(8,128)S(1)} custom-call(s32[2]{0:T(128)S(1)} %pad_add_fusion.along_ref.place_ref, f32[1152,128]{1,0:T(8,128)} %collective-permute-done.14.x_ref, f32[1152,128]{1,0:T(8,128)} %collective-permute-done.15.y_ref, f32[1152,128]{1,0:T(8,128)S(1)} %collective-permute-done.13.refs_0_.b1, f32[1152,128]{1,0:T(8,128)} %collective-permute-done.16.b2, ...), custom_call_target="tpu_custom_call" | custom-call | flops 134217728 | bytes 2097152 | tf_op jit(solution)/shard_map/pallas_call | solution.py:34
  182.3 14.4 %all_to_all.26 = f32[4,576,128]{2,1,0:T(8,128)S(1)} all-to-all(f32[4,576,128]{2,1,0:T(8,128)S(1)} %bitcast.63), channel_id=1, replica_groups=mesh['along'=32,'across'=4] {'across'}, dimensions={0} | all-to-all | bytes 2359296 | tf_op jit(solution)/shard_map/all_to_all | solution.py:493
  196.7 6.3 %shard_map.111 = f32[4096,128]{1,0:T(8,128)S(1)} custom-call(s32[16384]{0:T(1024)S(1)} %bitcast.68, f32[4104,128]{1,0:T(8,128)S(1)} %shard_map.109.refs_0_.cells_ref, f32[2304,128]{1,0:T(8,128)S(1)} %bitcast.60, f32[4096,128]{1,0:T(8,128)S(1)} %bitcast.53), custom_call_target="tpu_custom_call" | custom-call | flops 268435456 | bytes 2097152 | tf_op jit(solution)/shard_map/pallas_call | solution.py:34
  204.4 4.0 %collective-permute-start.18 = (f32[512,128]{1,0:T(8,128)S(1)}, f32[512,128]{1,0:T(8,128)S(1)}, u32[]{:S(2)}, u32[]{:S(2)}) collective-permute-start(f32[512,128]{1,0:T(8,128)S(1)} %get-tuple-element.24), channel_id=1, source_target_pairs={{0,1},{1,2},{2,3},{4,5},{5,6},{6,7},{8,9},{9,10},{10,11},{12,13},{... | collective-permute-start | bytes 786440 | tf_op jit(solution)/shard_map/ppermute | solution.py:465
  208.4 9.3 %collective-permute-start.20 = (f32[8,128]{1,0:T(8,128)S(1)}, f32[8,128]{1,0:T(8,128)S(1)}, u32[]{:S(2)}, u32[]{:S(2)}) collective-permute-start(f32[8,128]{1,0:T(8,128)S(1)} %bitcast.97), channel_id=1, source_target_pairs={{0,4},{4,8},{8,12},{12,16},{16,20},{20,24},{24,28},{28,32},{32,36}... | collective-permute-start | bytes 12296 | tf_op jit(solution)/shard_map/ppermute | solution.py:465
  217.8 2.5 %collective-permute-start.21 = (f32[8,128]{1,0:T(8,128)S(1)}, f32[8,128]{1,0:T(8,128)S(1)}, u32[]{:S(2)}, u32[]{:S(2)}) collective-permute-start(f32[8,128]{1,0:T(8,128)S(1)} %bitcast.96), channel_id=1, source_target_pairs={{4,0},{8,4},{12,8},{16,12},{20,16},{24,20},{28,24},{32,28},{36,32}... | collective-permute-start | bytes 12296 | tf_op jit(solution)/shard_map/ppermute | solution.py:465
  221.3 1.5 collective-permute-done.21.right_ref
  222.9 5.4 %shard_map.113 = f32[960,512]{1,0:T(8,128)} custom-call(s32[2]{0:T(128)S(1)} %pad_add_fusion.along_ref.place_ref, f32[3840,128]{1,0:T(8,128)S(1)} %shard_map.112.moved_ref, f32[512,128]{1,0:T(8,128)S(1)} %collective-permute-done.18.up_ref, f32[512,128]{1,0:T(8,128)S(1)} %collective-permute-done.19.down_ref, f32[8,128]{1,0:T(8,128)S(1)} %collective-permute-done.20.left_ref, ...), custom_call_target="tpu_custom_call" | custom-call | flops 1048576 | bytes 2097152 | tf_op jit(solution)/shard_map/pallas_call | solution.py:34
  (73 shorter events, 22.0 us)
Async XLA Ops:
  0.1 0.7 copy-start.15
  0.8 0.7 copy-start.16
  5.0 10.3 %all-to-all-start = ((s32[4,4,8,128]{3,2,1,0:T(8,128)}), s32[4,4,8,128]{3,2,1,0:T(8,128)S(1)}, u32[]{:S(2)}, u32[]{:S(2)}) async-start(s32[4,4,8,128]{3,2,1,0:T(8,128)} %bitcast.3), calls=%async_computation | async-start | bytes 131072 | tf_op jit(solution)/shard_map/all_to_all | solution.py:480
  15.3 9.8 %collective-permute-start.5 = (s32[4,8,128]{2,1,0:T(8,128)S(1)}, s32[4,8,128]{2,1,0:T(8,128)S(1)}, u32[]{:S(2)}, u32[]{:S(2)}) collective-permute-start(s32[4,8,128]{2,1,0:T(8,128)S(1)} %get-tuple-element.25), channel_id=1, source_target_pairs={{0,12},{1,13},{2,14},{3,15}} | collective-permute-start | bytes 49160 | tf_op jit(solution)/shard_map/ppermute | solution.py:486
  16.0 14.3 %collective-permute-start.4 = (s32[4,8,128]{2,1,0:T(8,128)S(1)}, s32[4,8,128]{2,1,0:T(8,128)S(1)}, u32[]{:S(2)}, u32[]{:S(2)}) collective-permute-start(s32[4,8,128]{2,1,0:T(8,128)S(1)} %get-tuple-element.26), channel_id=1, source_target_pairs={{0,8},{4,12},{1,9},{5,13},{2,10},{6,14},{3,11},{7,15}} | collective-permute-start | bytes 49160 | tf_op jit(solution)/shard_map/ppermute | solution.py:486
  19.8 10.4 %collective-permute-start.3 = (s32[4,8,128]{2,1,0:T(8,128)S(1)}, s32[4,8,128]{2,1,0:T(8,128)S(1)}, u32[]{:S(2)}, u32[]{:S(2)}) collective-permute-start(s32[4,8,128]{2,1,0:T(8,128)S(1)} %get-tuple-element.27), channel_id=1, source_target_pairs={{0,4},{4,8},{8,12},{1,5},{5,9},{9,13},{2,6},{6,10},{10,14},{3,7},{... | collective-permute-start | bytes 49160 | tf_op jit(solution)/shard_map/ppermute | solution.py:486
  22.5 7.8 %collective-permute-start.2 = (s32[4,8,128]{2,1,0:T(8,128)S(1)}, s32[4,8,128]{2,1,0:T(8,128)S(1)}, u32[]{:S(2)}, u32[]{:S(2)}) collective-permute-start(s32[4,8,128]{2,1,0:T(8,128)S(1)} %get-tuple-element.28), channel_id=1, source_target_pairs={{12,0},{16,4},{20,8},{24,12},{28,16},{32,20},{36,24},{40,28},{44,3... | collective-permute-start | bytes 49160 | tf_op jit(solution)/shard_map/ppermute | solution.py:465
  23.8 6.5 %collective-permute-start.1 = (s32[4,8,128]{2,1,0:T(8,128)S(1)}, s32[4,8,128]{2,1,0:T(8,128)S(1)}, u32[]{:S(2)}, u32[]{:S(2)}) collective-permute-start(s32[4,8,128]{2,1,0:T(8,128)S(1)} %get-tuple-element.29), channel_id=1, source_target_pairs={{8,0},{12,4},{16,8},{20,12},{24,16},{28,20},{32,24},{36,28},{40,32... | collective-permute-start | bytes 49160 | tf_op jit(solution)/shard_map/ppermute | solution.py:465
  25.1 6.0 %collective-permute-start = (s32[4,8,128]{2,1,0:T(8,128)S(1)}, s32[4,8,128]{2,1,0:T(8,128)S(1)}, u32[]{:S(2)}, u32[]{:S(2)}) collective-permute-start(s32[4,8,128]{2,1,0:T(8,128)S(1)} %get-tuple-element.30), channel_id=1, source_target_pairs={{4,0},{8,4},{12,8},{16,12},{20,16},{24,20},{28,24},{32,28},{36,32}... | collective-permute-start | bytes 49160 | tf_op jit(solution)/shard_map/ppermute | solution.py:465
  27.4 1.5 copy-start.9
  35.5 15.1 %collective-permute-start.6 = (f32[1152,128]{1,0:T(8,128)S(1)}, f32[1152,128]{1,0:T(8,128)S(1)}, u32[]{:S(2)}, u32[]{:S(2)}) collective-permute-start(f32[1152,128]{1,0:T(8,128)S(1)} %shard_map.93.refs_0_), channel_id=1, source_target_pairs={{0,4},{4,8},{8,12},{12,16},{16,20},{20,24},{24,28},{28,32},{32,36}... | collective-permute-start | bytes 1769480 | tf_op jit(solution)/shard_map/ppermute | solution.py:465
  41.2 6.5 %copy-start.10 = (f32[40,8,512]{2,1,0:T(8,128)S(1)}, f32[40,8,512]{2,1,0:T(8,128)}, u32[]{:S(2)}) copy-start(f32[40,8,512]{2,1,0:T(8,128)} %param.11) | copy-start | bytes 1966084
  44.0 0.8 copy-start.18
  44.8 0.8 copy-start.20
  45.6 3.2 %copy-start.4 = (f32[2,39,8,512]{3,2,1,0:T(8,128)S(1)}, f32[2,39,8,512]{3,2,1,0:T(8,128)}, u32[]{:S(2)}) copy-start(f32[2,39,8,512]{3,2,1,0:T(8,128)} %param.15) | copy-start | bytes 3833860
  45.6 3.2 %copy-start.13 = (f32[8,512]{1,0:T(8,128)S(1)}, f32[8,512]{1,0:T(8,128)}, u32[]{:S(2)}) copy-start(f32[8,512]{1,0:T(8,128)} %drag_ref.1) | copy-start | bytes 49156
  45.7 12.8 %collective-permute-start.7 = (f32[1152,128]{1,0:T(8,128)S(1)}, f32[1152,128]{1,0:T(8,128)S(1)}, u32[]{:S(2)}, u32[]{:S(2)}) collective-permute-start(f32[1152,128]{1,0:T(8,128)S(1)} %get-tuple-element.15), channel_id=1, source_target_pairs={{4,0},{8,4},{12,8},{5,1},{9,5},{13,9},{6,2},{10,6},{14,10},{7,3},{... | collective-permute-start | bytes 1769480 | tf_op jit(solution)/shard_map/ppermute | solution.py:502
  50.6 10.1 %copy-start = (f32[640,512]{1,0:T(8,128)}, f32[640,512]{1,0:T(8,128)S(1)}, u32[]{:S(2)}) copy-start(f32[640,512]{1,0:T(8,128)S(1)} %shard_map.98.refs_3_.inverse_ref) | copy-start | bytes 3932164
  58.4 2.3 %copy-start.7 = (f32[1152,128]{1,0:T(8,128)}, f32[1152,128]{1,0:T(8,128)S(1)}, u32[]{:S(2)}) copy-start(f32[1152,128]{1,0:T(8,128)S(1)} %collective-permute-done.7.refs_0_.b1) | copy-start | bytes 1769476
  60.7 1.0 copy-start.2
  61.8 14.8 %all-to-all-start.1 = ((f32[4,576,128]{2,1,0:T(8,128)}), f32[4,576,128]{2,1,0:T(8,128)}, u32[]{:S(2)}, u32[]{:S(2)}) async-start(f32[4,576,128]{2,1,0:T(8,128)} %bitcast.57), calls=%async_computation.1 | async-start | bytes 2359296 | tf_op jit(solution)/shard_map/all_to_all | solution.py:493
  66.0 16.6 %collective-permute-start.9 = (f32[1152,128]{1,0:T(8,128)S(1)}, f32[1152,128]{1,0:T(8,128)}, u32[]{:S(2)}, u32[]{:S(2)}) collective-permute-start(f32[1152,128]{1,0:T(8,128)S(1)} %shard_map.95.after.refs_0_.after_ref.refs_1_), channel_id=1, source_target_pairs={{0,12},{4,16},{8,20},{12,24},{16,28},{20,32},{24,36},{28,40},{32,4... | collective-permute-start | bytes 1769480 | tf_op jit(solution)/shard_map/ppermute | solution.py:465
  68.2 24.3 %collective-permute-start.8 = (f32[1152,128]{1,0:T(8,128)S(1)}, f32[1152,128]{1,0:T(8,128)}, u32[]{:S(2)}, u32[]{:S(2)}) collective-permute-start(f32[1152,128]{1,0:T(8,128)S(1)} %shard_map.94.refs_0_), channel_id=1, source_target_pairs={{0,8},{4,12},{8,16},{12,20},{16,24},{20,28},{24,32},{28,36},{32,40... | collective-permute-start | bytes 1769480 | tf_op jit(solution)/shard_map/ppermute | solution.py:465
  70.3 22.2 %collective-permute-start.10 = (f32[1152,128]{1,0:T(8,128)}, f32[1152,128]{1,0:T(8,128)}, u32[]{:S(2)}, u32[]{:S(2)}) collective-permute-start(f32[1152,128]{1,0:T(8,128)} %copy-done.20), channel_id=1, source_target_pairs={{8,0},{12,4},{9,1},{13,5},{10,2},{14,6},{11,3},{15,7}} | collective-permute-start | bytes 1769480 | tf_op jit(solution)/shard_map/ppermute | solution.py:502
  71.5 20.9 %collective-permute-start.11 = (f32[1152,128]{1,0:T(8,128)}, f32[1152,128]{1,0:T(8,128)}, u32[]{:S(2)}, u32[]{:S(2)}) collective-permute-start(f32[1152,128]{1,0:T(8,128)} %copy-done.18), channel_id=1, source_target_pairs={{12,0},{13,1},{14,2},{15,3}} | collective-permute-start | bytes 1769480 | tf_op jit(solution)/shard_map/ppermute | solution.py:502
  76.5 1.3 copy-start.3
  77.8 14.7 %copy-start.8 = (f32[1152,128]{1,0:T(8,128)S(1)}, f32[1152,128]{1,0:T(8,128)}, u32[]{:S(2)}) copy-start(f32[1152,128]{1,0:T(8,128)} %copy-done.7) | copy-start | bytes 1769476
  123.3 17.3 %collective-permute-start.12 = (f32[1152,128]{1,0:T(8,128)S(1)}, f32[1152,128]{1,0:T(8,128)S(1)}, u32[]{:S(2)}, u32[]{:S(2)}) collective-permute-start(f32[1152,128]{1,0:T(8,128)S(1)} %shard_map.103.refs_0_), channel_id=1, source_target_pairs={{0,4},{4,8},{8,12},{12,16},{16,20},{20,24},{24,28},{28,32},{32,36}... | collective-permute-start | bytes 1769480 | tf_op jit(solution)/shard_map/ppermute | solution.py:465
  132.2 0.8 copy-start.6
  133.0 6.4 %copy-start.11 = (f32[40,8,512]{2,1,0:T(8,128)S(1)}, f32[40,8,512]{2,1,0:T(8,128)}, u32[]{:S(2)}) copy-start(f32[40,8,512]{2,1,0:T(8,128)} %param.13) | copy-start | bytes 1966084
  135.8 0.8 copy-start.17
  136.7 0.8 copy-start.19
  137.5 11.7 %collective-permute-start.13 = (f32[1152,128]{1,0:T(8,128)S(1)}, f32[1152,128]{1,0:T(8,128)S(1)}, u32[]{:S(2)}, u32[]{:S(2)}) collective-permute-start(f32[1152,128]{1,0:T(8,128)S(1)} %get-tuple-element.18), channel_id=1, source_target_pairs={{4,0},{8,4},{12,8},{5,1},{9,5},{13,9},{6,2},{10,6},{14,10},{7,3},{... | collective-permute-start | bytes 1769480 | tf_op jit(solution)/shard_map/ppermute | solution.py:502
  152.6 14.8 %all-to-all-start.3 = ((f32[4,576,128]{2,1,0:T(8,128)}), f32[4,576,128]{2,1,0:T(8,128)}, u32[]{:S(2)}, u32[]{:S(2)}) async-start(f32[4,576,128]{2,1,0:T(8,128)} %bitcast.27), calls=%async_computation.3 | async-start | bytes 2359296 | tf_op jit(solution)/shard_map/all_to_all | solution.py:493
  156.8 15.3 %collective-permute-start.15 = (f32[1152,128]{1,0:T(8,128)S(1)}, f32[1152,128]{1,0:T(8,128)}, u32[]{:S(2)}, u32[]{:S(2)}) collective-permute-start(f32[1152,128]{1,0:T(8,128)S(1)} %shard_map.105.after.refs_0_.refs_1_), channel_id=1, source_target_pairs={{0,12},{4,16},{8,20},{12,24},{16,28},{20,32},{24,36},{28,40},{32,4... | collective-permute-start | bytes 1769480 | tf_op jit(solution)/shard_map/ppermute | solution.py:465
  159.0 20.7 %collective-permute-start.14 = (f32[1152,128]{1,0:T(8,128)}, f32[1152,128]{1,0:T(8,128)}, u32[]{:S(2)}, u32[]{:S(2)}) collective-permute-start(f32[1152,128]{1,0:T(8,128)} %copy-done.6), channel_id=1, source_target_pairs={{0,8},{4,12},{8,16},{12,20},{16,24},{20,28},{24,32},{28,36},{32,40... | collective-permute-start | bytes 1769480 | tf_op jit(solution)/shard_map/ppermute | solution.py:465
  161.1 18.6 %collective-permute-start.16 = (f32[1152,128]{1,0:T(8,128)}, f32[1152,128]{1,0:T(8,128)}, u32[]{:S(2)}, u32[]{:S(2)}) collective-permute-start(f32[1152,128]{1,0:T(8,128)} %copy-done.19), channel_id=1, source_target_pairs={{8,0},{12,4},{9,1},{13,5},{10,2},{14,6},{11,3},{15,7}} | collective-permute-start | bytes 1769480 | tf_op jit(solution)/shard_map/ppermute | solution.py:502
  162.4 17.3 %collective-permute-start.17 = (f32[1152,128]{1,0:T(8,128)}, f32[1152,128]{1,0:T(8,128)}, u32[]{:S(2)}, u32[]{:S(2)}) collective-permute-start(f32[1152,128]{1,0:T(8,128)} %copy-done.17), channel_id=1, source_target_pairs={{12,0},{13,1},{14,2},{15,3}} | collective-permute-start | bytes 1769480 | tf_op jit(solution)/shard_map/ppermute | solution.py:502
  203.1 19.8 %collective-permute-start.19 = (f32[512,128]{1,0:T(8,128)S(1)}, f32[512,128]{1,0:T(8,128)S(1)}, u32[]{:S(2)}, u32[]{:S(2)}) collective-permute-start(f32[512,128]{1,0:T(8,128)S(1)} %get-tuple-element.23), channel_id=1, source_target_pairs={{1,0},{2,1},{3,2},{5,4},{6,5},{7,6},{9,8},{10,9},{11,10},{13,12},{... | collective-permute-start | bytes 786440 | tf_op jit(solution)/shard_map/ppermute | solution.py:465
  204.4 18.5 %collective-permute-start.18 = (f32[512,128]{1,0:T(8,128)S(1)}, f32[512,128]{1,0:T(8,128)S(1)}, u32[]{:S(2)}, u32[]{:S(2)}) collective-permute-start(f32[512,128]{1,0:T(8,128)S(1)} %get-tuple-element.24), channel_id=1, source_target_pairs={{0,1},{1,2},{2,3},{4,5},{5,6},{6,7},{8,9},{9,10},{10,11},{12,13},{... | collective-permute-start | bytes 786440 | tf_op jit(solution)/shard_map/ppermute | solution.py:465
  208.4 12.9 %collective-permute-start.20 = (f32[8,128]{1,0:T(8,128)S(1)}, f32[8,128]{1,0:T(8,128)S(1)}, u32[]{:S(2)}, u32[]{:S(2)}) collective-permute-start(f32[8,128]{1,0:T(8,128)S(1)} %bitcast.97), channel_id=1, source_target_pairs={{0,4},{4,8},{8,12},{12,16},{16,20},{20,24},{24,28},{28,32},{32,36}... | collective-permute-start | bytes 12296 | tf_op jit(solution)/shard_map/ppermute | solution.py:465
  217.7 5.1 %copy-start.1 = (f32[640,512]{1,0:T(8,128)S(1)}, f32[640,512]{1,0:T(8,128)}, u32[]{:S(2)}) copy-start(f32[640,512]{1,0:T(8,128)} %copy-done) | copy-start | bytes 3932164
  217.8 5.1 %copy-start.5 = (f32[2,39,8,512]{3,2,1,0:T(8,128)S(1)}, f32[2,39,8,512]{3,2,1,0:T(8,128)}, u32[]{:S(2)}) copy-start(f32[2,39,8,512]{3,2,1,0:T(8,128)} %param.15) | copy-start | bytes 3833860
  217.8 5.1 %copy-start.12 = (f32[2,8,512]{2,1,0:T(8,128)S(1)}, f32[2,8,512]{2,1,0:T(8,128)}, u32[]{:S(2)}) copy-start(f32[2,8,512]{2,1,0:T(8,128)} %param.17) | copy-start | bytes 98308
  217.8 5.1 %copy-start.14 = (f32[8,512]{1,0:T(8,128)S(1)}, f32[8,512]{1,0:T(8,128)}, u32[]{:S(2)}) copy-start(f32[8,512]{1,0:T(8,128)} %lateral_ref.1) | copy-start | bytes 49156
  217.8 5.1 %collective-permute-start.21 = (f32[8,128]{1,0:T(8,128)S(1)}, f32[8,128]{1,0:T(8,128)S(1)}, u32[]{:S(2)}, u32[]{:S(2)}) collective-permute-start(f32[8,128]{1,0:T(8,128)S(1)} %bitcast.96), channel_id=1, source_target_pairs={{4,0},{8,4},{12,8},{16,12},{20,16},{24,20},{28,24},{32,28},{36,32}... | collective-permute-start | bytes 12296 | tf_op jit(solution)/shard_map/ppermute | solution.py:465

commit v3 on v2

--- a/solution.py
+++ b/solution.py
@@ -14,7 +14,6 @@
 CELLS = ROWS * COLS
 SLOTS = 288
 SPAN = 4
-ORDER = (1, 2, 3)
 WIDE = 128
 CHUNKS = COLS // WIDE
 LEVELS = 3 * LAYERS
@@ -127,47 +126,52 @@
     lax.fori_loop(0, SLOTS // 32, some, 0)
 
 
-def pick_rows(which, wanted_ref, table_ref, out_ref, pitch=SLOTS):
-    def per_across(z, _):
+def pick_rows(which, place_ref, wanted_ref, table_ref, out_ref):
+    def per_step(step, _):
+        base = ((place_ref[1] + step) & 3) * 1024 + which * 384
         copy_rows(
             table_ref,
             out_ref,
             lambda s, index: index,
-            lambda s, index: z * pitch + s,
-            lambda s: wanted_ref[z * 1024 + which * 384 + s],
+            lambda s, index: step * SLOTS + s,
+            lambda s: wanted_ref[base + s],
         )
         return 0
 
-    lax.fori_loop(0, 4, per_across, 0)
-
-
-def pick_body(which, wanted_ref, table_ref, *refs):
-    pick_rows(which, wanted_ref, table_ref, refs[-1])
+    lax.fori_loop(0, 4, per_step, 0)
+
+
+def pick_body(which, place_ref, wanted_ref, table_ref, *refs):
+    pick_rows(which, place_ref, wanted_ref, table_ref, refs[-1])
 
 
 MESSAGE = jax.ShapeDtypeStruct((4 * SLOTS, WIDE), F32)
 
 
-def pick(which, wanted, table, *after):
+def pick(which, place, wanted, table, *after):
     return kernel_call(
         functools.partial(pick_body, which),
         MESSAGE,
-        [SMEM, VMEM] + [ANY] * len(after),
+        [SMEM, SMEM, VMEM] + [ANY] * len(after),
         VMEM,
-        (wanted, table, *after),
+        (place, wanted, table, *after),
         flops=1 << 28,
     )
 
 
-def pick_back_body(which, along_ref, w1, w2, w3, table, after, o1, o2, o3, wanted, sem):
-    for u, w, o in ((1, w1, o1), (2, w2, o2), (3, w3, o3)):
-
-        @pl.when((along_ref[0] < SPAN) & (along_ref[0] >= u))
-        def _(w=w, o=o):
-            load = pltpu.make_async_copy(w, wanted, sem)
-            load.start()
-            load.wait()
-            pick_rows(which, wanted, table, o)
+def pick_back_body(which, along_ref, w1, w2, w3, table, after, o1, o2, o3, s1, s2, s3, sems):
+    steps = ((1, w1, o1, s1), (2, w2, o2, s2), (3, w3, o3, s3))
+    for act in ("start", "finish"):
+        for u, source, out, wanted in steps:
+
+            @pl.when((along_ref[0] < SPAN) & (along_ref[0] >= u))
+            def _(u=u, source=source, out=out, wanted=wanted):
+                load = pltpu.make_async_copy(source, wanted, sems.at[u - 1])
+                if act == "start":
+                    load.start()
+                else:
+                    load.wait()
+                    pick_rows(which, along_ref, wanted, table, out)
 
 
 def pick_back(which, along, wanted, table, after):
@@ -177,17 +181,20 @@
         [SMEM] + [ANY] * 3 + [VMEM, ANY],
         (VMEM,) * 3,
         (along, *wanted, table, after),
-        scratch=[pltpu.SMEM((4096,), I32), pltpu.SemaphoreType.DMA],
-    )
-
-
-def put_class(along_ref, kind, spot, x_ref, backs, out_ref, buffer, sem):
+        scratch=[*([pltpu.SMEM((4096,), I32)] * 3), pltpu.SemaphoreType.DMA((3,))],
+    )
+
+
+def put_class(along_ref, kind, spot, x_ref, backs, outs, buffer, sem, relayed=None):
     def put(source):
-        for z in range(4):
-            start = (2 * z + spot) * SLOTS
-            out_ref[start : start + SLOTS, :] = source[z * SLOTS : (z + 1) * SLOTS, :]
-
-    put(x_ref)
+        for step, out in enumerate(outs):
+            out[spot * SLOTS : (spot + 1) * SLOTS, :] = source[step * SLOTS : (step + 1) * SLOTS, :]
+
+    if relayed is None:
+        put(x_ref)
+    else:
+        pl.when(along_ref[0] & 1 == 1)(lambda: put(x_ref))
+        pl.when(along_ref[0] & 1 == 0)(lambda: put(relayed))
     for a in range(kind):
 
         @pl.when(along_ref[0] == a)
@@ -198,13 +205,17 @@
             put(buffer)
 
 
-PAIR = jax.ShapeDtypeStruct((8 * SLOTS, WIDE), F32)
+PAIR = (jax.ShapeDtypeStruct((2 * SLOTS, WIDE), F32),) * 4
 
 
 def pick_join_body(which, kind, along_ref, wanted_ref, table_ref, x_ref, *refs):
-    out_ref, buffer, sem = refs[-3:]
-    pick_rows(which, wanted_ref, table_ref, out_ref, 2 * SLOTS)
-    put_class(along_ref, kind, 1, x_ref, refs[:kind], out_ref, buffer, sem)
+    outs, (buffer, sem) = refs[-6:-2], refs[-2:]
+    for step, out in enumerate(outs):
+        base = ((along_ref[1] + step) & 3) * 1024 + which * 384
+        copy_rows(
+            table_ref, out, lambda s, index: index, lambda s, index: s, lambda s, base=base: wanted_ref[base + s]
+        )
+    put_class(along_ref, kind, 1, x_ref, refs[:kind], outs, buffer, sem)
 
 
 def pick_join(which, kind, along, wanted, table, x, backs, *after):
@@ -212,7 +223,7 @@
         functools.partial(pick_join_body, which, kind),
         PAIR,
         [SMEM, SMEM, VMEM, VMEM] + [ANY] * (kind + len(after)),
-        VMEM,
+        (VMEM,) * 4,
         (along, wanted, table, x, *backs[:kind], *after),
         scratch=[pltpu.VMEM((4 * SLOTS, WIDE), F32), pltpu.SemaphoreType.DMA],
         flops=1 << 28,
@@ -220,37 +231,31 @@
     )
 
 
-def join_body(kinds, along_ref, x_ref, y_ref, b1, b2, b3, *refs):
-    out_ref, buffer, sem = refs[-3:]
-    for spot, (kind, ref) in enumerate(zip(kinds, (x_ref, y_ref))):
-        put_class(along_ref, kind, spot, ref, (b1, b2, b3), out_ref, buffer, sem)
-
-
-def join(kinds, along, x, y, backs, *after):
-    return kernel_call(
-        functools.partial(join_body, kinds),
+def join_body(along_ref, x_ref, y_ref, relayed_ref, b1, b2, b3, *refs):
+    outs, (buffer, sem) = refs[-6:-2], refs[-2:]
+    put_class(along_ref, 2, 0, x_ref, (b1, b2, b3), outs, buffer, sem)
+    put_class(along_ref, 3, 1, y_ref, (b1, b2, b3), outs, buffer, sem, relayed_ref)
+
+
+def join(along, x, y, relayed, backs, *after):
+    return kernel_call(
+        join_body,
         PAIR,
-        [SMEM, VMEM, VMEM] + [ANY] * (3 + len(after)),
-        VMEM,
-        (along, x, y, *backs, *after),
+        [SMEM, VMEM, VMEM, VMEM] + [ANY] * (3 + len(after)),
+        (VMEM,) * 4,
+        (along, x, y, relayed, *backs, *after),
         scratch=[pltpu.VMEM((4 * SLOTS, WIDE), F32), pltpu.SemaphoreType.DMA],
         flops=1 << 27,
         limit=8,
     )
 
 
-def put_rows(own_ref, x, cells, pitch=SLOTS, start=0):
-    def per_across(z, _):
+def put_rows(place_ref, own_ref, xs, cells, start):
+    for step, x in enumerate(xs):
+        base = ((place_ref[1] - step) & 3) * 512
         copy_rows(
-            x,
-            cells,
-            lambda s, index: z * pitch + start + s,
-            lambda s, index: index,
-            lambda s: own_ref[z * 512 + s],
+            x, cells, lambda s, index: start + s, lambda s, index: index, lambda s, base=base: own_ref[base + s]
         )
-        return 0
-
-    lax.fori_loop(0, 4, per_across, 0)
 
 
 def load_own(which, kinds, own_any, own, sems):
@@ -263,48 +268,48 @@
     return loads
 
 
-def place_early_body(which, kinds, own_any, x, after, cells, own0, own1, sems):
+def place_early_body(which, kinds, place_ref, own_any, x0, x1, x2, x3, cells, own0, own1, sems):
     for i, load in enumerate(load_own(which, kinds, own_any, (own0, own1), sems)):
         load.wait()
-        put_rows((own0, own1)[i], x, cells, 2 * SLOTS, i * SLOTS)
-
-
-def place_early(which, kinds, own, x, after):
+        put_rows(place_ref, (own0, own1)[i], (x0, x1, x2, x3), cells, i * SLOTS)
+
+
+def place_early(which, kinds, place, own, xs):
     return kernel_call(
         functools.partial(place_early_body, which, kinds),
         jax.ShapeDtypeStruct((CELLS + 8, WIDE), F32),
-        [ANY, VMEM, ANY],
+        [SMEM, ANY] + [VMEM] * 4,
         VMEM,
-        (own, x, after),
+        (place, own, *xs),
         scratch=[*([pltpu.SMEM((2048,), I32)] * 2), pltpu.SemaphoreType.DMA((2,))],
         flops=1 << 28,
     )
 
 
-def place_body(which, kinds, own_any, cells_ref, x, weight_ref, out_ref, cells, own0, own1, sems):
+def place_body(which, kinds, place_ref, own_any, cells_ref, x0, x1, x2, x3, weight_ref, out_ref, cells, own0, own1, sems):
     loads = load_own(which, kinds, own_any, (own0, own1), sems)
     cells[...] = cells_ref[...]
     for i, load in enumerate(loads):
         load.wait()
-        put_rows((own0, own1)[i], x, cells, 2 * SLOTS, i * SLOTS)
+        put_rows(place_ref, (own0, own1)[i], (x0, x1, x2, x3), cells, i * SLOTS)
 
     def mix(i, _):
-        rows = pl.ds(pl.multiple_of(i * 128, 128), 128)
+        rows = pl.ds(pl.multiple_of(i * 256, 256), 256)
         here = cells[rows, :]
         upper = pltpu.roll(here, WIDE - 1, 1)
         out_ref[rows, :] = here + weight_ref[rows, :] * (upper - here)
         return 0
 
-    lax.fori_loop(0, CELLS // 128, mix, 0)
-
-
-def place(which, kinds, own, cells, x, weight):
+    lax.fori_loop(0, CELLS // 256, mix, 0)
+
+
+def place(which, kinds, where, own, cells, xs, weight):
     return kernel_call(
         functools.partial(place_body, which, kinds),
         jax.ShapeDtypeStruct((CELLS, WIDE), F32),
-        [ANY] + [VMEM] * 3,
+        [SMEM, ANY] + [VMEM] * 6,
         VMEM,
-        (own, cells, x, weight),
+        (where, own, cells, *xs, weight),
         scratch=[
             pltpu.VMEM((CELLS + 8, WIDE), F32),
             *([pltpu.SMEM((2048,), I32)] * 2),
@@ -465,6 +470,20 @@
     return lax.ppermute(x, axis, pairs)
 
 
+def three_up():
+    count = lax.axis_size("along")
+    direct, relay = [], []
+    for a in range(count - 3):
+        if a % 2 == 0:
+            direct.append((a, a + 3))
+        else:
+            chip = a // 2
+            between = 2 * (chip // 4 * 4 + (chip - 1) % 4)
+            direct.append((a, between))
+            relay.append((between, a + 3))
+    return direct, relay
+
+
 def body(fields, first_feet, first_fraction, second_feet, second_fraction, lateral_mix, vertical_mix, bottom_drag, surface_stress):
     along = lax.axis_index("along")
     across = lax.axis_index("across")
@@ -477,6 +496,7 @@
         (VMEM,) * 2,
         (where, first_feet, second_feet),
     )
+    table = cells_first(fields.reshape(LEVELS * 8, COLS), 1).reshape(CELLS, WIDE)
     wanted = lax.all_to_all(wanted.reshape(4, SPAN, 8, WIDE), "across", split_axis=0, concat_axis=0, tiled=True)
     ahead = [wanted[:, 0]] + [move(wanted[:, t], "along", -t) for t in range(1, SPAN)]
     back = []
@@ -488,26 +508,34 @@
     ahead = [x.reshape(-1) for x in ahead]
     back = [x.reshape(-1) for x in back]
 
-    def turn(x):
-        x = x.reshape(4, 2 * SLOTS, WIDE)
-        return lax.all_to_all(x, "across", split_axis=0, concat_axis=0, tiled=True).reshape(-1, WIDE)
+    def turn(xs):
+        moved = {0: xs[0]}
+        for step in (2, 1, 3):
+            pairs = [(z, (z + step) % 4) for z in range(4)]
+            moved[step] = lax.ppermute(xs[step], "across", pairs)
+        return [moved[step] for step in range(4)]
 
     def fetch(which, table, weigh):
-        i, j, k = ORDER
-        pi = pick(which, ahead[i], table, *ahead[1:], *back)
-        pj = pick(which, ahead[j], table, pi)
-        pk = pick(which, ahead[k], table, pj)
-        xi, xj, xk = [move(p, "along", t) for t, p in ((i, pi), (j, pj), (k, pk))]
-        behind = [
-            lax.ppermute(x, "along", [(b, b - u) for b in range(u, SPAN)])
-            for u, x in zip((1, 2, 3), pick_back(which, where, back, table, pk))
-        ]
-        weight, done = weigh(pk)
-        joined = pick_join(which, i, where, ahead[0], table, xi, behind, pk, *done)
+        p3 = pick(which, where, ahead[3], table, *ahead[1:], *back)
+        answers = pick_back(which, where, back, table, p3)
+        behind = {}
+        for u in (3, 2, 1):
+            pairs = [(b, b - u) for b in range(u, SPAN)]
+            behind[u] = lax.ppermute(answers[u - 1], "along", pairs)
+        behind = [behind[u] for u in (1, 2, 3)]
+        p1 = pick(which, where, ahead[1], table, p3, *answers)
+        p2 = pick(which, where, ahead[2], table, p1)
+        direct, relay = three_up()
+        x3 = lax.ppermute(p3, "along", direct)
+        x1 = move(p1, "along", 1)
+        x2 = move(p2, "along", 2)
+        relayed = lax.ppermute(x3, "along", relay)
+        weight, done = weigh(p2)
+        joined = pick_join(which, 1, where, ahead[0], table, x1, behind, p2)
         early = turn(joined)
-        cells = place_early(which, (0, i), own, early, joined)
-        late = turn(join((j, k), where, xj, xk, behind, cells))
-        return place(which, (j, k), own, cells, late, weight)
+        late = turn(join(where, x2, x3, relayed, behind, joined[0], *done))
+        cells = place_early(which, (0, 1), where, own, early)
+        return place(which, (2, 3), where, own, cells, late, weight)
 
     mix = vertical_mix.reshape(2 * 39 * 8, COLS)
     inverse = []
@@ -521,7 +549,6 @@
         weight = cells_first(second_fraction.reshape(LAYERS * 8, COLS), 3, after)
         return weight.reshape(CELLS, WIDE), (weight,)
 
-    table = cells_first(fields.reshape(LEVELS * 8, COLS), 1).reshape(CELLS, WIDE)
     middle = fetch(0, table, first_weight)
     moved = fetch(1, middle, second_weight).reshape(ROWS, COLS, WIDE)
     up = move(moved[ROWS - 1], "across", 1)

time: 230 us -> 192 us (0.83)
  blocking collectives: 31.8 us -> 0 us
  Pallas kernels: 67.3 us -> 59.7 us
  local copies, waits for them, and re-layouts: 9.48 us -> 3.07 us
  waiting for transfers between devices: 47.5 us -> 52.6 us
  starting transfers between devices: 71.5 us -> 75 us
    all_to_all x2 -> x0, blocking collectives: 31.8 us -> none  [turn(): lax.all_to_all(x, 'across', split_axis=0, concat_axis=0, tiled=True)]
    ppermute x6 -> x22, waiting for transfers between devices: 16.4 us -> 41.5 us  [the longest x12 22.4 us: turn(): moved[step] = lax.ppermute(xs[step], 'across', pairs)]
    ppermute x6 -> x22, starting transfers between devices: 9.51 us -> 27.2 us  [the longest x6 12.5 us: fetch(): behind[u] = lax.ppermute(answers[u - 1], 'along', pairs)]
    ppermute x13 -> x11, waiting for transfers between devices: 19.6 us -> 6.55 us  [move(): return lax.ppermute(x, axis, pairs)]
    all_to_all x2 -> x0, starting transfers between devices: 8.54 us -> none  [turn(): lax.all_to_all(x, 'across', split_axis=0, concat_axis=0, tiled=True)]
    pallas_call x23, Pallas kernels: 67.3 us -> 59.7 us  [kernel_call(): pl.pallas_call(body, out_shape=out_shapes, in_specs=in_specs, out_specs=o...]
    all_to_all x2 -> x0, waiting for transfers between devices: 6.98 us -> none  [turn(): lax.all_to_all(x, 'across', split_axis=0, concat_axis=0, tiled=True)]
    ppermute x13 -> x11, starting transfers between devices: 40.5 us -> 33.8 us  [move(): return lax.ppermute(x, axis, pairs)]
  transfers between devices with their start and end apart: 25 -> 37, of which waited for: 9 -> 16; matrix products, arithmetic and copies ran while one was open for 0% -> 0% of each run, Pallas kernels for 11% -> 13%
where the time goes in v3:
time: 192 us; the launch traced here: 191 us
  starting transfers between devices  75 us (39%)
  Pallas kernels  59.7 us (31%)
  waiting for transfers between devices  52.6 us (27%)
  local copies, waits for them, and re-layouts  3.07 us (2%)
    pallas_call x23, Pallas kernels, kernel_call(): pl.pallas_call(body, out_shape=out_shapes, in_specs=in_specs, out_specs=o...  59.7 us
    ppermute x11, starting transfers between devices, move(): return lax.ppermute(x, axis, pairs)  33.8 us
    ppermute x12, waiting for transfers between devices, turn(): moved[step] = lax.ppermute(xs[step], 'across', pairs)  22.4 us
    ppermute x6, waiting for transfers between devices, fetch(): behind[u] = lax.ppermute(answers[u - 1], 'along', pairs)  19.2 us
    ppermute x6, starting transfers between devices, fetch(): behind[u] = lax.ppermute(answers[u - 1], 'along', pairs)  12.5 us
    ppermute x12, starting transfers between devices, turn(): moved[step] = lax.ppermute(xs[step], 'across', pairs)  10.6 us
    ppermute x3, starting transfers between devices, body(): back.append(lax.ppermute(payload, 'along', pairs))  8.21 us
    ppermute x11, waiting for transfers between devices, move(): return lax.ppermute(x, axis, pairs)  6.55 us
  transfers between devices with their start and end apart: 37, of which 16 were waited for; matrix products, arithmetic and copies ran while one was open for 0% of the time, Pallas kernels for 13%

profile of v3, /device:TPU:1, one launch (start us, length us, event | category | flops | bytes accessed | tf_op | source)
XLA Modules:
  0.0 191.1 jit_solution(18293176211401240446)
XLA Ops:
  1.5 3.5 %shard_map.91 = (s32[128,128]{1,0:T(8,128)}, s32[128,128]{1,0:T(8,128)S(1)}) custom-call(s32[2]{0:T(128)S(1)} %pad_add_fusion.along_ref.place_ref, s32[8,512]{1,0:T(8,128)S(1)} %copy-done.7, s32[8,512]{1,0:T(8,128)S(1)} %copy-done.8), custom_call_target="tpu_custom_call" | custom-call | flops 1048576 | bytes 2097152 | tf_op jit(solution)/shard_map/pallas_call | solution.py:33
  5.0 5.8 %all-to-all-start = ((s32[4,4,8,128]{3,2,1,0:T(8,128)}), s32[4,4,8,128]{3,2,1,0:T(8,128)S(1)}, u32[]{:S(2)}, u32[]{:S(2)}) async-start(s32[4,4,8,128]{3,2,1,0:T(8,128)} %bitcast.3), calls=%async_computation | async-start | bytes 131072 | tf_op jit(solution)/shard_map/all_to_all | solution.py:500
  10.8 4.5 %all-to-all-done = s32[4,4,8,128]{3,2,1,0:T(8,128)S(1)} async-done(((s32[4,4,8,128]{3,2,1,0:T(8,128)}), s32[4,4,8,128]{3,2,1,0:T(8,128)S(1)}, u32[]{:S(2)}, u32[]{:S(2)}) %all-to-all-start) | async-done | bytes 65568 | tf_op jit(solution)/shard_map/all_to_all | solution.py:500
  16.6 6.3 %collective-permute-start.3 = (s32[4,8,128]{2,1,0:T(8,128)S(1)}, s32[4,8,128]{2,1,0:T(8,128)S(1)}, u32[]{:S(2)}, u32[]{:S(2)}) collective-permute-start(s32[4,8,128]{2,1,0:T(8,128)S(1)} %get-tuple-element.59), channel_id=1, source_target_pairs={{0,4},{4,8},{8,12},{1,5},{5,9},{9,13},{2,6},{6,10},{10,14},{3,7},{... | collective-permute-start | bytes 49160 | tf_op jit(solution)/shard_map/ppermute | solution.py:506
  24.9 3.6 %collective-permute-start = (s32[4,8,128]{2,1,0:T(8,128)S(1)}, s32[4,8,128]{2,1,0:T(8,128)S(1)}, u32[]{:S(2)}, u32[]{:S(2)}) collective-permute-start(s32[4,8,128]{2,1,0:T(8,128)S(1)} %get-tuple-element.62), channel_id=1, source_target_pairs={{4,0},{8,4},{12,8},{16,12},{20,16},{24,20},{28,24},{32,28},{36,32}... | collective-permute-start | bytes 49160 | tf_op jit(solution)/shard_map/ppermute | solution.py:470
  29.7 1.5 copy-done.1
  32.6 2.4 %collective-permute-done.1 = s32[4,8,128]{2,1,0:T(8,128)S(1)} collective-permute-done((s32[4,8,128]{2,1,0:T(8,128)S(1)}, s32[4,8,128]{2,1,0:T(8,128)S(1)}, u32[]{:S(2)}, u32[]{:S(2)}) %collective-permute-start.1) | collective-permute-done | bytes 16416 | tf_op jit(solution)/shard_map/ppermute | solution.py:470
  35.0 2.2 %shard_map.93.after.refs_0_ = f32[1152,128]{1,0:T(8,128)S(1)} custom-call(s32[2]{0:T(128)S(1)} %pad_add_fusion.along_ref.place_ref, s32[4096]{0:T(1024)S(1)} %bitcast.78, f32[4096,128]{1,0:T(8,128)S(1)} %bitcast.40, s32[4096]{0:T(1024)S(1)} %bitcast.74, s32[4096]{0:T(1024)S(1)} %bitcast.58, s32[4096]{0:T(1024)S(1)} %bitcast.79, s32[4096]{0:T(1024)S(1)} %bitcast.62, ...), custom_call_target="tpu_custom_call" | custom-call | flops 268435456 | bytes 2097152 | tf_op jit(solution)/shard_map/pallas_call | solution.py:33
  37.2 2.8 %shard_map.94 = (f32[1152,128]{1,0:T(8,128)S(1)}, f32[1152,128]{1,0:T(8,128)S(1)}, f32[1152,128]{1,0:T(8,128)S(1)}) custom-call(s32[2]{0:T(128)S(1)} %pad_add_fusion.along_ref.place_ref, s32[4096]{0:T(1024)S(1)} %bitcast.63, s32[4096]{0:T(1024)S(1)} %bitcast.67, s32[4096]{0:T(1024)S(1)} %bitcast.71, f32[4096,128]{1,0:T(8,128)S(1)} %bitcast.41, ...), custom_call_target="tpu_custom_call" | custom-call | flops 1048576 | bytes 2097152 | tf_op jit(solution)/shard_map/pallas_call | solution.py:33
  40.1 2.2 %shard_map.95.refs_0_ = f32[1152,128]{1,0:T(8,128)S(1)} custom-call(s32[2]{0:T(128)S(1)} %pad_add_fusion.along_ref.place_ref, s32[4096]{0:T(1024)S(1)} %bitcast.75, f32[4096,128]{1,0:T(8,128)S(1)} %bitcast.42, f32[1152,128]{1,0:T(8,128)S(1)} %shard_map.93.after.refs_0_, f32[1152,128]{1,0:T(8,128)S(1)} %get-tuple-element.31.refs_1_, ...), custom_call_target="tpu_custom_call" | custom-call | flops 268435456 | bytes 2097152 | tf_op jit(solution)/shard_map/pallas_call | solution.py:33
  42.3 1.9 %collective-permute-start.6 = (f32[1152,128]{1,0:T(8,128)S(1)}, f32[1152,128]{1,0:T(8,128)S(1)}, u32[]{:S(2)}, u32[]{:S(2)}) collective-permute-start(f32[1152,128]{1,0:T(8,128)S(1)} %shard_map.95.refs_0_), channel_id=1, source_target_pairs={{0,4},{4,8},{8,12},{12,16},{16,20},{20,24},{24,28},{28,32},{32,36}... | collective-permute-start | bytes 1769480 | tf_op jit(solution)/shard_map/ppermute | solution.py:470
  44.3 1.3 collective-permute-start.12
  45.6 4.7 %collective-permute-start.7 = (f32[1152,128]{1,0:T(8,128)S(1)}, f32[1152,128]{1,0:T(8,128)S(1)}, u32[]{:S(2)}, u32[]{:S(2)}) collective-permute-start(f32[1152,128]{1,0:T(8,128)S(1)} %get-tuple-element.31.refs_1_), channel_id=1, source_target_pairs={{4,0},{8,4},{12,8},{5,1},{9,5},{13,9},{6,2},{10,6},{14,10},{7,3},{... | collective-permute-start | bytes 1769480 | tf_op jit(solution)/shard_map/ppermute | solution.py:524
  50.4 2.2 %shard_map.96.refs_1_.refs_0_.after_ref = f32[1152,128]{1,0:T(8,128)S(1)} custom-call(s32[2]{0:T(128)S(1)} %pad_add_fusion.along_ref.place_ref, s32[4096]{0:T(1024)S(1)} %bitcast.59, f32[4096,128]{1,0:T(8,128)S(1)} %bitcast.43, f32[1152,128]{1,0:T(8,128)S(1)} %shard_map.95.refs_0_), custom_call_target="tpu_custom_call" | custom-call | flops 268435456 | bytes 2097152 | tf_op jit(solution)/shard_map/pallas_call | solution.py:33
  52.6 2.2 %collective-permute-start.11 = (f32[1152,128]{1,0:T(8,128)S(1)}, f32[1152,128]{1,0:T(8,128)S(1)}, u32[]{:S(2)}, u32[]{:S(2)}) collective-permute-start(f32[1152,128]{1,0:T(8,128)S(1)} %shard_map.96.refs_1_.refs_0_.after_ref), channel_id=1, source_target_pairs={{0,8},{4,12},{8,16},{12,20},{16,24},{20,28},{24,32},{28,36},{32,40... | collective-permute-start | bytes 1769480 | tf_op jit(solution)/shard_map/ppermute | solution.py:470
  57.6 6.5 %collective-permute-done.7.refs_0_.b1 = f32[1152,128]{1,0:T(8,128)S(1)} collective-permute-done((f32[1152,128]{1,0:T(8,128)S(1)}, f32[1152,128]{1,0:T(8,128)S(1)}, u32[]{:S(2)}, u32[]{:S(2)}) %collective-permute-start.7) | collective-permute-done | bytes 589856 | tf_op jit(solution)/shard_map/ppermute | solution.py:524
  64.1 2.2 %shard_map.97 = (f32[576,128]{1,0:T(8,128)S(1)}, f32[576,128]{1,0:T(8,128)S(1)}, f32[576,128]{1,0:T(8,128)S(1)}, f32[576,128]{1,0:T(8,128)S(1)}) custom-call(s32[2]{0:T(128)S(1)} %pad_add_fusion.along_ref.place_ref, s32[4096]{0:T(1024)S(1)} %get-tuple-element.63.wanted_ref, f32[4096,128]{1,0:T(8,128)S(1)} %bitcast.44, ...), custom_call_target="tpu_custom_call" | custom-call | flops 268435456 | bytes 2097152 | tf_op jit(solution)/shard_map/pallas_call | solution.py:33
  68.2 3.9 %collective-permute-done.14.b2 = f32[1152,128]{1,0:T(8,128)S(1)} collective-permute-done((f32[1152,128]{1,0:T(8,128)S(1)}, f32[1152,128]{1,0:T(8,128)S(1)}, u32[]{:S(2)}, u32[]{:S(2)}) %collective-permute-start.14) | collective-permute-done | bytes 589856 | tf_op jit(solution)/shard_map/ppermute | solution.py:524
  74.0 1.7 shard_map.100.refs_2_.inverse_ref
  77.5 2.4 %collective-permute-start.17 = (f32[576,128]{1,0:T(8,128)S(1)}, f32[576,128]{1,0:T(8,128)S(1)}, u32[]{:S(2)}, u32[]{:S(2)}) collective-permute-start(f32[576,128]{1,0:T(8,128)S(1)} %get-tuple-element.40), channel_id=1, source_target_pairs={{0,2},{1,3},{2,0},{3,1},{4,6},{5,7},{6,4},{7,5},{8,10},{9,11},{10,... | collective-permute-start | bytes 884744 | tf_op jit(solution)/shard_map/ppermute | solution.py:515
  81.1 3.9 %shard_map.98.cells_ref = f32[4104,128]{1,0:T(8,128)S(1)} custom-call(s32[2]{0:T(128)S(1)} %pad_add_fusion.along_ref.place_ref, s32[16384]{0:T(1024)S(1)} %bitcast.52, f32[576,128]{1,0:T(8,128)S(1)} %get-tuple-element.34.x0.refs_0_, f32[576,128]{1,0:T(8,128)S(1)} %collective-permute-done.8.x1, f32[576,128]{1,0:T(8,128)S(1)} %collective-permute-done.9.x2, ...), custom_call_target="tpu_custom_call" | custom-call | flops 268435456 | bytes 2097152 | tf_op jit(solution)/shard_map/pallas_call | solution.py:33
  85.1 3.7 %collective-permute-done.16.x1 = f32[576,128]{1,0:T(8,128)S(1)} collective-permute-done((f32[576,128]{1,0:T(8,128)S(1)}, f32[576,128]{1,0:T(8,128)S(1)}, u32[]{:S(2)}, u32[]{:S(2)}) %collective-permute-start.16) | collective-permute-done | bytes 294944 | tf_op jit(solution)/shard_map/ppermute | solution.py:515
  88.8 3.8 %collective-permute-done.17.x2 = f32[576,128]{1,0:T(8,128)S(1)} collective-permute-done((f32[576,128]{1,0:T(8,128)S(1)}, f32[576,128]{1,0:T(8,128)S(1)}, u32[]{:S(2)}, u32[]{:S(2)}) %collective-permute-start.17) | collective-permute-done | bytes 294944 | tf_op jit(solution)/shard_map/ppermute | solution.py:515
  93.8 5.6 %shard_map.102.table_ref.table = f32[4096,128]{1,0:T(8,128)S(1)} custom-call(s32[2]{0:T(128)S(1)} %pad_add_fusion.along_ref.place_ref, s32[16384]{0:T(1024)S(1)} %bitcast.53, f32[4104,128]{1,0:T(8,128)S(1)} %shard_map.98.cells_ref, f32[576,128]{1,0:T(8,128)S(1)} %get-tuple-element.38.x0, f32[576,128]{1,0:T(8,128)S(1)} %collective-permute-done.16.x1, ...), custom_call_target="tpu_custom_call" | custom-call | flops 268435456 | bytes 2097152 | tf_op jit(solution)/shard_map/pallas_call | solution.py:33
  99.4 2.2 %shard_map.103.after.refs_0_ = f32[1152,128]{1,0:T(8,128)S(1)} custom-call(s32[2]{0:T(128)S(1)} %pad_add_fusion.along_ref.place_ref, s32[4096]{0:T(1024)S(1)} %bitcast.80, f32[4096,128]{1,0:T(8,128)S(1)} %shard_map.102.table_ref.table, s32[4096]{0:T(1024)S(1)} %bitcast.76, s32[4096]{0:T(1024)S(1)} %bitcast.60, s32[4096]{0:T(1024)S(1)} %bitcast.81, ...), custom_call_target="tpu_custom_call" | custom-call | flops 268435456 | bytes 2097152 | tf_op jit(solution)/shard_map/pallas_call | solution.py:33
  101.7 2.8 %shard_map.104 = (f32[1152,128]{1,0:T(8,128)S(1)}, f32[1152,128]{1,0:T(8,128)S(1)}, f32[1152,128]{1,0:T(8,128)S(1)}) custom-call(s32[2]{0:T(128)S(1)} %pad_add_fusion.along_ref.place_ref, s32[4096]{0:T(1024)S(1)} %bitcast.65, s32[4096]{0:T(1024)S(1)} %bitcast.69, s32[4096]{0:T(1024)S(1)} %bitcast.73, f32[4096,128]{1,0:T(8,128)S(1)} %shard_map.102.table_ref.table, ...), custom_call_target="tpu_custom_call" | custom-call | flops 1048576 | bytes 2097152 | tf_op jit(solution)/shard_map/pallas_call | solution.py:33
  104.5 2.2 %shard_map.105.refs_0_ = f32[1152,128]{1,0:T(8,128)S(1)} custom-call(s32[2]{0:T(128)S(1)} %pad_add_fusion.along_ref.place_ref, s32[4096]{0:T(1024)S(1)} %bitcast.77, f32[4096,128]{1,0:T(8,128)S(1)} %shard_map.102.table_ref.table, f32[1152,128]{1,0:T(8,128)S(1)} %shard_map.103.after.refs_0_, f32[1152,128]{1,0:T(8,128)S(1)} %get-tuple-element.42.refs_1_, ...), custom_call_target="tpu_custom_call" | custom-call | flops 268435456 | bytes 2097152 | tf_op jit(solution)/shard_map/pallas_call | solution.py:33
  106.8 9.2 %collective-permute-start.19 = (f32[1152,128]{1,0:T(8,128)S(1)}, f32[1152,128]{1,0:T(8,128)S(1)}, u32[]{:S(2)}, u32[]{:S(2)}) collective-permute-start(f32[1152,128]{1,0:T(8,128)S(1)} %shard_map.105.refs_0_), channel_id=1, source_target_pairs={{0,4},{4,8},{8,12},{12,16},{16,20},{20,24},{24,28},{28,32},{32,36}... | collective-permute-start | bytes 1769480 | tf_op jit(solution)/shard_map/ppermute | solution.py:470
  116.0 1.3 collective-permute-start.25
  117.3 3.8 %collective-permute-start.20 = (f32[1152,128]{1,0:T(8,128)S(1)}, f32[1152,128]{1,0:T(8,128)S(1)}, u32[]{:S(2)}, u32[]{:S(2)}) collective-permute-start(f32[1152,128]{1,0:T(8,128)S(1)} %get-tuple-element.42.refs_1_), channel_id=1, source_target_pairs={{4,0},{8,4},{12,8},{5,1},{9,5},{13,9},{6,2},{10,6},{14,10},{7,3},{... | collective-permute-start | bytes 1769480 | tf_op jit(solution)/shard_map/ppermute | solution.py:524
  121.1 2.2 %shard_map.106.refs_1_.refs_0_ = f32[1152,128]{1,0:T(8,128)S(1)} custom-call(s32[2]{0:T(128)S(1)} %pad_add_fusion.along_ref.place_ref, s32[4096]{0:T(1024)S(1)} %bitcast.61, f32[4096,128]{1,0:T(8,128)S(1)} %shard_map.102.table_ref.table, f32[1152,128]{1,0:T(8,128)S(1)} %shard_map.105.refs_0_), custom_call_target="tpu_custom_call" | custom-call | flops 268435456 | bytes 2097152 | tf_op jit(solution)/shard_map/pallas_call | solution.py:33
  123.3 2.2 %collective-permute-start.24 = (f32[1152,128]{1,0:T(8,128)S(1)}, f32[1152,128]{1,0:T(8,128)S(1)}, u32[]{:S(2)}, u32[]{:S(2)}) collective-permute-start(f32[1152,128]{1,0:T(8,128)S(1)} %shard_map.106.refs_1_.refs_0_), channel_id=1, source_target_pairs={{0,8},{4,12},{8,16},{12,20},{16,24},{20,28},{24,32},{28,36},{32,40... | collective-permute-start | bytes 1769480 | tf_op jit(solution)/shard_map/ppermute | solution.py:470
  128.3 6.5 %collective-permute-done.20.refs_0_.b1 = f32[1152,128]{1,0:T(8,128)S(1)} collective-permute-done((f32[1152,128]{1,0:T(8,128)S(1)}, f32[1152,128]{1,0:T(8,128)S(1)}, u32[]{:S(2)}, u32[]{:S(2)}) %collective-permute-start.20) | collective-permute-done | bytes 589856 | tf_op jit(solution)/shard_map/ppermute | solution.py:524
  134.8 2.2 %shard_map.107 = (f32[576,128]{1,0:T(8,128)S(1)}, f32[576,128]{1,0:T(8,128)S(1)}, f32[576,128]{1,0:T(8,128)S(1)}, f32[576,128]{1,0:T(8,128)S(1)}) custom-call(s32[2]{0:T(128)S(1)} %pad_add_fusion.along_ref.place_ref, s32[4096]{0:T(1024)S(1)} %get-tuple-element.63.wanted_ref, f32[4096,128]{1,0:T(8,128)S(1)} %shard_map.102.table_ref.table, ...), custom_call_target="tpu_custom_call" | custom-call | flops 268435456 | bytes 2097152 | tf_op jit(solution)/shard_map/pallas_call | solution.py:33
  137.1 1.5 collective-permute-done.24.x_ref
  138.7 1.9 collective-permute-start.22
  140.5 2.3 %collective-permute-done.27.b2 = f32[1152,128]{1,0:T(8,128)S(1)} collective-permute-done((f32[1152,128]{1,0:T(8,128)S(1)}, f32[1152,128]{1,0:T(8,128)S(1)}, u32[]{:S(2)}, u32[]{:S(2)}) %collective-permute-start.27) | collective-permute-done | bytes 589856 | tf_op jit(solution)/shard_map/ppermute | solution.py:524
  147.3 5.8 %collective-permute-done.21.x1 = f32[576,128]{1,0:T(8,128)S(1)} collective-permute-done((f32[576,128]{1,0:T(8,128)S(1)}, f32[576,128]{1,0:T(8,128)S(1)}, u32[]{:S(2)}, u32[]{:S(2)}) %collective-permute-start.21) | collective-permute-done | bytes 294944 | tf_op jit(solution)/shard_map/ppermute | solution.py:515
  153.2 3.9 %shard_map.108.cells_ref = f32[4104,128]{1,0:T(8,128)S(1)} custom-call(s32[2]{0:T(128)S(1)} %pad_add_fusion.along_ref.place_ref, s32[16384]{0:T(1024)S(1)} %bitcast.54, f32[576,128]{1,0:T(8,128)S(1)} %get-tuple-element.45.x0.refs_0_, f32[576,128]{1,0:T(8,128)S(1)} %collective-permute-done.21.x1, f32[576,128]{1,0:T(8,128)S(1)} %collective-permute-done.22.x2, ...), custom_call_target="tpu_custom_call" | custom-call | flops 268435456 | bytes 2097152 | tf_op jit(solution)/shard_map/pallas_call | solution.py:33
  157.1 1.4 collective-permute-done.29.x1
  158.5 2.5 %collective-permute-done.30.x2 = f32[576,128]{1,0:T(8,128)S(1)} collective-permute-done((f32[576,128]{1,0:T(8,128)S(1)}, f32[576,128]{1,0:T(8,128)S(1)}, u32[]{:S(2)}, u32[]{:S(2)}) %collective-permute-start.30) | collective-permute-done | bytes 294944 | tf_op jit(solution)/shard_map/ppermute | solution.py:515
  161.0 3.9 %collective-permute-done.31.x3 = f32[576,128]{1,0:T(8,128)S(1)} collective-permute-done((f32[576,128]{1,0:T(8,128)S(1)}, f32[576,128]{1,0:T(8,128)S(1)}, u32[]{:S(2)}, u32[]{:S(2)}) %collective-permute-start.31) | collective-permute-done | bytes 294944 | tf_op jit(solution)/shard_map/ppermute | solution.py:515
  164.9 5.6 %shard_map.111 = f32[4096,128]{1,0:T(8,128)S(1)} custom-call(s32[2]{0:T(128)S(1)} %pad_add_fusion.along_ref.place_ref, s32[16384]{0:T(1024)S(1)} %bitcast.55, f32[4104,128]{1,0:T(8,128)S(1)} %shard_map.108.cells_ref, f32[576,128]{1,0:T(8,128)S(1)} %get-tuple-element.49.x0, f32[576,128]{1,0:T(8,128)S(1)} %collective-permute-done.29.x1, ...), custom_call_target="tpu_custom_call" | custom-call | flops 268435456 | bytes 2097152 | tf_op jit(solution)/shard_map/pallas_call | solution.py:33
  170.6 1.6 collective-permute-start.32
  173.5 7.3 %collective-permute-start.34 = (f32[8,128]{1,0:T(8,128)S(1)}, f32[8,128]{1,0:T(8,128)S(1)}, u32[]{:S(2)}, u32[]{:S(2)}) collective-permute-start(f32[8,128]{1,0:T(8,128)S(1)} %bitcast.84), channel_id=1, source_target_pairs={{0,4},{4,8},{8,12},{12,16},{16,20},{20,24},{24,28},{28,32},{32,36}... | collective-permute-start | bytes 12296 | tf_op jit(solution)/shard_map/ppermute | solution.py:470
  180.8 1.9 %collective-permute-start.35 = (f32[8,128]{1,0:T(8,128)S(1)}, f32[8,128]{1,0:T(8,128)S(1)}, u32[]{:S(2)}, u32[]{:S(2)}) collective-permute-start(f32[8,128]{1,0:T(8,128)S(1)} %bitcast.83), channel_id=1, source_target_pairs={{4,0},{8,4},{12,8},{16,12},{20,16},{24,20},{28,24},{32,28},{36,32}... | collective-permute-start | bytes 12296 | tf_op jit(solution)/shard_map/ppermute | solution.py:470
  183.7 2.0 %collective-permute-done.35.right_ref = f32[8,128]{1,0:T(8,128)S(1)} collective-permute-done((f32[8,128]{1,0:T(8,128)S(1)}, f32[8,128]{1,0:T(8,128)S(1)}, u32[]{:S(2)}, u32[]{:S(2)}) %collective-permute-start.35) | collective-permute-done | bytes 4128 | tf_op jit(solution)/shard_map/ppermute | solution.py:470
  185.7 5.3 %shard_map.113 = f32[960,512]{1,0:T(8,128)} custom-call(s32[2]{0:T(128)S(1)} %pad_add_fusion.along_ref.place_ref, f32[3840,128]{1,0:T(8,128)S(1)} %shard_map.112.moved_ref, f32[512,128]{1,0:T(8,128)S(1)} %collective-permute-done.32.up_ref, f32[512,128]{1,0:T(8,128)S(1)} %collective-permute-done.33.down_ref, f32[8,128]{1,0:T(8,128)S(1)} %collective-permute-done.34.left_ref, ...), custom_call_target="tpu_custom_call" | custom-call | flops 1048576 | bytes 2097152 | tf_op jit(solution)/shard_map/pallas_call | solution.py:33
  (71 shorter events, 27.6 us)
Async XLA Ops:
  0.1 0.7 copy-start.7
  0.8 0.7 copy-start.8
  5.0 10.3 %all-to-all-start = ((s32[4,4,8,128]{3,2,1,0:T(8,128)}), s32[4,4,8,128]{3,2,1,0:T(8,128)S(1)}, u32[]{:S(2)}, u32[]{:S(2)}) async-start(s32[4,4,8,128]{3,2,1,0:T(8,128)} %bitcast.3), calls=%async_computation | async-start | bytes 131072 | tf_op jit(solution)/shard_map/all_to_all | solution.py:500
  15.3 13.1 %collective-permute-start.2 = (s32[4,8,128]{2,1,0:T(8,128)S(1)}, s32[4,8,128]{2,1,0:T(8,128)S(1)}, u32[]{:S(2)}, u32[]{:S(2)}) collective-permute-start(s32[4,8,128]{2,1,0:T(8,128)S(1)} %get-tuple-element.60), channel_id=1, source_target_pairs={{8,0},{12,4},{16,8},{20,12},{24,16},{28,20},{32,24},{36,28},{40,32... | collective-permute-start | bytes 49160 | tf_op jit(solution)/shard_map/ppermute | solution.py:470
  16.6 16.0 %collective-permute-start.3 = (s32[4,8,128]{2,1,0:T(8,128)S(1)}, s32[4,8,128]{2,1,0:T(8,128)S(1)}, u32[]{:S(2)}, u32[]{:S(2)}) collective-permute-start(s32[4,8,128]{2,1,0:T(8,128)S(1)} %get-tuple-element.59), channel_id=1, source_target_pairs={{0,4},{4,8},{8,12},{1,5},{5,9},{9,13},{2,6},{6,10},{10,14},{3,7},{... | collective-permute-start | bytes 49160 | tf_op jit(solution)/shard_map/ppermute | solution.py:506
  22.9 9.7 %collective-permute-start.4 = (s32[4,8,128]{2,1,0:T(8,128)S(1)}, s32[4,8,128]{2,1,0:T(8,128)S(1)}, u32[]{:S(2)}, u32[]{:S(2)}) collective-permute-start(s32[4,8,128]{2,1,0:T(8,128)S(1)} %get-tuple-element.58), channel_id=1, source_target_pairs={{0,8},{4,12},{1,9},{5,13},{2,10},{6,14},{3,11},{7,15}} | collective-permute-start | bytes 49160 | tf_op jit(solution)/shard_map/ppermute | solution.py:506
  24.2 8.4 %collective-permute-start.5 = (s32[4,8,128]{2,1,0:T(8,128)S(1)}, s32[4,8,128]{2,1,0:T(8,128)S(1)}, u32[]{:S(2)}, u32[]{:S(2)}) collective-permute-start(s32[4,8,128]{2,1,0:T(8,128)S(1)} %get-tuple-element.57), channel_id=1, source_target_pairs={{0,12},{1,13},{2,14},{3,15}} | collective-permute-start | bytes 49160 | tf_op jit(solution)/shard_map/ppermute | solution.py:506
  24.9 7.8 %collective-permute-start = (s32[4,8,128]{2,1,0:T(8,128)S(1)}, s32[4,8,128]{2,1,0:T(8,128)S(1)}, u32[]{:S(2)}, u32[]{:S(2)}) collective-permute-start(s32[4,8,128]{2,1,0:T(8,128)S(1)} %get-tuple-element.62), channel_id=1, source_target_pairs={{4,0},{8,4},{12,8},{16,12},{20,16},{24,20},{28,24},{32,28},{36,32}... | collective-permute-start | bytes 49160 | tf_op jit(solution)/shard_map/ppermute | solution.py:470
  28.4 6.6 %collective-permute-start.1 = (s32[4,8,128]{2,1,0:T(8,128)S(1)}, s32[4,8,128]{2,1,0:T(8,128)S(1)}, u32[]{:S(2)}, u32[]{:S(2)}) collective-permute-start(s32[4,8,128]{2,1,0:T(8,128)S(1)} %get-tuple-element.61), channel_id=1, source_target_pairs={{12,0},{16,4},{20,8},{24,12},{28,16},{32,20},{36,24},{40,28},{44,3... | collective-permute-start | bytes 49160 | tf_op jit(solution)/shard_map/ppermute | solution.py:470
  29.7 1.5 copy-start.1
  42.3 13.8 %collective-permute-start.6 = (f32[1152,128]{1,0:T(8,128)S(1)}, f32[1152,128]{1,0:T(8,128)S(1)}, u32[]{:S(2)}, u32[]{:S(2)}) collective-permute-start(f32[1152,128]{1,0:T(8,128)S(1)} %shard_map.95.refs_0_), channel_id=1, source_target_pairs={{0,4},{4,8},{8,12},{12,16},{16,20},{20,24},{24,28},{28,32},{32,36}... | collective-permute-start | bytes 1769480 | tf_op jit(solution)/shard_map/ppermute | solution.py:470
  44.3 12.6 %collective-permute-start.12 = (f32[1152,128]{1,0:T(8,128)S(1)}, f32[1152,128]{1,0:T(8,128)S(1)}, u32[]{:S(2)}, u32[]{:S(2)}) collective-permute-start(f32[1152,128]{1,0:T(8,128)S(1)} %shard_map.93.after.refs_0_), channel_id=1, source_target_pairs={{0,12},{4,24},{8,20},{12,0},{16,28},{20,8},{24,36},{28,16},{32,44}... | collective-permute-start | bytes 1769480 | tf_op jit(solution)/shard_map/ppermute | solution.py:529
  45.6 18.5 %collective-permute-start.7 = (f32[1152,128]{1,0:T(8,128)S(1)}, f32[1152,128]{1,0:T(8,128)S(1)}, u32[]{:S(2)}, u32[]{:S(2)}) collective-permute-start(f32[1152,128]{1,0:T(8,128)S(1)} %get-tuple-element.31.refs_1_), channel_id=1, source_target_pairs={{4,0},{8,4},{12,8},{5,1},{9,5},{13,9},{6,2},{10,6},{14,10},{7,3},{... | collective-permute-start | bytes 1769480 | tf_op jit(solution)/shard_map/ppermute | solution.py:524
  52.6 20.2 %copy-start.2 = (f32[40,8,512]{2,1,0:T(8,128)S(1)}, f32[40,8,512]{2,1,0:T(8,128)}, u32[]{:S(2)}) copy-start(f32[40,8,512]{2,1,0:T(8,128)} %param.11) | copy-start | bytes 1966084
  52.6 15.3 %collective-permute-start.11 = (f32[1152,128]{1,0:T(8,128)S(1)}, f32[1152,128]{1,0:T(8,128)S(1)}, u32[]{:S(2)}, u32[]{:S(2)}) collective-permute-start(f32[1152,128]{1,0:T(8,128)S(1)} %shard_map.96.refs_1_.refs_0_.after_ref), channel_id=1, source_target_pairs={{0,8},{4,12},{8,16},{12,20},{16,24},{20,28},{24,32},{28,36},{32,40... | collective-permute-start | bytes 1769480 | tf_op jit(solution)/shard_map/ppermute | solution.py:470
  54.9 17.2 %collective-permute-start.14 = (f32[1152,128]{1,0:T(8,128)S(1)}, f32[1152,128]{1,0:T(8,128)S(1)}, u32[]{:S(2)}, u32[]{:S(2)}) collective-permute-start(f32[1152,128]{1,0:T(8,128)S(1)} %get-tuple-element.32.refs_2_), channel_id=1, source_target_pairs={{8,0},{12,4},{9,1},{13,5},{10,2},{14,6},{11,3},{15,7}} | collective-permute-start | bytes 1769480 | tf_op jit(solution)/shard_map/ppermute | solution.py:524
  56.2 19.5 %collective-permute-start.15 = (f32[1152,128]{1,0:T(8,128)S(1)}, f32[1152,128]{1,0:T(8,128)S(1)}, u32[]{:S(2)}, u32[]{:S(2)}) collective-permute-start(f32[1152,128]{1,0:T(8,128)S(1)} %get-tuple-element.33.refs_3_), channel_id=1, source_target_pairs={{12,0},{13,1},{14,2},{15,3}} | collective-permute-start | bytes 1769480 | tf_op jit(solution)/shard_map/ppermute | solution.py:524
  56.9 18.8 %collective-permute-start.13 = (f32[1152,128]{1,0:T(8,128)S(1)}, f32[1152,128]{1,0:T(8,128)S(1)}, u32[]{:S(2)}, u32[]{:S(2)}) collective-permute-start(f32[1152,128]{1,0:T(8,128)S(1)} %collective-permute-done.12.y_ref), channel_id=1, source_target_pairs={{24,16},{0,24},{8,32},{16,40},{56,48},{32,56},{40,64},{48,72},{88,... | collective-permute-start | bytes 1769480 | tf_op jit(solution)/shard_map/ppermute | solution.py:532
  66.3 7.6 %copy-start = (f32[2,39,8,512]{3,2,1,0:T(8,128)S(1)}, f32[2,39,8,512]{3,2,1,0:T(8,128)}, u32[]{:S(2)}) copy-start(f32[2,39,8,512]{3,2,1,0:T(8,128)} %param.15) | copy-start | bytes 3833860
  66.3 7.6 %copy-start.5 = (f32[8,512]{1,0:T(8,128)S(1)}, f32[8,512]{1,0:T(8,128)}, u32[]{:S(2)}) copy-start(f32[8,512]{1,0:T(8,128)} %drag_ref.1) | copy-start | bytes 49156
  66.3 13.6 %collective-permute-start.10 = (f32[576,128]{1,0:T(8,128)S(1)}, f32[576,128]{1,0:T(8,128)S(1)}, u32[]{:S(2)}, u32[]{:S(2)}) collective-permute-start(f32[576,128]{1,0:T(8,128)S(1)} %get-tuple-element.37), channel_id=1, source_target_pairs={{0,3},{1,0},{2,1},{3,2},{4,7},{5,4},{6,5},{7,6},{8,11},{9,8},{10,9... | collective-permute-start | bytes 884744 | tf_op jit(solution)/shard_map/ppermute | solution.py:515
  67.9 13.2 %collective-permute-start.8 = (f32[576,128]{1,0:T(8,128)S(1)}, f32[576,128]{1,0:T(8,128)S(1)}, u32[]{:S(2)}, u32[]{:S(2)}) collective-permute-start(f32[576,128]{1,0:T(8,128)S(1)} %get-tuple-element.35), channel_id=1, source_target_pairs={{0,1},{1,2},{2,3},{3,0},{4,5},{5,6},{6,7},{7,4},{8,9},{9,10},{10,1... | collective-permute-start | bytes 884744 | tf_op jit(solution)/shard_map/ppermute | solution.py:515
  72.1 9.0 %collective-permute-start.9 = (f32[576,128]{1,0:T(8,128)S(1)}, f32[576,128]{1,0:T(8,128)S(1)}, u32[]{:S(2)}, u32[]{:S(2)}) collective-permute-start(f32[576,128]{1,0:T(8,128)S(1)} %get-tuple-element.36), channel_id=1, source_target_pairs={{0,2},{1,3},{2,0},{3,1},{4,6},{5,7},{6,4},{7,5},{8,10},{9,11},{10,... | collective-permute-start | bytes 884744 | tf_op jit(solution)/shard_map/ppermute | solution.py:515
  76.7 12.1 %collective-permute-start.16 = (f32[576,128]{1,0:T(8,128)S(1)}, f32[576,128]{1,0:T(8,128)S(1)}, u32[]{:S(2)}, u32[]{:S(2)}) collective-permute-start(f32[576,128]{1,0:T(8,128)S(1)} %get-tuple-element.39), channel_id=1, source_target_pairs={{0,1},{1,2},{2,3},{3,0},{4,5},{5,6},{6,7},{7,4},{8,9},{9,10},{10,1... | collective-permute-start | bytes 884744 | tf_op jit(solution)/shard_map/ppermute | solution.py:515
  77.5 15.1 %collective-permute-start.17 = (f32[576,128]{1,0:T(8,128)S(1)}, f32[576,128]{1,0:T(8,128)S(1)}, u32[]{:S(2)}, u32[]{:S(2)}) collective-permute-start(f32[576,128]{1,0:T(8,128)S(1)} %get-tuple-element.40), channel_id=1, source_target_pairs={{0,2},{1,3},{2,0},{3,1},{4,6},{5,7},{6,4},{7,5},{8,10},{9,11},{10,... | collective-permute-start | bytes 884744 | tf_op jit(solution)/shard_map/ppermute | solution.py:515
  79.9 13.9 %collective-permute-start.18 = (f32[576,128]{1,0:T(8,128)S(1)}, f32[576,128]{1,0:T(8,128)S(1)}, u32[]{:S(2)}, u32[]{:S(2)}) collective-permute-start(f32[576,128]{1,0:T(8,128)S(1)} %get-tuple-element.41), channel_id=1, source_target_pairs={{0,3},{1,0},{2,1},{3,2},{4,7},{5,4},{6,5},{7,6},{8,11},{9,8},{10,9... | collective-permute-start | bytes 884744 | tf_op jit(solution)/shard_map/ppermute | solution.py:515
  106.8 20.1 %collective-permute-start.19 = (f32[1152,128]{1,0:T(8,128)S(1)}, f32[1152,128]{1,0:T(8,128)S(1)}, u32[]{:S(2)}, u32[]{:S(2)}) collective-permute-start(f32[1152,128]{1,0:T(8,128)S(1)} %shard_map.105.refs_0_), channel_id=1, source_target_pairs={{0,4},{4,8},{8,12},{12,16},{16,20},{20,24},{24,28},{28,32},{32,36}... | collective-permute-start | bytes 1769480 | tf_op jit(solution)/shard_map/ppermute | solution.py:470
  116.0 11.6 %collective-permute-start.25 = (f32[1152,128]{1,0:T(8,128)S(1)}, f32[1152,128]{1,0:T(8,128)S(1)}, u32[]{:S(2)}, u32[]{:S(2)}) collective-permute-start(f32[1152,128]{1,0:T(8,128)S(1)} %shard_map.103.after.refs_0_), channel_id=1, source_target_pairs={{0,12},{4,24},{8,20},{12,0},{16,28},{20,8},{24,36},{28,16},{32,44}... | collective-permute-start | bytes 1769480 | tf_op jit(solution)/shard_map/ppermute | solution.py:529
  117.3 17.5 %collective-permute-start.20 = (f32[1152,128]{1,0:T(8,128)S(1)}, f32[1152,128]{1,0:T(8,128)S(1)}, u32[]{:S(2)}, u32[]{:S(2)}) collective-permute-start(f32[1152,128]{1,0:T(8,128)S(1)} %get-tuple-element.42.refs_1_), channel_id=1, source_target_pairs={{4,0},{8,4},{12,8},{5,1},{9,5},{13,9},{6,2},{10,6},{14,10},{7,3},{... | collective-permute-start | bytes 1769480 | tf_op jit(solution)/shard_map/ppermute | solution.py:524
  123.3 20.4 %copy-start.3 = (f32[40,8,512]{2,1,0:T(8,128)S(1)}, f32[40,8,512]{2,1,0:T(8,128)}, u32[]{:S(2)}) copy-start(f32[40,8,512]{2,1,0:T(8,128)} %param.13) | copy-start | bytes 1966084
  123.3 15.3 %collective-permute-start.24 = (f32[1152,128]{1,0:T(8,128)S(1)}, f32[1152,128]{1,0:T(8,128)S(1)}, u32[]{:S(2)}, u32[]{:S(2)}) collective-permute-start(f32[1152,128]{1,0:T(8,128)S(1)} %shard_map.106.refs_1_.refs_0_), channel_id=1, source_target_pairs={{0,8},{4,12},{8,16},{12,20},{16,24},{20,28},{24,32},{28,36},{32,40... | collective-permute-start | bytes 1769480 | tf_op jit(solution)/shard_map/ppermute | solution.py:470
  125.6 17.2 %collective-permute-start.27 = (f32[1152,128]{1,0:T(8,128)S(1)}, f32[1152,128]{1,0:T(8,128)S(1)}, u32[]{:S(2)}, u32[]{:S(2)}) collective-permute-start(f32[1152,128]{1,0:T(8,128)S(1)} %get-tuple-element.43.refs_2_), channel_id=1, source_target_pairs={{8,0},{12,4},{9,1},{13,5},{10,2},{14,6},{11,3},{15,7}} | collective-permute-start | bytes 1769480 | tf_op jit(solution)/shard_map/ppermute | solution.py:524
  126.9 18.0 %collective-permute-start.28 = (f32[1152,128]{1,0:T(8,128)S(1)}, f32[1152,128]{1,0:T(8,128)S(1)}, u32[]{:S(2)}, u32[]{:S(2)}) collective-permute-start(f32[1152,128]{1,0:T(8,128)S(1)} %get-tuple-element.44.refs_3_), channel_id=1, source_target_pairs={{12,0},{13,1},{14,2},{15,3}} | collective-permute-start | bytes 1769480 | tf_op jit(solution)/shard_map/ppermute | solution.py:524
  127.6 17.3 %collective-permute-start.26 = (f32[1152,128]{1,0:T(8,128)S(1)}, f32[1152,128]{1,0:T(8,128)S(1)}, u32[]{:S(2)}, u32[]{:S(2)}) collective-permute-start(f32[1152,128]{1,0:T(8,128)S(1)} %collective-permute-done.25.y_ref), channel_id=1, source_target_pairs={{24,16},{0,24},{8,32},{16,40},{56,48},{32,56},{40,64},{48,72},{88,... | collective-permute-start | bytes 1769480 | tf_op jit(solution)/shard_map/ppermute | solution.py:532
  137.0 16.1 %collective-permute-start.21 = (f32[576,128]{1,0:T(8,128)S(1)}, f32[576,128]{1,0:T(8,128)S(1)}, u32[]{:S(2)}, u32[]{:S(2)}) collective-permute-start(f32[576,128]{1,0:T(8,128)S(1)} %get-tuple-element.46), channel_id=1, source_target_pairs={{0,1},{1,2},{2,3},{3,0},{4,5},{5,6},{6,7},{7,4},{8,9},{9,10},{10,1... | collective-permute-start | bytes 884744 | tf_op jit(solution)/shard_map/ppermute | solution.py:515
  138.7 14.5 %collective-permute-start.22 = (f32[576,128]{1,0:T(8,128)S(1)}, f32[576,128]{1,0:T(8,128)S(1)}, u32[]{:S(2)}, u32[]{:S(2)}) collective-permute-start(f32[576,128]{1,0:T(8,128)S(1)} %get-tuple-element.47), channel_id=1, source_target_pairs={{0,2},{1,3},{2,0},{3,1},{4,6},{5,7},{6,4},{7,5},{8,10},{9,11},{10,... | collective-permute-start | bytes 884744 | tf_op jit(solution)/shard_map/ppermute | solution.py:515
  142.8 10.4 %collective-permute-start.23 = (f32[576,128]{1,0:T(8,128)S(1)}, f32[576,128]{1,0:T(8,128)S(1)}, u32[]{:S(2)}, u32[]{:S(2)}) collective-permute-start(f32[576,128]{1,0:T(8,128)S(1)} %get-tuple-element.48), channel_id=1, source_target_pairs={{0,3},{1,0},{2,1},{3,2},{4,7},{5,4},{6,5},{7,6},{8,11},{9,8},{10,9... | collective-permute-start | bytes 884744 | tf_op jit(solution)/shard_map/ppermute | solution.py:515
  145.9 12.6 %collective-permute-start.29 = (f32[576,128]{1,0:T(8,128)S(1)}, f32[576,128]{1,0:T(8,128)S(1)}, u32[]{:S(2)}, u32[]{:S(2)}) collective-permute-start(f32[576,128]{1,0:T(8,128)S(1)} %get-tuple-element.50), channel_id=1, source_target_pairs={{0,1},{1,2},{2,3},{3,0},{4,5},{5,6},{6,7},{7,4},{8,9},{9,10},{10,1... | collective-permute-start | bytes 884744 | tf_op jit(solution)/shard_map/ppermute | solution.py:515
  146.7 14.3 %collective-permute-start.30 = (f32[576,128]{1,0:T(8,128)S(1)}, f32[576,128]{1,0:T(8,128)S(1)}, u32[]{:S(2)}, u32[]{:S(2)}) collective-permute-start(f32[576,128]{1,0:T(8,128)S(1)} %get-tuple-element.51), channel_id=1, source_target_pairs={{0,2},{1,3},{2,0},{3,1},{4,6},{5,7},{6,4},{7,5},{8,10},{9,11},{10,... | collective-permute-start | bytes 884744 | tf_op jit(solution)/shard_map/ppermute | solution.py:515
  153.1 11.7 %collective-permute-start.31 = (f32[576,128]{1,0:T(8,128)S(1)}, f32[576,128]{1,0:T(8,128)S(1)}, u32[]{:S(2)}, u32[]{:S(2)}) collective-permute-start(f32[576,128]{1,0:T(8,128)S(1)} %get-tuple-element.52), channel_id=1, source_target_pairs={{0,3},{1,0},{2,1},{3,2},{4,7},{5,4},{6,5},{7,6},{8,11},{9,8},{10,9... | collective-permute-start | bytes 884744 | tf_op jit(solution)/shard_map/ppermute | solution.py:515
  170.5 15.2 %copy-start.4 = (f32[2,8,512]{2,1,0:T(8,128)S(1)}, f32[2,8,512]{2,1,0:T(8,128)}, u32[]{:S(2)}) copy-start(f32[2,8,512]{2,1,0:T(8,128)} %param.17) | copy-start | bytes 98308
  170.5 15.2 %copy-start.6 = (f32[8,512]{1,0:T(8,128)S(1)}, f32[8,512]{1,0:T(8,128)}, u32[]{:S(2)}) copy-start(f32[8,512]{1,0:T(8,128)} %lateral_ref.1) | copy-start | bytes 49156
  170.6 15.2 %collective-permute-start.32 = (f32[512,128]{1,0:T(8,128)S(1)}, f32[512,128]{1,0:T(8,128)S(1)}, u32[]{:S(2)}, u32[]{:S(2)}) collective-permute-start(f32[512,128]{1,0:T(8,128)S(1)} %get-tuple-element.56), channel_id=1, source_target_pairs={{0,1},{1,2},{2,3},{4,5},{5,6},{6,7},{8,9},{9,10},{10,11},{12,13},{... | collective-permute-start | bytes 786440 | tf_op jit(solution)/shard_map/ppermute | solution.py:470
  172.2 13.5 %collective-permute-start.33 = (f32[512,128]{1,0:T(8,128)S(1)}, f32[512,128]{1,0:T(8,128)S(1)}, u32[]{:S(2)}, u32[]{:S(2)}) collective-permute-start(f32[512,128]{1,0:T(8,128)S(1)} %get-tuple-element.55), channel_id=1, source_target_pairs={{1,0},{2,1},{3,2},{5,4},{6,5},{7,6},{9,8},{10,9},{11,10},{13,12},{... | collective-permute-start | bytes 786440 | tf_op jit(solution)/shard_map/ppermute | solution.py:470
  173.5 10.2 %collective-permute-start.34 = (f32[8,128]{1,0:T(8,128)S(1)}, f32[8,128]{1,0:T(8,128)S(1)}, u32[]{:S(2)}, u32[]{:S(2)}) collective-permute-start(f32[8,128]{1,0:T(8,128)S(1)} %bitcast.84), channel_id=1, source_target_pairs={{0,4},{4,8},{8,12},{12,16},{16,20},{20,24},{24,28},{28,32},{32,36}... | collective-permute-start | bytes 12296 | tf_op jit(solution)/shard_map/ppermute | solution.py:470
  180.8 4.9 %collective-permute-start.35 = (f32[8,128]{1,0:T(8,128)S(1)}, f32[8,128]{1,0:T(8,128)S(1)}, u32[]{:S(2)}, u32[]{:S(2)}) collective-permute-start(f32[8,128]{1,0:T(8,128)S(1)} %bitcast.83), channel_id=1, source_target_pairs={{4,0},{8,4},{12,8},{16,12},{20,16},{24,20},{28,24},{32,28},{36,32}... | collective-permute-start | bytes 12296 | tf_op jit(solution)/shard_map/ppermute | solution.py:470

commit v4 on v3

--- a/solution.py
+++ b/solution.py
@@ -286,7 +286,8 @@
     )
 
 
-def place_body(which, kinds, place_ref, own_any, cells_ref, x0, x1, x2, x3, weight_ref, out_ref, cells, own0, own1, sems):
+def place_body(which, kinds, place_ref, own_any, cells_ref, x0, x1, x2, x3, weight_ref, out_ref, *refs):
+    edges, (cells, own0, own1, sems) = refs[:-4], refs[-4:]
     loads = load_own(which, kinds, own_any, (own0, own1), sems)
     cells[...] = cells_ref[...]
     for i, load in enumerate(loads):
@@ -301,14 +302,35 @@
         return 0
 
     lax.fori_loop(0, CELLS // 256, mix, 0)
+    if not edges:
+        return
+
+    for even in (True, False):
+
+        @pl.when((place_ref[1] & 1 == 0) == even)
+        def _(even=even):
+            high, low = edges[:2] if even else edges[1::-1]
+            high[...] = out_ref[(ROWS - 1) * COLS :, :]
+            low[...] = out_ref[:COLS, :]
+
+        @pl.when((place_ref[0] & 1 == 0) == even)
+        def _(even=even):
+            high, low = edges[2:] if even else edges[:1:-1]
+            for row in range(ROWS):
+                high[row : row + 1, :] = out_ref[(row + 1) * COLS - 1 : (row + 1) * COLS, :]
+                low[row : row + 1, :] = out_ref[row * COLS : row * COLS + 1, :]
+
+
+EDGES = tuple(jax.ShapeDtypeStruct((n, WIDE), F32) for n in (COLS, COLS, ROWS, ROWS))
 
 
 def place(which, kinds, where, own, cells, xs, weight):
+    edges = EDGES if which == 1 else ()
     return kernel_call(
         functools.partial(place_body, which, kinds),
-        jax.ShapeDtypeStruct((CELLS, WIDE), F32),
+        (jax.ShapeDtypeStruct((CELLS, WIDE), F32), *edges),
         [SMEM, ANY] + [VMEM] * 6,
-        VMEM,
+        (VMEM,) * (1 + len(edges)),
         (where, own, cells, *xs, weight),
         scratch=[
             pltpu.VMEM((CELLS + 8, WIDE), F32),
@@ -368,29 +390,32 @@
 
 
 def solve_body(
-    place_ref, moved_ref, up_ref, down_ref, left_ref, right_ref, lateral_ref, mix_ref, inverse_ref, stress_ref, out_ref, edge
+    place_ref, moved_ref, even_row_ref, odd_row_ref, even_column_ref, odd_column_ref, lateral_ref, mix_ref, inverse_ref, stress_ref, out_ref, edge
 ):
     j = pl.program_id(0)
     sub, lane = iota((8, WIDE), 0), iota((8, WIDE), 1)
     size = LEVELS * 8
 
-    def spread(source_ref):
-        source = source_ref[...]
+    even_along, even_across = place_ref[0] & 1 == 0, place_ref[1] & 1 == 0
+
+    def spread(low):
+        source = jnp.where(even_along != low, even_column_ref[...], odd_column_ref[...])
         for level in range(LEVELS):
             edge[level * 8 : level * 8 + 8, :] = jnp.broadcast_to(source[:, level : level + 1], (8, WIDE))
 
     @pl.when(j == 0)
     def _():
-        spread(left_ref)
+        spread(True)
 
     @pl.when(j == CHUNKS - 1)
     def _():
-        spread(right_ref)
+        spread(False)
 
     start = pl.multiple_of(j * size, size)
     before = pl.multiple_of(jnp.maximum(j - 1, 0) * size, size)
     after = pl.multiple_of(jnp.minimum(j + 1, CHUNKS - 1) * size, size)
-    up, down = up_ref[...].T, down_ref[...].T
+    up = jnp.where(even_across, odd_row_ref[...], even_row_ref[...]).T
+    down = jnp.where(even_across, even_row_ref[...], odd_row_ref[...]).T
     lateral = lateral_ref[...]
     count = 4.0 - (
         ((place_ref[0] == 0) & (j == 0) & (lane == 0)).astype(F32)
@@ -430,7 +455,7 @@
             out_ref[rows, :] = value
 
 
-def solve(where, moved, up, down, left, right, lateral, mix, inverse, stress):
+def solve(where, moved, even_row, odd_row, even_column, odd_column, lateral, mix, inverse, stress):
     def chunk(rows):
         return pl.BlockSpec((rows, WIDE), lambda j: (0, j))
 
@@ -456,7 +481,7 @@
             chunk(16),
         ],
         chunk(LEVELS * 8),
-        (where, moved, up, down, left, right, lateral, mix, inverse, stress),
+        (where, moved, even_row, odd_row, even_column, odd_column, lateral, mix, inverse, stress),
         grid=(CHUNKS,),
         scratch=[pltpu.VMEM((LEVELS * 8, WIDE), F32)],
         limit=14,
@@ -549,15 +574,17 @@
         weight = cells_first(second_fraction.reshape(LAYERS * 8, COLS), 3, after)
         return weight.reshape(CELLS, WIDE), (weight,)
 
-    middle = fetch(0, table, first_weight)
-    moved = fetch(1, middle, second_weight).reshape(ROWS, COLS, WIDE)
-    up = move(moved[ROWS - 1], "across", 1)
-    down = move(moved[0], "across", -1)
-    left = move(moved[:, COLS - 1], "along", 1)
-    right = move(moved[:, 0], "along", -1)
-    result = solve(
-        where, layers_first(moved), up, down, left, right, lateral_mix, mix, inverse[0], surface_stress.reshape(16, COLS)
-    )
+    (middle,) = fetch(0, table, first_weight)
+    moved, *edges = fetch(1, middle, second_weight)
+    beside = []
+    for axis, pair in (("across", edges[:2]), ("along", edges[2:])):
+        for first, edge in enumerate(pair):
+            swaps = []
+            for i in range(first, lax.axis_size(axis) - 1, 2):
+                swaps += [(i, i + 1), (i + 1, i)]
+            beside.append(lax.ppermute(edge, axis, swaps))
+    moved = layers_first(moved.reshape(ROWS, COLS, WIDE))
+    result = solve(where, moved, *beside, lateral_mix, mix, inverse[0], surface_stress.reshape(16, COLS))
     return result.reshape(LAYERS, 3, ROWS, COLS)
 
 

time: 192 us -> 189 us (0.984)
  the two profiles are of different devices: /device:TPU:1 before, /device:TPU:40 now
where the time goes in v4:
time: 189 us; the launch traced here: 188 us
  starting transfers between devices  74 us (39%)
  Pallas kernels  62.4 us (33%)
  waiting for transfers between devices  47.7 us (25%)
  local copies, waits for them, and re-layouts  3.02 us (2%)
    pallas_call x23, Pallas kernels, kernel_call(): pl.pallas_call(body, out_shape=out_shapes, in_specs=in_specs, out_specs=o...  62.4 us
    ppermute x7, starting transfers between devices, move(): return lax.ppermute(x, axis, pairs)  18.9 us
    ppermute x12, starting transfers between devices, turn(): moved[step] = lax.ppermute(xs[step], 'across', pairs)  18.5 us
    ppermute x12, waiting for transfers between devices, turn(): moved[step] = lax.ppermute(xs[step], 'across', pairs)  17.7 us
    ppermute x6, starting transfers between devices, fetch(): behind[u] = lax.ppermute(answers[u - 1], 'along', pairs)  13.2 us
    ppermute x7, waiting for transfers between devices, move(): return lax.ppermute(x, axis, pairs)  12.7 us
    ppermute x4, starting transfers between devices, body(): beside.append(lax.ppermute(edge, axis, swaps))  7.6 us
    ppermute x2, waiting for transfers between devices, fetch(): x3 = lax.ppermute(p3, 'along', direct)  5.47 us
  transfers between devices with their start and end apart: 37, of which 18 were waited for; matrix products, arithmetic and copies ran while one was open for 0% of the time, Pallas kernels for 13%

profile of v4, /device:TPU:40, one launch (start us, length us, event | category | flops | bytes accessed | tf_op | source)
XLA Modules:
  0.0 187.8 jit_solution(2788373438772400224)
XLA Ops:
  1.5 3.5 %shard_map.91 = (s32[128,128]{1,0:T(8,128)}, s32[128,128]{1,0:T(8,128)S(1)}) custom-call(s32[2]{0:T(128)S(1)} %pad_add_fusion.along_ref.place_ref, s32[8,512]{1,0:T(8,128)S(1)} %copy-done.7, s32[8,512]{1,0:T(8,128)S(1)} %copy-done.8), custom_call_target="tpu_custom_call" | custom-call | flops 1048576 | bytes 2097152 | tf_op jit(solution)/shard_map/pallas_call | solution.py:33
  5.0 5.4 %all-to-all-start = ((s32[4,4,8,128]{3,2,1,0:T(8,128)}), s32[4,4,8,128]{3,2,1,0:T(8,128)S(1)}, u32[]{:S(2)}, u32[]{:S(2)}) async-start(s32[4,4,8,128]{3,2,1,0:T(8,128)} %bitcast.3), calls=%async_computation | async-start | bytes 131072 | tf_op jit(solution)/shard_map/all_to_all | solution.py:525
  10.4 4.2 %all-to-all-done = s32[4,4,8,128]{3,2,1,0:T(8,128)S(1)} async-done(((s32[4,4,8,128]{3,2,1,0:T(8,128)}), s32[4,4,8,128]{3,2,1,0:T(8,128)S(1)}, u32[]{:S(2)}, u32[]{:S(2)}) %all-to-all-start) | async-done | bytes 65568 | tf_op jit(solution)/shard_map/all_to_all | solution.py:525
  14.6 2.4 %collective-permute-start.2 = (s32[4,8,128]{2,1,0:T(8,128)S(1)}, s32[4,8,128]{2,1,0:T(8,128)S(1)}, u32[]{:S(2)}, u32[]{:S(2)}) collective-permute-start(s32[4,8,128]{2,1,0:T(8,128)S(1)} %get-tuple-element.66), channel_id=1, source_target_pairs={{8,0},{12,4},{16,8},{20,12},{24,16},{28,20},{32,24},{36,28},{40,32... | collective-permute-start | bytes 49160 | tf_op jit(solution)/shard_map/ppermute | solution.py:495
  16.9 1.9 %collective-permute-start.3 = (s32[4,8,128]{2,1,0:T(8,128)S(1)}, s32[4,8,128]{2,1,0:T(8,128)S(1)}, u32[]{:S(2)}, u32[]{:S(2)}) collective-permute-start(s32[4,8,128]{2,1,0:T(8,128)S(1)} %get-tuple-element.65), channel_id=1, source_target_pairs={{0,4},{4,8},{8,12},{1,5},{5,9},{9,13},{2,6},{6,10},{10,14},{3,7},{... | collective-permute-start | bytes 49160 | tf_op jit(solution)/shard_map/ppermute | solution.py:531
  20.8 3.6 %collective-permute-start = (s32[4,8,128]{2,1,0:T(8,128)S(1)}, s32[4,8,128]{2,1,0:T(8,128)S(1)}, u32[]{:S(2)}, u32[]{:S(2)}) collective-permute-start(s32[4,8,128]{2,1,0:T(8,128)S(1)} %get-tuple-element.68), channel_id=1, source_target_pairs={{4,0},{8,4},{12,8},{16,12},{20,16},{24,20},{28,24},{32,28},{36,32}... | collective-permute-start | bytes 49160 | tf_op jit(solution)/shard_map/ppermute | solution.py:495
  29.6 2.2 %shard_map.93.after.refs_0_ = f32[1152,128]{1,0:T(8,128)S(1)} custom-call(s32[2]{0:T(128)S(1)} %pad_add_fusion.along_ref.place_ref, s32[4096]{0:T(1024)S(1)} %bitcast.71, f32[4096,128]{1,0:T(8,128)S(1)} %bitcast.34, s32[4096]{0:T(1024)S(1)} %bitcast.67, s32[4096]{0:T(1024)S(1)} %bitcast.51, s32[4096]{0:T(1024)S(1)} %bitcast.72, s32[4096]{0:T(1024)S(1)} %bitcast.55, ...), custom_call_target="tpu_custom_call" | custom-call | flops 268435456 | bytes 2097152 | tf_op jit(solution)/shard_map/pallas_call | solution.py:33
  31.8 4.3 %shard_map.94 = (f32[1152,128]{1,0:T(8,128)S(1)}, f32[1152,128]{1,0:T(8,128)S(1)}, f32[1152,128]{1,0:T(8,128)S(1)}) custom-call(s32[2]{0:T(128)S(1)} %pad_add_fusion.along_ref.place_ref, s32[4096]{0:T(1024)S(1)} %bitcast.56, s32[4096]{0:T(1024)S(1)} %bitcast.60, s32[4096]{0:T(1024)S(1)} %bitcast.64, f32[4096,128]{1,0:T(8,128)S(1)} %bitcast.35, ...), custom_call_target="tpu_custom_call" | custom-call | flops 1048576 | bytes 2097152 | tf_op jit(solution)/shard_map/pallas_call | solution.py:33
  36.1 2.2 %shard_map.95.refs_0_ = f32[1152,128]{1,0:T(8,128)S(1)} custom-call(s32[2]{0:T(128)S(1)} %pad_add_fusion.along_ref.place_ref, s32[4096]{0:T(1024)S(1)} %bitcast.68, f32[4096,128]{1,0:T(8,128)S(1)} %bitcast.36, f32[1152,128]{1,0:T(8,128)S(1)} %shard_map.93.after.refs_0_, f32[1152,128]{1,0:T(8,128)S(1)} %get-tuple-element.36.refs_1_, ...), custom_call_target="tpu_custom_call" | custom-call | flops 268435456 | bytes 2097152 | tf_op jit(solution)/shard_map/pallas_call | solution.py:33
  38.3 4.1 %collective-permute-start.6 = (f32[1152,128]{1,0:T(8,128)S(1)}, f32[1152,128]{1,0:T(8,128)S(1)}, u32[]{:S(2)}, u32[]{:S(2)}) collective-permute-start(f32[1152,128]{1,0:T(8,128)S(1)} %shard_map.95.refs_0_), channel_id=1, source_target_pairs={{0,4},{4,8},{8,12},{12,16},{16,20},{20,24},{24,28},{28,32},{32,36}... | collective-permute-start | bytes 1769480 | tf_op jit(solution)/shard_map/ppermute | solution.py:495
  42.5 1.9 %collective-permute-start.12 = (f32[1152,128]{1,0:T(8,128)S(1)}, f32[1152,128]{1,0:T(8,128)S(1)}, u32[]{:S(2)}, u32[]{:S(2)}) collective-permute-start(f32[1152,128]{1,0:T(8,128)S(1)} %shard_map.93.after.refs_0_), channel_id=1, source_target_pairs={{0,12},{4,24},{8,20},{12,0},{16,28},{20,8},{24,36},{28,16},{32,44}... | collective-permute-start | bytes 1769480 | tf_op jit(solution)/shard_map/ppermute | solution.py:554
  44.4 1.9 %collective-permute-start.7 = (f32[1152,128]{1,0:T(8,128)S(1)}, f32[1152,128]{1,0:T(8,128)S(1)}, u32[]{:S(2)}, u32[]{:S(2)}) collective-permute-start(f32[1152,128]{1,0:T(8,128)S(1)} %get-tuple-element.36.refs_1_), channel_id=1, source_target_pairs={{4,0},{8,4},{12,8},{5,1},{9,5},{13,9},{6,2},{10,6},{14,10},{7,3},{... | collective-permute-start | bytes 1769480 | tf_op jit(solution)/shard_map/ppermute | solution.py:549
  46.3 2.2 %shard_map.96.refs_1_.refs_0_.after_ref = f32[1152,128]{1,0:T(8,128)S(1)} custom-call(s32[2]{0:T(128)S(1)} %pad_add_fusion.along_ref.place_ref, s32[4096]{0:T(1024)S(1)} %bitcast.52, f32[4096,128]{1,0:T(8,128)S(1)} %bitcast.37, f32[1152,128]{1,0:T(8,128)S(1)} %shard_map.95.refs_0_), custom_call_target="tpu_custom_call" | custom-call | flops 268435456 | bytes 2097152 | tf_op jit(solution)/shard_map/pallas_call | solution.py:33
  48.6 2.1 %collective-permute-start.11 = (f32[1152,128]{1,0:T(8,128)S(1)}, f32[1152,128]{1,0:T(8,128)S(1)}, u32[]{:S(2)}, u32[]{:S(2)}) collective-permute-start(f32[1152,128]{1,0:T(8,128)S(1)} %shard_map.96.refs_1_.refs_0_.after_ref), channel_id=1, source_target_pairs={{0,8},{4,12},{8,16},{12,20},{16,24},{20,28},{24,32},{28,36},{32,40... | collective-permute-start | bytes 1769480 | tf_op jit(solution)/shard_map/ppermute | solution.py:495
  50.7 4.0 %collective-permute-start.14 = (f32[1152,128]{1,0:T(8,128)S(1)}, f32[1152,128]{1,0:T(8,128)S(1)}, u32[]{:S(2)}, u32[]{:S(2)}) collective-permute-start(f32[1152,128]{1,0:T(8,128)S(1)} %get-tuple-element.37.refs_2_), channel_id=1, source_target_pairs={{8,0},{12,4},{9,1},{13,5},{10,2},{14,6},{11,3},{15,7}} | collective-permute-start | bytes 1769480 | tf_op jit(solution)/shard_map/ppermute | solution.py:549
  55.4 2.7 %collective-permute-done.12.y_ref = f32[1152,128]{1,0:T(8,128)S(1)} collective-permute-done((f32[1152,128]{1,0:T(8,128)S(1)}, f32[1152,128]{1,0:T(8,128)S(1)}, u32[]{:S(2)}, u32[]{:S(2)}) %collective-permute-start.12) | collective-permute-done | bytes 589856 | tf_op jit(solution)/shard_map/ppermute | solution.py:554
  59.9 2.2 %shard_map.97 = (f32[576,128]{1,0:T(8,128)S(1)}, f32[576,128]{1,0:T(8,128)S(1)}, f32[576,128]{1,0:T(8,128)S(1)}, f32[576,128]{1,0:T(8,128)S(1)}) custom-call(s32[2]{0:T(128)S(1)} %pad_add_fusion.along_ref.place_ref, s32[4096]{0:T(1024)S(1)} %get-tuple-element.69.wanted_ref, f32[4096,128]{1,0:T(8,128)S(1)} %bitcast.38, ...), custom_call_target="tpu_custom_call" | custom-call | flops 268435456 | bytes 2097152 | tf_op jit(solution)/shard_map/pallas_call | solution.py:33
  63.7 4.8 %collective-permute-done.11.x_ref = f32[1152,128]{1,0:T(8,128)S(1)} collective-permute-done((f32[1152,128]{1,0:T(8,128)S(1)}, f32[1152,128]{1,0:T(8,128)S(1)}, u32[]{:S(2)}, u32[]{:S(2)}) %collective-permute-start.11) | collective-permute-done | bytes 589856 | tf_op jit(solution)/shard_map/ppermute | solution.py:495
  68.9 3.7 %collective-permute-done.14.b2 = f32[1152,128]{1,0:T(8,128)S(1)} collective-permute-done((f32[1152,128]{1,0:T(8,128)S(1)}, f32[1152,128]{1,0:T(8,128)S(1)}, u32[]{:S(2)}, u32[]{:S(2)}) %collective-permute-start.14) | collective-permute-done | bytes 589856 | tf_op jit(solution)/shard_map/ppermute | solution.py:549
  75.2 1.7 shard_map.100.refs_2_.inverse_ref
  82.6 3.9 %shard_map.98.cells_ref = f32[4104,128]{1,0:T(8,128)S(1)} custom-call(s32[2]{0:T(128)S(1)} %pad_add_fusion.along_ref.place_ref, s32[16384]{0:T(1024)S(1)} %bitcast.45, f32[576,128]{1,0:T(8,128)S(1)} %get-tuple-element.39.x0.refs_0_, f32[576,128]{1,0:T(8,128)S(1)} %collective-permute-done.8.x1, f32[576,128]{1,0:T(8,128)S(1)} %collective-permute-done.9.x2, ...), custom_call_target="tpu_custom_call" | custom-call | flops 268435456 | bytes 2097152 | tf_op jit(solution)/shard_map/pallas_call | solution.py:33
  86.5 3.4 %collective-permute-done.16.x1 = f32[576,128]{1,0:T(8,128)S(1)} collective-permute-done((f32[576,128]{1,0:T(8,128)S(1)}, f32[576,128]{1,0:T(8,128)S(1)}, u32[]{:S(2)}, u32[]{:S(2)}) %collective-permute-start.16) | collective-permute-done | bytes 294944 | tf_op jit(solution)/shard_map/ppermute | solution.py:540
  90.7 3.4 %collective-permute-done.18.x3 = f32[576,128]{1,0:T(8,128)S(1)} collective-permute-done((f32[576,128]{1,0:T(8,128)S(1)}, f32[576,128]{1,0:T(8,128)S(1)}, u32[]{:S(2)}, u32[]{:S(2)}) %collective-permute-start.18) | collective-permute-done | bytes 294944 | tf_op jit(solution)/shard_map/ppermute | solution.py:540
  94.1 5.6 %shard_map.102.table_ref.table = f32[4096,128]{1,0:T(8,128)S(1)} custom-call(s32[2]{0:T(128)S(1)} %pad_add_fusion.along_ref.place_ref, s32[16384]{0:T(1024)S(1)} %bitcast.46, f32[4104,128]{1,0:T(8,128)S(1)} %shard_map.98.cells_ref, f32[576,128]{1,0:T(8,128)S(1)} %get-tuple-element.43.x0, f32[576,128]{1,0:T(8,128)S(1)} %collective-permute-done.16.x1, ...), custom_call_target="tpu_custom_call" | custom-call | flops 268435456 | bytes 2097152 | tf_op jit(solution)/shard_map/pallas_call | solution.py:33
  99.7 2.2 %shard_map.103.after.refs_0_ = f32[1152,128]{1,0:T(8,128)S(1)} custom-call(s32[2]{0:T(128)S(1)} %pad_add_fusion.along_ref.place_ref, s32[4096]{0:T(1024)S(1)} %bitcast.73, f32[4096,128]{1,0:T(8,128)S(1)} %shard_map.102.table_ref.table, s32[4096]{0:T(1024)S(1)} %bitcast.69, s32[4096]{0:T(1024)S(1)} %bitcast.53, s32[4096]{0:T(1024)S(1)} %bitcast.74, ...), custom_call_target="tpu_custom_call" | custom-call | flops 268435456 | bytes 2097152 | tf_op jit(solution)/shard_map/pallas_call | solution.py:33
  102.0 4.3 %shard_map.104 = (f32[1152,128]{1,0:T(8,128)S(1)}, f32[1152,128]{1,0:T(8,128)S(1)}, f32[1152,128]{1,0:T(8,128)S(1)}) custom-call(s32[2]{0:T(128)S(1)} %pad_add_fusion.along_ref.place_ref, s32[4096]{0:T(1024)S(1)} %bitcast.58, s32[4096]{0:T(1024)S(1)} %bitcast.62, s32[4096]{0:T(1024)S(1)} %bitcast.66, f32[4096,128]{1,0:T(8,128)S(1)} %shard_map.102.table_ref.table, ...), custom_call_target="tpu_custom_call" | custom-call | flops 1048576 | bytes 2097152 | tf_op jit(solution)/shard_map/pallas_call | solution.py:33
  106.3 2.2 %shard_map.105.refs_0_ = f32[1152,128]{1,0:T(8,128)S(1)} custom-call(s32[2]{0:T(128)S(1)} %pad_add_fusion.along_ref.place_ref, s32[4096]{0:T(1024)S(1)} %bitcast.70, f32[4096,128]{1,0:T(8,128)S(1)} %shard_map.102.table_ref.table, f32[1152,128]{1,0:T(8,128)S(1)} %shard_map.103.after.refs_0_, f32[1152,128]{1,0:T(8,128)S(1)} %get-tuple-element.47.refs_1_, ...), custom_call_target="tpu_custom_call" | custom-call | flops 268435456 | bytes 2097152 | tf_op jit(solution)/shard_map/pallas_call | solution.py:33
  108.5 3.4 %collective-permute-start.19 = (f32[1152,128]{1,0:T(8,128)S(1)}, f32[1152,128]{1,0:T(8,128)S(1)}, u32[]{:S(2)}, u32[]{:S(2)}) collective-permute-start(f32[1152,128]{1,0:T(8,128)S(1)} %shard_map.105.refs_0_), channel_id=1, source_target_pairs={{0,4},{4,8},{8,12},{12,16},{16,20},{20,24},{24,28},{28,32},{32,36}... | collective-permute-start | bytes 1769480 | tf_op jit(solution)/shard_map/ppermute | solution.py:495
  111.9 1.9 %collective-permute-start.25 = (f32[1152,128]{1,0:T(8,128)S(1)}, f32[1152,128]{1,0:T(8,128)S(1)}, u32[]{:S(2)}, u32[]{:S(2)}) collective-permute-start(f32[1152,128]{1,0:T(8,128)S(1)} %shard_map.103.after.refs_0_), channel_id=1, source_target_pairs={{0,12},{4,24},{8,20},{12,0},{16,28},{20,8},{24,36},{28,16},{32,44}... | collective-permute-start | bytes 1769480 | tf_op jit(solution)/shard_map/ppermute | solution.py:554
  113.8 1.9 %collective-permute-start.20 = (f32[1152,128]{1,0:T(8,128)S(1)}, f32[1152,128]{1,0:T(8,128)S(1)}, u32[]{:S(2)}, u32[]{:S(2)}) collective-permute-start(f32[1152,128]{1,0:T(8,128)S(1)} %get-tuple-element.47.refs_1_), channel_id=1, source_target_pairs={{4,0},{8,4},{12,8},{5,1},{9,5},{13,9},{6,2},{10,6},{14,10},{7,3},{... | collective-permute-start | bytes 1769480 | tf_op jit(solution)/shard_map/ppermute | solution.py:549
  115.8 2.2 %shard_map.106.refs_1_.refs_0_ = f32[1152,128]{1,0:T(8,128)S(1)} custom-call(s32[2]{0:T(128)S(1)} %pad_add_fusion.along_ref.place_ref, s32[4096]{0:T(1024)S(1)} %bitcast.54, f32[4096,128]{1,0:T(8,128)S(1)} %shard_map.102.table_ref.table, f32[1152,128]{1,0:T(8,128)S(1)} %shard_map.105.refs_0_), custom_call_target="tpu_custom_call" | custom-call | flops 268435456 | bytes 2097152 | tf_op jit(solution)/shard_map/pallas_call | solution.py:33
  118.0 2.1 %collective-permute-start.24 = (f32[1152,128]{1,0:T(8,128)S(1)}, f32[1152,128]{1,0:T(8,128)S(1)}, u32[]{:S(2)}, u32[]{:S(2)}) collective-permute-start(f32[1152,128]{1,0:T(8,128)S(1)} %shard_map.106.refs_1_.refs_0_), channel_id=1, source_target_pairs={{0,8},{4,12},{8,16},{12,20},{16,24},{20,28},{24,32},{28,36},{32,40... | collective-permute-start | bytes 1769480 | tf_op jit(solution)/shard_map/ppermute | solution.py:495
  120.1 4.0 %collective-permute-start.27 = (f32[1152,128]{1,0:T(8,128)S(1)}, f32[1152,128]{1,0:T(8,128)S(1)}, u32[]{:S(2)}, u32[]{:S(2)}) collective-permute-start(f32[1152,128]{1,0:T(8,128)S(1)} %get-tuple-element.48.refs_2_), channel_id=1, source_target_pairs={{8,0},{12,4},{9,1},{13,5},{10,2},{14,6},{11,3},{15,7}} | collective-permute-start | bytes 1769480 | tf_op jit(solution)/shard_map/ppermute | solution.py:549
  124.8 2.7 %collective-permute-done.25.y_ref = f32[1152,128]{1,0:T(8,128)S(1)} collective-permute-done((f32[1152,128]{1,0:T(8,128)S(1)}, f32[1152,128]{1,0:T(8,128)S(1)}, u32[]{:S(2)}, u32[]{:S(2)}) %collective-permute-start.25) | collective-permute-done | bytes 589856 | tf_op jit(solution)/shard_map/ppermute | solution.py:554
  129.3 2.2 %shard_map.107 = (f32[576,128]{1,0:T(8,128)S(1)}, f32[576,128]{1,0:T(8,128)S(1)}, f32[576,128]{1,0:T(8,128)S(1)}, f32[576,128]{1,0:T(8,128)S(1)}) custom-call(s32[2]{0:T(128)S(1)} %pad_add_fusion.along_ref.place_ref, s32[4096]{0:T(1024)S(1)} %get-tuple-element.69.wanted_ref, f32[4096,128]{1,0:T(8,128)S(1)} %shard_map.102.table_ref.table, ...), custom_call_target="tpu_custom_call" | custom-call | flops 268435456 | bytes 2097152 | tf_op jit(solution)/shard_map/pallas_call | solution.py:33
  131.6 7.1 %collective-permute-done.24.x_ref = f32[1152,128]{1,0:T(8,128)S(1)} collective-permute-done((f32[1152,128]{1,0:T(8,128)S(1)}, f32[1152,128]{1,0:T(8,128)S(1)}, u32[]{:S(2)}, u32[]{:S(2)}) %collective-permute-start.24) | collective-permute-done | bytes 589856 | tf_op jit(solution)/shard_map/ppermute | solution.py:495
  138.7 3.0 %collective-permute-start.22 = (f32[576,128]{1,0:T(8,128)S(1)}, f32[576,128]{1,0:T(8,128)S(1)}, u32[]{:S(2)}, u32[]{:S(2)}) collective-permute-start(f32[576,128]{1,0:T(8,128)S(1)} %get-tuple-element.52), channel_id=1, source_target_pairs={{0,2},{1,3},{2,0},{3,1},{4,6},{5,7},{6,4},{7,5},{8,10},{9,11},{10,... | collective-permute-start | bytes 884744 | tf_op jit(solution)/shard_map/ppermute | solution.py:540
  141.9 2.8 %collective-permute-start.23 = (f32[576,128]{1,0:T(8,128)S(1)}, f32[576,128]{1,0:T(8,128)S(1)}, u32[]{:S(2)}, u32[]{:S(2)}) collective-permute-start(f32[576,128]{1,0:T(8,128)S(1)} %get-tuple-element.53), channel_id=1, source_target_pairs={{0,3},{1,0},{2,1},{3,2},{4,7},{5,4},{6,5},{7,6},{8,11},{9,8},{10,9... | collective-permute-start | bytes 884744 | tf_op jit(solution)/shard_map/ppermute | solution.py:540
  147.0 3.2 %collective-permute-start.30 = (f32[576,128]{1,0:T(8,128)S(1)}, f32[576,128]{1,0:T(8,128)S(1)}, u32[]{:S(2)}, u32[]{:S(2)}) collective-permute-start(f32[576,128]{1,0:T(8,128)S(1)} %get-tuple-element.56), channel_id=1, source_target_pairs={{0,2},{1,3},{2,0},{3,1},{4,6},{5,7},{6,4},{7,5},{8,10},{9,11},{10,... | collective-permute-start | bytes 884744 | tf_op jit(solution)/shard_map/ppermute | solution.py:540
  151.3 1.7 collective-permute-done.23.x3
  153.1 3.9 %shard_map.108.cells_ref = f32[4104,128]{1,0:T(8,128)S(1)} custom-call(s32[2]{0:T(128)S(1)} %pad_add_fusion.along_ref.place_ref, s32[16384]{0:T(1024)S(1)} %bitcast.47, f32[576,128]{1,0:T(8,128)S(1)} %get-tuple-element.50.x0.refs_0_, f32[576,128]{1,0:T(8,128)S(1)} %collective-permute-done.21.x1, f32[576,128]{1,0:T(8,128)S(1)} %collective-permute-done.22.x2, ...), custom_call_target="tpu_custom_call" | custom-call | flops 268435456 | bytes 2097152 | tf_op jit(solution)/shard_map/pallas_call | solution.py:33
  157.0 2.5 %collective-permute-done.30.x2 = f32[576,128]{1,0:T(8,128)S(1)} collective-permute-done((f32[576,128]{1,0:T(8,128)S(1)}, f32[576,128]{1,0:T(8,128)S(1)}, u32[]{:S(2)}, u32[]{:S(2)}) %collective-permute-start.30) | collective-permute-done | bytes 294944 | tf_op jit(solution)/shard_map/ppermute | solution.py:540
  159.5 5.8 %collective-permute-done.31.x3 = f32[576,128]{1,0:T(8,128)S(1)} collective-permute-done((f32[576,128]{1,0:T(8,128)S(1)}, f32[576,128]{1,0:T(8,128)S(1)}, u32[]{:S(2)}, u32[]{:S(2)}) %collective-permute-start.31) | collective-permute-done | bytes 294944 | tf_op jit(solution)/shard_map/ppermute | solution.py:540
  165.3 5.7 %shard_map.111 = (f32[4096,128]{1,0:T(8,128)S(1)}, f32[512,128]{1,0:T(8,128)S(1)}, f32[512,128]{1,0:T(8,128)S(1)}, f32[8,128]{1,0:T(8,128)S(1)}, f32[8,128]{1,0:T(8,128)S(1)}) custom-call(s32[2]{0:T(128)S(1)} %pad_add_fusion.along_ref.place_ref, s32[16384]{0:T(1024)S(1)} %bitcast.48, f32[4104,128]{1,0:T(8,128)S(1)} %shard_map.108.cells_ref, ...), custom_call_target="tpu_custom_call" | custom-call | flops 268435456 | bytes 2097152 | tf_op jit(solution)/shard_map/pallas_call | solution.py:33
  172.4 3.9 %collective-permute-start.33 = (f32[512,128]{1,0:T(8,128)S(1)}, f32[512,128]{1,0:T(8,128)S(1)}, u32[]{:S(2)}, u32[]{:S(2)}) collective-permute-start(f32[512,128]{1,0:T(8,128)S(1)} %get-tuple-element.60), channel_id=1, source_target_pairs={{1,2},{2,1},{5,6},{6,5},{9,10},{10,9},{13,14},{14,13},{17,18},{18,... | collective-permute-start | bytes 786440 | tf_op jit(solution)/shard_map/ppermute | solution.py:585
  176.4 2.2 %collective-permute-start.35 = (f32[8,128]{1,0:T(8,128)S(1)}, f32[8,128]{1,0:T(8,128)S(1)}, u32[]{:S(2)}, u32[]{:S(2)}) collective-permute-start(f32[8,128]{1,0:T(8,128)S(1)} %get-tuple-element.62), channel_id=1, source_target_pairs={{4,8},{8,4},{12,16},{16,12},{20,24},{24,20},{28,32},{32,28},{36,40... | collective-permute-start | bytes 12296 | tf_op jit(solution)/shard_map/ppermute | solution.py:585
  179.7 1.7 collective-permute-done.35.odd_column_ref
  182.4 5.4 %shard_map.113 = f32[960,512]{1,0:T(8,128)} custom-call(s32[2]{0:T(128)S(1)} %pad_add_fusion.along_ref.place_ref, f32[3840,128]{1,0:T(8,128)S(1)} %shard_map.112.moved_ref, f32[512,128]{1,0:T(8,128)S(1)} %collective-permute-done.32.even_row_ref, f32[512,128]{1,0:T(8,128)S(1)} %collective-permute-done.33.odd_row_ref, ...), custom_call_target="tpu_custom_call" | custom-call | flops 1048576 | bytes 2097152 | tf_op jit(solution)/shard_map/pallas_call | solution.py:33
  (69 shorter events, 31.6 us)
Async XLA Ops:
  0.1 0.7 copy-start.7
  0.8 0.7 copy-start.8
  5.0 9.6 %all-to-all-start = ((s32[4,4,8,128]{3,2,1,0:T(8,128)}), s32[4,4,8,128]{3,2,1,0:T(8,128)S(1)}, u32[]{:S(2)}, u32[]{:S(2)}) async-start(s32[4,4,8,128]{3,2,1,0:T(8,128)} %bitcast.3), calls=%async_computation | async-start | bytes 131072 | tf_op jit(solution)/shard_map/all_to_all | solution.py:525
  14.6 9.9 %collective-permute-start.2 = (s32[4,8,128]{2,1,0:T(8,128)S(1)}, s32[4,8,128]{2,1,0:T(8,128)S(1)}, u32[]{:S(2)}, u32[]{:S(2)}) collective-permute-start(s32[4,8,128]{2,1,0:T(8,128)S(1)} %get-tuple-element.66), channel_id=1, source_target_pairs={{8,0},{12,4},{16,8},{20,12},{24,16},{28,20},{32,24},{36,28},{40,32... | collective-permute-start | bytes 49160 | tf_op jit(solution)/shard_map/ppermute | solution.py:495
  16.9 11.7 %collective-permute-start.3 = (s32[4,8,128]{2,1,0:T(8,128)S(1)}, s32[4,8,128]{2,1,0:T(8,128)S(1)}, u32[]{:S(2)}, u32[]{:S(2)}) collective-permute-start(s32[4,8,128]{2,1,0:T(8,128)S(1)} %get-tuple-element.65), channel_id=1, source_target_pairs={{0,4},{4,8},{8,12},{1,5},{5,9},{9,13},{2,6},{6,10},{10,14},{3,7},{... | collective-permute-start | bytes 49160 | tf_op jit(solution)/shard_map/ppermute | solution.py:531
  18.9 9.8 %collective-permute-start.4 = (s32[4,8,128]{2,1,0:T(8,128)S(1)}, s32[4,8,128]{2,1,0:T(8,128)S(1)}, u32[]{:S(2)}, u32[]{:S(2)}) collective-permute-start(s32[4,8,128]{2,1,0:T(8,128)S(1)} %get-tuple-element.64), channel_id=1, source_target_pairs={{0,8},{4,12},{1,9},{5,13},{2,10},{6,14},{3,11},{7,15}} | collective-permute-start | bytes 49160 | tf_op jit(solution)/shard_map/ppermute | solution.py:531
  20.2 8.5 %collective-permute-start.5 = (s32[4,8,128]{2,1,0:T(8,128)S(1)}, s32[4,8,128]{2,1,0:T(8,128)S(1)}, u32[]{:S(2)}, u32[]{:S(2)}) collective-permute-start(s32[4,8,128]{2,1,0:T(8,128)S(1)} %get-tuple-element.63), channel_id=1, source_target_pairs={{0,12},{1,13},{2,14},{3,15}} | collective-permute-start | bytes 49160 | tf_op jit(solution)/shard_map/ppermute | solution.py:531
  20.8 7.8 %collective-permute-start = (s32[4,8,128]{2,1,0:T(8,128)S(1)}, s32[4,8,128]{2,1,0:T(8,128)S(1)}, u32[]{:S(2)}, u32[]{:S(2)}) collective-permute-start(s32[4,8,128]{2,1,0:T(8,128)S(1)} %get-tuple-element.68), channel_id=1, source_target_pairs={{4,0},{8,4},{12,8},{16,12},{20,16},{24,20},{28,24},{32,28},{36,32}... | collective-permute-start | bytes 49160 | tf_op jit(solution)/shard_map/ppermute | solution.py:495
  24.5 5.1 %collective-permute-start.1 = (s32[4,8,128]{2,1,0:T(8,128)S(1)}, s32[4,8,128]{2,1,0:T(8,128)S(1)}, u32[]{:S(2)}, u32[]{:S(2)}) collective-permute-start(s32[4,8,128]{2,1,0:T(8,128)S(1)} %get-tuple-element.67), channel_id=1, source_target_pairs={{12,0},{16,4},{20,8},{24,12},{28,16},{32,20},{36,24},{40,28},{44,3... | collective-permute-start | bytes 49160 | tf_op jit(solution)/shard_map/ppermute | solution.py:495
  25.8 1.5 copy-start.1
  38.3 16.3 %collective-permute-start.6 = (f32[1152,128]{1,0:T(8,128)S(1)}, f32[1152,128]{1,0:T(8,128)S(1)}, u32[]{:S(2)}, u32[]{:S(2)}) collective-permute-start(f32[1152,128]{1,0:T(8,128)S(1)} %shard_map.95.refs_0_), channel_id=1, source_target_pairs={{0,4},{4,8},{8,12},{12,16},{16,20},{20,24},{24,28},{28,32},{32,36}... | collective-permute-start | bytes 1769480 | tf_op jit(solution)/shard_map/ppermute | solution.py:495
  42.5 15.6 %collective-permute-start.12 = (f32[1152,128]{1,0:T(8,128)S(1)}, f32[1152,128]{1,0:T(8,128)S(1)}, u32[]{:S(2)}, u32[]{:S(2)}) collective-permute-start(f32[1152,128]{1,0:T(8,128)S(1)} %shard_map.93.after.refs_0_), channel_id=1, source_target_pairs={{0,12},{4,24},{8,20},{12,0},{16,28},{20,8},{24,36},{28,16},{32,44}... | collective-permute-start | bytes 1769480 | tf_op jit(solution)/shard_map/ppermute | solution.py:554
  44.4 15.5 %collective-permute-start.7 = (f32[1152,128]{1,0:T(8,128)S(1)}, f32[1152,128]{1,0:T(8,128)S(1)}, u32[]{:S(2)}, u32[]{:S(2)}) collective-permute-start(f32[1152,128]{1,0:T(8,128)S(1)} %get-tuple-element.36.refs_1_), channel_id=1, source_target_pairs={{4,0},{8,4},{12,8},{5,1},{9,5},{13,9},{6,2},{10,6},{14,10},{7,3},{... | collective-permute-start | bytes 1769480 | tf_op jit(solution)/shard_map/ppermute | solution.py:549
  48.6 25.4 %copy-start.2 = (f32[40,8,512]{2,1,0:T(8,128)S(1)}, f32[40,8,512]{2,1,0:T(8,128)}, u32[]{:S(2)}) copy-start(f32[40,8,512]{2,1,0:T(8,128)} %param.11) | copy-start | bytes 1966084
  48.6 19.9 %collective-permute-start.11 = (f32[1152,128]{1,0:T(8,128)S(1)}, f32[1152,128]{1,0:T(8,128)S(1)}, u32[]{:S(2)}, u32[]{:S(2)}) collective-permute-start(f32[1152,128]{1,0:T(8,128)S(1)} %shard_map.96.refs_1_.refs_0_.after_ref), channel_id=1, source_target_pairs={{0,8},{4,12},{8,16},{12,20},{16,24},{20,28},{24,32},{28,36},{32,40... | collective-permute-start | bytes 1769480 | tf_op jit(solution)/shard_map/ppermute | solution.py:495
  50.7 21.9 %collective-permute-start.14 = (f32[1152,128]{1,0:T(8,128)S(1)}, f32[1152,128]{1,0:T(8,128)S(1)}, u32[]{:S(2)}, u32[]{:S(2)}) collective-permute-start(f32[1152,128]{1,0:T(8,128)S(1)} %get-tuple-element.37.refs_2_), channel_id=1, source_target_pairs={{8,0},{12,4},{9,1},{13,5},{10,2},{14,6},{11,3},{15,7}} | collective-permute-start | bytes 1769480 | tf_op jit(solution)/shard_map/ppermute | solution.py:549
  54.7 22.2 %collective-permute-start.15 = (f32[1152,128]{1,0:T(8,128)S(1)}, f32[1152,128]{1,0:T(8,128)S(1)}, u32[]{:S(2)}, u32[]{:S(2)}) collective-permute-start(f32[1152,128]{1,0:T(8,128)S(1)} %get-tuple-element.38.refs_3_), channel_id=1, source_target_pairs={{12,0},{13,1},{14,2},{15,3}} | collective-permute-start | bytes 1769480 | tf_op jit(solution)/shard_map/ppermute | solution.py:549
  58.1 18.8 %collective-permute-start.13 = (f32[1152,128]{1,0:T(8,128)S(1)}, f32[1152,128]{1,0:T(8,128)S(1)}, u32[]{:S(2)}, u32[]{:S(2)}) collective-permute-start(f32[1152,128]{1,0:T(8,128)S(1)} %collective-permute-done.12.y_ref), channel_id=1, source_target_pairs={{24,16},{0,24},{8,32},{16,40},{56,48},{32,56},{40,64},{48,72},{88,... | collective-permute-start | bytes 1769480 | tf_op jit(solution)/shard_map/ppermute | solution.py:557
  62.1 13.0 %copy-start = (f32[2,39,8,512]{3,2,1,0:T(8,128)S(1)}, f32[2,39,8,512]{3,2,1,0:T(8,128)}, u32[]{:S(2)}) copy-start(f32[2,39,8,512]{3,2,1,0:T(8,128)} %param.15) | copy-start | bytes 3833860
  62.1 13.0 %copy-start.5 = (f32[8,512]{1,0:T(8,128)S(1)}, f32[8,512]{1,0:T(8,128)}, u32[]{:S(2)}) copy-start(f32[8,512]{1,0:T(8,128)} %drag_ref.1) | copy-start | bytes 49156
  62.2 18.8 %collective-permute-start.10 = (f32[576,128]{1,0:T(8,128)S(1)}, f32[576,128]{1,0:T(8,128)S(1)}, u32[]{:S(2)}, u32[]{:S(2)}) collective-permute-start(f32[576,128]{1,0:T(8,128)S(1)} %get-tuple-element.42), channel_id=1, source_target_pairs={{0,3},{1,0},{2,1},{3,2},{4,7},{5,4},{6,5},{7,6},{8,11},{9,8},{10,9... | collective-permute-start | bytes 884744 | tf_op jit(solution)/shard_map/ppermute | solution.py:540
  68.5 14.1 %collective-permute-start.8 = (f32[576,128]{1,0:T(8,128)S(1)}, f32[576,128]{1,0:T(8,128)S(1)}, u32[]{:S(2)}, u32[]{:S(2)}) collective-permute-start(f32[576,128]{1,0:T(8,128)S(1)} %get-tuple-element.40), channel_id=1, source_target_pairs={{0,1},{1,2},{2,3},{3,0},{4,5},{5,6},{6,7},{7,4},{8,9},{9,10},{10,1... | collective-permute-start | bytes 884744 | tf_op jit(solution)/shard_map/ppermute | solution.py:540
  72.5 10.0 %collective-permute-start.9 = (f32[576,128]{1,0:T(8,128)S(1)}, f32[576,128]{1,0:T(8,128)S(1)}, u32[]{:S(2)}, u32[]{:S(2)}) collective-permute-start(f32[576,128]{1,0:T(8,128)S(1)} %get-tuple-element.41), channel_id=1, source_target_pairs={{0,2},{1,3},{2,0},{3,1},{4,6},{5,7},{6,4},{7,5},{8,10},{9,11},{10,... | collective-permute-start | bytes 884744 | tf_op jit(solution)/shard_map/ppermute | solution.py:540
  77.8 12.2 %collective-permute-start.16 = (f32[576,128]{1,0:T(8,128)S(1)}, f32[576,128]{1,0:T(8,128)S(1)}, u32[]{:S(2)}, u32[]{:S(2)}) collective-permute-start(f32[576,128]{1,0:T(8,128)S(1)} %get-tuple-element.44), channel_id=1, source_target_pairs={{0,1},{1,2},{2,3},{3,0},{4,5},{5,6},{6,7},{7,4},{8,9},{9,10},{10,1... | collective-permute-start | bytes 884744 | tf_op jit(solution)/shard_map/ppermute | solution.py:540
  79.3 11.4 %collective-permute-start.17 = (f32[576,128]{1,0:T(8,128)S(1)}, f32[576,128]{1,0:T(8,128)S(1)}, u32[]{:S(2)}, u32[]{:S(2)}) collective-permute-start(f32[576,128]{1,0:T(8,128)S(1)} %get-tuple-element.45), channel_id=1, source_target_pairs={{0,2},{1,3},{2,0},{3,1},{4,6},{5,7},{6,4},{7,5},{8,10},{9,11},{10,... | collective-permute-start | bytes 884744 | tf_op jit(solution)/shard_map/ppermute | solution.py:540
  80.9 13.2 %collective-permute-start.18 = (f32[576,128]{1,0:T(8,128)S(1)}, f32[576,128]{1,0:T(8,128)S(1)}, u32[]{:S(2)}, u32[]{:S(2)}) collective-permute-start(f32[576,128]{1,0:T(8,128)S(1)} %get-tuple-element.46), channel_id=1, source_target_pairs={{0,3},{1,0},{2,1},{3,2},{4,7},{5,4},{6,5},{7,6},{8,11},{9,8},{10,9... | collective-permute-start | bytes 884744 | tf_op jit(solution)/shard_map/ppermute | solution.py:540
  108.5 15.6 %collective-permute-start.19 = (f32[1152,128]{1,0:T(8,128)S(1)}, f32[1152,128]{1,0:T(8,128)S(1)}, u32[]{:S(2)}, u32[]{:S(2)}) collective-permute-start(f32[1152,128]{1,0:T(8,128)S(1)} %shard_map.105.refs_0_), channel_id=1, source_target_pairs={{0,4},{4,8},{8,12},{12,16},{16,20},{20,24},{24,28},{28,32},{32,36}... | collective-permute-start | bytes 1769480 | tf_op jit(solution)/shard_map/ppermute | solution.py:495
  111.9 15.6 %collective-permute-start.25 = (f32[1152,128]{1,0:T(8,128)S(1)}, f32[1152,128]{1,0:T(8,128)S(1)}, u32[]{:S(2)}, u32[]{:S(2)}) collective-permute-start(f32[1152,128]{1,0:T(8,128)S(1)} %shard_map.103.after.refs_0_), channel_id=1, source_target_pairs={{0,12},{4,24},{8,20},{12,0},{16,28},{20,8},{24,36},{28,16},{32,44}... | collective-permute-start | bytes 1769480 | tf_op jit(solution)/shard_map/ppermute | solution.py:554
  113.8 15.5 %collective-permute-start.20 = (f32[1152,128]{1,0:T(8,128)S(1)}, f32[1152,128]{1,0:T(8,128)S(1)}, u32[]{:S(2)}, u32[]{:S(2)}) collective-permute-start(f32[1152,128]{1,0:T(8,128)S(1)} %get-tuple-element.47.refs_1_), channel_id=1, source_target_pairs={{4,0},{8,4},{12,8},{5,1},{9,5},{13,9},{6,2},{10,6},{14,10},{7,3},{... | collective-permute-start | bytes 1769480 | tf_op jit(solution)/shard_map/ppermute | solution.py:549
  118.0 26.7 %copy-start.3 = (f32[40,8,512]{2,1,0:T(8,128)S(1)}, f32[40,8,512]{2,1,0:T(8,128)}, u32[]{:S(2)}) copy-start(f32[40,8,512]{2,1,0:T(8,128)} %param.13) | copy-start | bytes 1966084
  118.0 20.7 %collective-permute-start.24 = (f32[1152,128]{1,0:T(8,128)S(1)}, f32[1152,128]{1,0:T(8,128)S(1)}, u32[]{:S(2)}, u32[]{:S(2)}) collective-permute-start(f32[1152,128]{1,0:T(8,128)S(1)} %shard_map.106.refs_1_.refs_0_), channel_id=1, source_target_pairs={{0,8},{4,12},{8,16},{12,20},{16,24},{20,28},{24,32},{28,36},{32,40... | collective-permute-start | bytes 1769480 | tf_op jit(solution)/shard_map/ppermute | solution.py:495
  120.1 21.9 %collective-permute-start.27 = (f32[1152,128]{1,0:T(8,128)S(1)}, f32[1152,128]{1,0:T(8,128)S(1)}, u32[]{:S(2)}, u32[]{:S(2)}) collective-permute-start(f32[1152,128]{1,0:T(8,128)S(1)} %get-tuple-element.48.refs_2_), channel_id=1, source_target_pairs={{8,0},{12,4},{9,1},{13,5},{10,2},{14,6},{11,3},{15,7}} | collective-permute-start | bytes 1769480 | tf_op jit(solution)/shard_map/ppermute | solution.py:549
  124.1 21.8 %collective-permute-start.28 = (f32[1152,128]{1,0:T(8,128)S(1)}, f32[1152,128]{1,0:T(8,128)S(1)}, u32[]{:S(2)}, u32[]{:S(2)}) collective-permute-start(f32[1152,128]{1,0:T(8,128)S(1)} %get-tuple-element.49.refs_3_), channel_id=1, source_target_pairs={{12,0},{13,1},{14,2},{15,3}} | collective-permute-start | bytes 1769480 | tf_op jit(solution)/shard_map/ppermute | solution.py:549
  127.5 18.3 %collective-permute-start.26 = (f32[1152,128]{1,0:T(8,128)S(1)}, f32[1152,128]{1,0:T(8,128)S(1)}, u32[]{:S(2)}, u32[]{:S(2)}) collective-permute-start(f32[1152,128]{1,0:T(8,128)S(1)} %collective-permute-done.25.y_ref), channel_id=1, source_target_pairs={{24,16},{0,24},{8,32},{16,40},{56,48},{32,56},{40,64},{48,72},{88,... | collective-permute-start | bytes 1769480 | tf_op jit(solution)/shard_map/ppermute | solution.py:557
  131.5 18.7 %collective-permute-start.21 = (f32[576,128]{1,0:T(8,128)S(1)}, f32[576,128]{1,0:T(8,128)S(1)}, u32[]{:S(2)}, u32[]{:S(2)}) collective-permute-start(f32[576,128]{1,0:T(8,128)S(1)} %get-tuple-element.51), channel_id=1, source_target_pairs={{0,1},{1,2},{2,3},{3,0},{4,5},{5,6},{6,7},{7,4},{8,9},{9,10},{10,1... | collective-permute-start | bytes 884744 | tf_op jit(solution)/shard_map/ppermute | solution.py:540
  138.7 12.6 %collective-permute-start.22 = (f32[576,128]{1,0:T(8,128)S(1)}, f32[576,128]{1,0:T(8,128)S(1)}, u32[]{:S(2)}, u32[]{:S(2)}) collective-permute-start(f32[576,128]{1,0:T(8,128)S(1)} %get-tuple-element.52), channel_id=1, source_target_pairs={{0,2},{1,3},{2,0},{3,1},{4,6},{5,7},{6,4},{7,5},{8,10},{9,11},{10,... | collective-permute-start | bytes 884744 | tf_op jit(solution)/shard_map/ppermute | solution.py:540
  141.9 11.1 %collective-permute-start.23 = (f32[576,128]{1,0:T(8,128)S(1)}, f32[576,128]{1,0:T(8,128)S(1)}, u32[]{:S(2)}, u32[]{:S(2)}) collective-permute-start(f32[576,128]{1,0:T(8,128)S(1)} %get-tuple-element.53), channel_id=1, source_target_pairs={{0,3},{1,0},{2,1},{3,2},{4,7},{5,4},{6,5},{7,6},{8,11},{9,8},{10,9... | collective-permute-start | bytes 884744 | tf_op jit(solution)/shard_map/ppermute | solution.py:540
  146.7 10.3 %collective-permute-start.29 = (f32[576,128]{1,0:T(8,128)S(1)}, f32[576,128]{1,0:T(8,128)S(1)}, u32[]{:S(2)}, u32[]{:S(2)}) collective-permute-start(f32[576,128]{1,0:T(8,128)S(1)} %get-tuple-element.55), channel_id=1, source_target_pairs={{0,1},{1,2},{2,3},{3,0},{4,5},{5,6},{6,7},{7,4},{8,9},{9,10},{10,1... | collective-permute-start | bytes 884744 | tf_op jit(solution)/shard_map/ppermute | solution.py:540
  147.0 12.5 %collective-permute-start.30 = (f32[576,128]{1,0:T(8,128)S(1)}, f32[576,128]{1,0:T(8,128)S(1)}, u32[]{:S(2)}, u32[]{:S(2)}) collective-permute-start(f32[576,128]{1,0:T(8,128)S(1)} %get-tuple-element.56), channel_id=1, source_target_pairs={{0,2},{1,3},{2,0},{3,1},{4,6},{5,7},{6,4},{7,5},{8,10},{9,11},{10,... | collective-permute-start | bytes 884744 | tf_op jit(solution)/shard_map/ppermute | solution.py:540
  150.2 15.1 %collective-permute-start.31 = (f32[576,128]{1,0:T(8,128)S(1)}, f32[576,128]{1,0:T(8,128)S(1)}, u32[]{:S(2)}, u32[]{:S(2)}) collective-permute-start(f32[576,128]{1,0:T(8,128)S(1)} %get-tuple-element.57), channel_id=1, source_target_pairs={{0,3},{1,0},{2,1},{3,2},{4,7},{5,4},{6,5},{7,6},{8,11},{9,8},{10,9... | collective-permute-start | bytes 884744 | tf_op jit(solution)/shard_map/ppermute | solution.py:540
  171.0 11.4 %copy-start.4 = (f32[2,8,512]{2,1,0:T(8,128)S(1)}, f32[2,8,512]{2,1,0:T(8,128)}, u32[]{:S(2)}) copy-start(f32[2,8,512]{2,1,0:T(8,128)} %param.17) | copy-start | bytes 98308
  171.0 11.4 %copy-start.6 = (f32[8,512]{1,0:T(8,128)S(1)}, f32[8,512]{1,0:T(8,128)}, u32[]{:S(2)}) copy-start(f32[8,512]{1,0:T(8,128)} %lateral_ref.1) | copy-start | bytes 49156
  171.0 10.3 %collective-permute-start.32 = (f32[512,128]{1,0:T(8,128)S(1)}, f32[512,128]{1,0:T(8,128)S(1)}, u32[]{:S(2)}, u32[]{:S(2)}) collective-permute-start(f32[512,128]{1,0:T(8,128)S(1)} %get-tuple-element.59), channel_id=1, source_target_pairs={{0,1},{1,0},{2,3},{3,2},{4,5},{5,4},{6,7},{7,6},{8,9},{9,8},{10,11... | collective-permute-start | bytes 786440 | tf_op jit(solution)/shard_map/ppermute | solution.py:585
  172.4 10.0 %collective-permute-start.33 = (f32[512,128]{1,0:T(8,128)S(1)}, f32[512,128]{1,0:T(8,128)S(1)}, u32[]{:S(2)}, u32[]{:S(2)}) collective-permute-start(f32[512,128]{1,0:T(8,128)S(1)} %get-tuple-element.60), channel_id=1, source_target_pairs={{1,2},{2,1},{5,6},{6,5},{9,10},{10,9},{13,14},{14,13},{17,18},{18,... | collective-permute-start | bytes 786440 | tf_op jit(solution)/shard_map/ppermute | solution.py:585
  176.3 3.3 %collective-permute-start.34 = (f32[8,128]{1,0:T(8,128)S(1)}, f32[8,128]{1,0:T(8,128)S(1)}, u32[]{:S(2)}, u32[]{:S(2)}) collective-permute-start(f32[8,128]{1,0:T(8,128)S(1)} %get-tuple-element.61), channel_id=1, source_target_pairs={{0,4},{4,0},{8,12},{12,8},{16,20},{20,16},{24,28},{28,24},{32,36},... | collective-permute-start | bytes 12296 | tf_op jit(solution)/shard_map/ppermute | solution.py:585
  176.4 4.9 %collective-permute-start.35 = (f32[8,128]{1,0:T(8,128)S(1)}, f32[8,128]{1,0:T(8,128)S(1)}, u32[]{:S(2)}, u32[]{:S(2)}) collective-permute-start(f32[8,128]{1,0:T(8,128)S(1)} %get-tuple-element.62), channel_id=1, source_target_pairs={{4,8},{8,4},{12,16},{16,12},{20,24},{24,20},{28,32},{32,28},{36,40... | collective-permute-start | bytes 12296 | tf_op jit(solution)/shard_map/ppermute | solution.py:585
